TPU v7x, 512 devices: a whole 4x4x16 slice. The times are simulated.
512 devices in a mesh: ctx: 64 (over z, y_lo, core), tp: 8 (over x, y_hi).
Axes of the slice: x: 4, y: 4 (y_hi: 2, y_lo: 2; y = y_hi * 2 + y_lo), z: 16, core: 2. Of those that a mesh axis runs over, the one named last changes fastest.
Arguments:
- query_se: bfloat16 [14336, 8192], P('ctx', 'tp'), may hold values from -6 to 6
- key_se: bfloat16 [14336, 8192], P('ctx', 'tp'), may hold values from -6 to 6
- value_se: bfloat16 [14336, 8192], P('ctx', 'tp'), may hold values from -6 to 6
- query_mr: bfloat16 [14336, 8192], P('ctx', 'tp'), may hold values from -6 to 6
- key_mr: bfloat16 [14336, 8192], P('ctx', 'tp'), may hold values from -6 to 6
- upstream: bfloat16 [14336, 8192], P('ctx', 'tp'), may hold values from -6 to 6
- filter_se: float32 [7, 8192], P(None, 'tp'), may hold values from -2 to 2
- filter_mr: float32 [128, 8192], P(None, 'tp'), may hold values from -0.5 to 0.5
- skip_mr: float32 [8192], P('tp'), may hold values from -1 to 1
- norm_gain: float32 [8192], P('tp'), may hold values from 0.1 to 1.9
Outputs:
- grad_query_se: bfloat16 [14336, 8192], P('ctx', 'tp')
- grad_key_se: bfloat16 [14336, 8192], P('ctx', 'tp')
- grad_value_se: bfloat16 [14336, 8192], P('ctx', 'tp')
- grad_query_mr: bfloat16 [14336, 8192], P('ctx', 'tp')
- grad_key_mr: bfloat16 [14336, 8192], P('ctx', 'tp')
- grad_filter_se: float32 [7, 8192], P(None, ('tp', 'ctx'))
- grad_filter_mr: float32 [128, 8192], P(None, ('tp', 'ctx'))
- grad_skip: float32 [8192], P(('tp', 'ctx'))
- grad_gain: float32 [8192], P(('tp', 'ctx'))
All inputs are finite; a program needn't handle non-finite values.
Results may differ from a plain program's by a relative error of at most 0.0062.
Values may be sent and summed in bfloat16 or wider, within the bound.
No kernel may reach another device: no remote copies, remote signals or barrier semaphores. Data moves between devices by JAX's collectives and lax.ppermute only.
A program may use at most 64 MiB of HBM per device.

v0:
```python
import math

import jax
import jax.numpy as jnp
from jax import lax
from jax.sharding import PartitionSpec as P

D = 8192


EPSILON = 0.1


def shifted(block, axis, distance):
    devices = range(lax.axis_size(axis))
    route = [(i - distance, i) for i in devices if i - distance in devices]
    return lax.ppermute(block, axis, route)


def sent_to_all(x, axis):
    copies = jnp.broadcast_to(x, (lax.axis_size(axis), *x.shape))
    return lax.all_to_all(copies, axis, split_axis=0, concat_axis=0, tiled=True)


def taken_together(x, axis):
    everything = sent_to_all(x, axis)
    return jnp.sum(everything, axis=0)


def in_blocks(x, dim, length):
    lengths = x.shape
    tiles = x.reshape(*lengths[:dim], length, lengths[dim] // length, *lengths[dim + 1 :])
    return jnp.moveaxis(tiles, dim, 0)


def sum_at_owner(x, axis, dim):
    length = lax.axis_size(axis)
    tiles = lax.all_to_all(in_blocks(x, dim, length), axis, 0, 0, tiled=True)
    return jnp.sum(tiles.astype(jnp.float32), axis=0)


def rounded(value):
    half = lax.optimization_barrier(value.astype(jnp.bfloat16))
    return half.astype(jnp.float32)


def depthwise(signal, kernel):
    result = lax.conv_general_dilated(
        signal[None],
        kernel[:, None, :],
        (1,),
        "VALID",
        dimension_numbers=("NWC", "WIO", "NWC"),
        feature_group_count=signal.shape[1],
        precision=lax.Precision.HIGHEST,
    )
    return result[0]


def local(
    query_se, key_se, value_se, query_mr, key_mr, upstream, filter_se, filter_mr, skip_mr, norm_gain
):
    rows = query_se.shape[0]
    se_span = filter_se.shape[0] - 1
    mr_span = filter_mr.shape[0] - 1
    flip_se = filter_se[::-1]
    flip_mr = filter_mr[::-1]
    product_se = rounded(key_se.astype(jnp.float32) * value_se.astype(jnp.float32))
    tail_se = shifted(product_se[rows - se_span :].astype(jnp.bfloat16), "ctx", 1)
    padded_se = jnp.concatenate([tail_se.astype(jnp.float32), product_se], 0)
    conv_se = depthwise(padded_se, flip_se)
    mixed_se = query_se.astype(jnp.float32) * conv_se
    squares = taken_together(jnp.sum(mixed_se * mixed_se, axis=1), "tp")
    scale_rows = lax.rsqrt(squares / D + EPSILON)
    normed = mixed_se * scale_rows[:, None] * norm_gain
    product_mr = rounded(key_mr.astype(jnp.float32) * normed)
    tail_mr = shifted(product_mr[rows - mr_span :].astype(jnp.bfloat16), "ctx", 1)
    padded_mr = jnp.concatenate([tail_mr.astype(jnp.float32), product_mr], 0)
    conv_mr = depthwise(padded_mr, flip_mr) + skip_mr * product_mr
    cotangent = upstream.astype(jnp.float32)
    grad_query_mr = (cotangent * conv_mr).astype(jnp.bfloat16)
    grad_conv_mr = rounded(cotangent * query_mr.astype(jnp.float32))
    head_mr = shifted(grad_conv_mr[:mr_span].astype(jnp.bfloat16), "ctx", -1)
    grad_product_mr = depthwise(
        jnp.concatenate([grad_conv_mr, head_mr.astype(jnp.float32)], 0), filter_mr
    )
    grad_product_mr = grad_product_mr + skip_mr * grad_conv_mr
    grad_key_mr = (grad_product_mr * normed).astype(jnp.bfloat16)
    grad_normed = grad_product_mr * key_mr.astype(jnp.float32)
    local_filter_mr = depthwise(padded_mr, grad_conv_mr)[::-1]
    local_skip = jnp.sum(grad_conv_mr * product_mr, axis=0)
    local_gain = jnp.sum(grad_normed * mixed_se * scale_rows[:, None], axis=0)
    weighted = taken_together(jnp.sum(grad_normed * norm_gain * mixed_se, axis=1), "tp")
    grad_mixed = (
        norm_gain * scale_rows[:, None] * grad_normed
        - mixed_se * (scale_rows**3 * weighted / D)[:, None]
    )
    grad_query_se = (grad_mixed * conv_se).astype(jnp.bfloat16)
    grad_conv_se = rounded(grad_mixed * query_se.astype(jnp.float32))
    head_se = shifted(grad_conv_se[:se_span].astype(jnp.bfloat16), "ctx", -1)
    grad_product_se = depthwise(
        jnp.concatenate([grad_conv_se, head_se.astype(jnp.float32)], 0), filter_se
    )
    grad_key_se = (grad_product_se * value_se.astype(jnp.float32)).astype(jnp.bfloat16)
    grad_value_se = (grad_product_se * key_se.astype(jnp.float32)).astype(jnp.bfloat16)
    local_filter_se = depthwise(padded_se, grad_conv_se)[::-1]
    total_se, total_mr, total_skip, total_gain = (
        sum_at_owner(local_filter_se.astype(jnp.bfloat16), "ctx", 1),
        sum_at_owner(local_filter_mr.astype(jnp.bfloat16), "ctx", 1),
        sum_at_owner(local_skip.astype(jnp.bfloat16), "ctx", 0),
        sum_at_owner(local_gain.astype(jnp.bfloat16), "ctx", 0),
    )
    factor = 1.0 / math.sqrt(rows * lax.axis_size("ctx"))
    return (
        grad_query_se,
        grad_key_se,
        grad_value_se,
        grad_query_mr,
        grad_key_mr,
        total_se * factor,
        total_mr * factor,
        total_skip * factor,
        total_gain * factor,
    )


def solution(mesh):
    in_specs = (
        P("ctx", "tp"),
        P("ctx", "tp"),
        P("ctx", "tp"),
        P("ctx", "tp"),
        P("ctx", "tp"),
        P("ctx", "tp"),
        P(None, "tp"),
        P(None, "tp"),
        P("tp"),
        P("tp"),
    )
    out_specs = (
        P("ctx", "tp"),
        P("ctx", "tp"),
        P("ctx", "tp"),
        P("ctx", "tp"),
        P("ctx", "tp"),
        P(None, ("tp", "ctx")),
        P(None, ("tp", "ctx")),
        P(("tp", "ctx")),
        P(("tp", "ctx")),
    )
    return jax.shard_map(local, mesh=mesh, in_specs=in_specs, out_specs=out_specs, check_vma=False)
```

profile of v0, /device:TPU:1, one launch (start us, length us, event | category | flops | bytes accessed | tf_op | source)
XLA Modules:
  0.0 174.5 jit_solution(8641536419231418933)
XLA Ops:
  0.7 1.4 fusion.6
  2.1 4.6 %collective-permute-start = (bf16[6,1024]{1,0:T(8,128)(2,1)S(1)}, bf16[6,1024]{1,0:T(8,128)(2,1)S(1)}, u32[]{:S(2)}, u32[]{:S(2)}) collective-permute-start(bf16[6,1024]{1,0:T(8,128)(2,1)S(1)} %slice.24), channel_id=1, source_target_pairs={{0,8},{8,16},{16,24},{24,32},{32,40},{40,48},{48,56},{56,64},{64,7... | collective-permute-start | bytes 36872 | tf_op jit(solution)/shard_map/ppermute | solution.py:17
  7.6 5.4 %collective-permute-start.1 = (bf16[127,1024]{1,0:T(8,128)(2,1)}, bf16[127,1024]{1,0:T(8,128)(2,1)}, u32[]{:S(2)}, u32[]{:S(2)}) collective-permute-start(bf16[127,1024]{1,0:T(8,128)(2,1)} %slice.27), channel_id=1, source_target_pairs={{8,0},{16,8},{24,16},{32,24},{40,32},{48,40},{56,48},{64,56},{72,6... | collective-permute-start | bytes 780296 | tf_op jit(solution)/shard_map/ppermute | solution.py:17
  16.1 1.2 multiply_reduce_fusion.3
  17.9 3.3 %all-to-all-start = ((f32[8,1,224]{2,1,0:T(1,128)}), f32[8,1,224]{2,1,0:T(1,128)S(1)}, u32[]{:S(2)}, u32[]{:S(2)}) async-start(f32[8,1,224]{2,1,0:T(1,128)} %broadcast_in_dim.56), calls=%async_computation | async-start | bytes 16384 | tf_op jit(solution)/shard_map/all_to_all | solution.py:22
  21.3 6.5 %all-to-all-done = f32[8,1,224]{2,1,0:T(1,128)S(1)} async-done(((f32[8,1,224]{2,1,0:T(1,128)}), f32[8,1,224]{2,1,0:T(1,128)S(1)}, u32[]{:S(2)}, u32[]{:S(2)}) %all-to-all-start) | async-done | bytes 7200 | tf_op jit(solution)/shard_map/all_to_all | solution.py:22
  27.9 1.0 convert_element_type.125
  29.0 1.0 broadcast_in_dim.57
  30.1 9.2 %fusion.30 = f32[1,224,1024]{2,0,1:T(1,128)S(1)} fusion(f32[1,351,1024]{2,0,1:T(1,128)S(1)} %broadcast_in_dim.57, f32[128,1,1024]{2,0,1:T(8,128)S(1)} %bitcast.56), kind=kOutput, calls=%fused_computation.55 | convolution fusion | flops 352321536 | bytes 2879488 | tf_op jit(solution)/shard_map/conv_general_dilated | solution.py:48
  39.4 1.6 multiply_reduce_fusion
  41.5 3.3 %all-to-all-start.1 = ((f32[8,1,224]{2,1,0:T(1,128)}), f32[8,1,224]{2,1,0:T(1,128)S(1)}, u32[]{:S(2)}, u32[]{:S(2)}) async-start(f32[8,1,224]{2,1,0:T(1,128)} %broadcast_in_dim.59), calls=%async_computation.1 | async-start | bytes 16384 | tf_op jit(solution)/shard_map/all_to_all | solution.py:22
  44.9 2.7 %rev.13 = f32[128,1024]{1,0:T(8,128)} reverse(f32[128,1024]{1,0:T(8,128)S(1)} %copy-done.10), dimensions={0} | reverse | bytes 1048576 | tf_op jit(solution)/shard_map/rev | solution.py:67
  48.4 1.0 convert_element_type.133
  50.1 3.9 %collective-permute-start.3 = (bf16[127,1024]{1,0:T(8,128)(2,1)}, bf16[127,1024]{1,0:T(8,128)(2,1)}, u32[]{:S(2)}, u32[]{:S(2)}) collective-permute-start(bf16[127,1024]{1,0:T(8,128)(2,1)} %slice.31), channel_id=1, source_target_pairs={{0,8},{8,16},{16,24},{24,32},{32,40},{40,48},{48,56},{56,64},{64,7... | collective-permute-start | bytes 780296 | tf_op jit(solution)/shard_map/ppermute | solution.py:17
  54.0 18.7 %all-to-all-start.5 = ((bf16[64,1,16]{2,1,0:T(2,128)(2,1)}), bf16[64,1,16]{2,1,0:T(2,128)(2,1)S(1)}, u32[]{:S(2)}, u32[]{:S(2)}) async-start(bf16[64,1,16]{2,1,0:T(2,128)(2,1)} %convert_element_type.147), calls=%async_computation.5 | async-start | bytes 65536 | tf_op jit(solution)/shard_map/all_to_all | solution.py:38
  72.7 2.5 %fusion.4 = (bf16[224,1024]{1,0:T(8,128)(2,1)S(1)}, bf16[224,1024]{1,0:T(8,128)(2,1)}) fusion(bf16[224,1024]{1,0:T(8,128)(2,1)} %param.10, f32[224,1024]{1,0:T(8,128)S(1)} %get-tuple-element.13, f32[224]{0:T(256)S(1)} %fusion.37, f32[224,1024]{1,0:T(8,128)} %get-tuple-element.11, f32[224]{0:T(256)S(1)} %add_rsqrt_fusion, f32[1024]{0:T(1024)S(1)} %copy-done.16, ...), kind=kLoop, calls=%fused_computation.18 | loop fusion | flops 2064384 | bytes 4134656 | tf_op jit(solution)/shard_map/convert_element_type | solution.py:43
  75.2 2.1 %fusion.2 = bf16[1,7,1024]{2,0,1:T(2,128)(2,1)S(1)} fusion(bf16[1,230,1024]{2,1,0:T(8,128)(2,1)S(1)} %copy-done.2, bf16[224,1,1024]{2,0,1:T(8,128)(2,1)S(1)} %bitcast.54), kind=kOutput, calls=%fused_computation.16 | convolution fusion | flops 3211264 | bytes 944128 | tf_op jit(solution)/shard_map/conv_general_dilated | solution.py:48
  77.5 2.4 %collective-permute-start.2 = (bf16[6,1024]{1,0:T(8,128)(2,1)S(1)}, bf16[6,1024]{1,0:T(8,128)(2,1)S(1)}, u32[]{:S(2)}, u32[]{:S(2)}) collective-permute-start(bf16[6,1024]{1,0:T(8,128)(2,1)S(1)} %slice.28), channel_id=1, source_target_pairs={{8,0},{16,8},{24,16},{32,24},{40,32},{48,40},{56,48},{64,56},{72,6... | collective-permute-start | bytes 36872 | tf_op jit(solution)/shard_map/ppermute | solution.py:17
  80.8 5.0 %all-to-all-done.5 = bf16[64,1,16]{2,1,0:T(2,128)(2,1)S(1)} async-done(((bf16[64,1,16]{2,1,0:T(2,128)(2,1)}), bf16[64,1,16]{2,1,0:T(2,128)(2,1)S(1)}, u32[]{:S(2)}, u32[]{:S(2)}) %all-to-all-start.5) | async-done | bytes 2080 | tf_op jit(solution)/shard_map/all_to_all | solution.py:38
  85.8 8.4 %all-to-all-start.2 = ((bf16[64,7,16]{2,1,0:T(8,128)(2,1)}), bf16[64,7,16]{2,1,0:T(8,128)(2,1)S(1)}, u32[]{:S(2)}, u32[]{:S(2)}) async-start(bf16[64,7,16]{2,1,0:T(8,128)(2,1)} %copy.98), calls=%async_computation.2 | async-start | bytes 262144 | tf_op jit(solution)/shard_map/all_to_all | solution.py:38
  96.1 1.0 convert_element_type.132
  97.3 0.9 copy-done.11
  98.2 9.5 %fusion.15 = f32[1,224,1024]{2,0,1:T(1,128)S(1)} fusion(f32[1,351,1024]{2,1,0:T(8,128)S(1)} %maximum_bitcast_fusion, f32[128,1,1024]{2,0,1:T(8,128)S(1)} %bitcast.57), kind=kOutput, calls=%fused_computation.41 | convolution fusion | flops 352321536 | bytes 2879488 | tf_op jit(solution)/shard_map/conv_general_dilated | solution.py:48
  107.7 1.2 multiply_reduce_fusion.1
  109.6 1.7 all-to-all-done.2
  111.3 11.9 %all-to-all-start.4 = ((bf16[64,1,16]{2,1,0:T(2,128)(2,1)}), bf16[64,1,16]{2,1,0:T(2,128)(2,1)S(1)}, u32[]{:S(2)}, u32[]{:S(2)}) async-start(bf16[64,1,16]{2,1,0:T(2,128)(2,1)} %convert_element_type.146), calls=%async_computation.4 | async-start | bytes 65536 | tf_op jit(solution)/shard_map/all_to_all | solution.py:38
  123.2 13.5 %fusion.11 = bf16[1,128,1024]{2,0,1:T(2,128)(2,1)S(1)} fusion(bf16[224,1,1024]{2,0,1:T(8,128)(2,1)S(1)} %bitcast.53, f32[1,351,1024]{2,1,0:T(8,128)} %copy-done.7), kind=kOutput, calls=%fused_computation.29 | convolution fusion | flops 352321536 | bytes 2158592 | tf_op jit(solution)/shard_map/conv_general_dilated | solution.py:48
  137.1 0.8 copy.101
  137.9 13.6 %all-to-all-start.3 = ((bf16[64,128,16]{1,2,0:T(8,128)(2,1)}), bf16[64,128,16]{1,2,0:T(8,128)(2,1)S(1)}, u32[]{:S(2)}, u32[]{:S(2)}) async-start(bf16[64,128,16]{1,2,0:T(8,128)(2,1)} %bitcast.15), calls=%async_computation.3 | async-start | bytes 524288 | tf_op jit(solution)/shard_map/all_to_all | solution.py:38
  152.8 0.9 copy-done.5
  153.8 1.2 fusion.5
  156.2 17.6 %all-to-all-done.3 = bf16[64,128,16]{1,2,0:T(8,128)(2,1)S(1)} async-done(((bf16[64,128,16]{1,2,0:T(8,128)(2,1)}), bf16[64,128,16]{1,2,0:T(8,128)(2,1)S(1)}, u32[]{:S(2)}, u32[]{:S(2)}) %all-to-all-start.3) | async-done | bytes 262176 | tf_op jit(solution)/shard_map/all_to_all | solution.py:38
  (87 shorter events, 14.4 us)
Async XLA Ops:
  0.6 6.0 %copy-start.3 = (bf16[224,1024]{1,0:T(8,128)(2,1)S(1)}, bf16[224,1024]{1,0:T(8,128)(2,1)}, u32[]{:S(2)}) copy-start(bf16[224,1024]{1,0:T(8,128)(2,1)} %param.15) | copy-start | bytes 1376260
  0.7 6.0 %copy-start.12 = (bf16[224,1024]{1,0:T(8,128)(2,1)S(1)}, bf16[224,1024]{1,0:T(8,128)(2,1)}, u32[]{:S(2)}) copy-start(bf16[224,1024]{1,0:T(8,128)(2,1)} %param.13) | copy-start | bytes 1376260
  0.7 12.4 %copy-start.14 = (f32[7,1024]{1,0:T(8,128)S(1)}, f32[7,1024]{1,0:T(8,128)}, u32[]{:S(2)}) copy-start(f32[7,1024]{1,0:T(8,128)} %param.16) | copy-start | bytes 86020
  2.1 11.2 %collective-permute-start = (bf16[6,1024]{1,0:T(8,128)(2,1)S(1)}, bf16[6,1024]{1,0:T(8,128)(2,1)S(1)}, u32[]{:S(2)}, u32[]{:S(2)}) collective-permute-start(bf16[6,1024]{1,0:T(8,128)(2,1)S(1)} %slice.24), channel_id=1, source_target_pairs={{0,8},{8,16},{16,24},{24,32},{32,40},{40,48},{48,56},{56,64},{64,7... | collective-permute-start | bytes 36872 | tf_op jit(solution)/shard_map/ppermute | solution.py:17
  7.6 20.3 %collective-permute-start.1 = (bf16[127,1024]{1,0:T(8,128)(2,1)}, bf16[127,1024]{1,0:T(8,128)(2,1)}, u32[]{:S(2)}, u32[]{:S(2)}) collective-permute-start(bf16[127,1024]{1,0:T(8,128)(2,1)} %slice.27), channel_id=1, source_target_pairs={{8,0},{16,8},{24,16},{32,24},{40,32},{48,40},{56,48},{64,56},{72,6... | collective-permute-start | bytes 780296 | tf_op jit(solution)/shard_map/ppermute | solution.py:17
  13.4 0.8 copy-start.1
  14.2 0.7 copy-start.17
  17.9 9.9 %all-to-all-start = ((f32[8,1,224]{2,1,0:T(1,128)}), f32[8,1,224]{2,1,0:T(1,128)S(1)}, u32[]{:S(2)}, u32[]{:S(2)}) async-start(f32[8,1,224]{2,1,0:T(1,128)} %broadcast_in_dim.56), calls=%async_computation | async-start | bytes 16384 | tf_op jit(solution)/shard_map/all_to_all | solution.py:22
  29.0 1.0 copy-start.10
  30.1 9.3 %copy-start.13 = (bf16[224,1024]{1,0:T(8,128)(2,1)S(1)}, bf16[224,1024]{1,0:T(8,128)(2,1)}, u32[]{:S(2)}) copy-start(bf16[224,1024]{1,0:T(8,128)(2,1)} %param.14) | copy-start | bytes 1376260
  30.1 9.3 %copy-start.15 = (f32[1024]{0:T(1024)S(1)}, f32[1024]{0:T(1024)}, u32[]{:S(2)}) copy-start(f32[1024]{0:T(1024)} %param.18) | copy-start | bytes 12292
  30.1 9.3 %copy-start.16 = (f32[1024]{0:T(1024)S(1)}, f32[1024]{0:T(1024)}, u32[]{:S(2)}) copy-start(f32[1024]{0:T(1024)} %param.19) | copy-start | bytes 12292
  41.5 12.4 %all-to-all-start.1 = ((f32[8,1,224]{2,1,0:T(1,128)}), f32[8,1,224]{2,1,0:T(1,128)S(1)}, u32[]{:S(2)}, u32[]{:S(2)}) async-start(f32[8,1,224]{2,1,0:T(1,128)} %broadcast_in_dim.59), calls=%async_computation.1 | async-start | bytes 16384 | tf_op jit(solution)/shard_map/all_to_all | solution.py:22
  50.1 45.3 %collective-permute-start.3 = (bf16[127,1024]{1,0:T(8,128)(2,1)}, bf16[127,1024]{1,0:T(8,128)(2,1)}, u32[]{:S(2)}, u32[]{:S(2)}) collective-permute-start(bf16[127,1024]{1,0:T(8,128)(2,1)} %slice.31), channel_id=1, source_target_pairs={{0,8},{8,16},{16,24},{24,32},{32,40},{40,48},{48,56},{56,64},{64,7... | collective-permute-start | bytes 780296 | tf_op jit(solution)/shard_map/ppermute | solution.py:17
  54.0 31.8 %all-to-all-start.5 = ((bf16[64,1,16]{2,1,0:T(2,128)(2,1)}), bf16[64,1,16]{2,1,0:T(2,128)(2,1)S(1)}, u32[]{:S(2)}, u32[]{:S(2)}) async-start(bf16[64,1,16]{2,1,0:T(2,128)(2,1)} %convert_element_type.147), calls=%async_computation.5 | async-start | bytes 65536 | tf_op jit(solution)/shard_map/all_to_all | solution.py:38
  72.7 2.5 %copy-start.2 = (bf16[1,230,1024]{2,1,0:T(8,128)(2,1)S(1)}, bf16[1,230,1024]{2,1,0:T(8,128)(2,1)}, u32[]{:S(2)}) copy-start(bf16[1,230,1024]{2,1,0:T(8,128)(2,1)} %copy-done.1) | copy-start | bytes 1413124
  77.5 17.3 %collective-permute-start.2 = (bf16[6,1024]{1,0:T(8,128)(2,1)S(1)}, bf16[6,1024]{1,0:T(8,128)(2,1)S(1)}, u32[]{:S(2)}, u32[]{:S(2)}) collective-permute-start(bf16[6,1024]{1,0:T(8,128)(2,1)S(1)} %slice.28), channel_id=1, source_target_pairs={{8,0},{16,8},{24,16},{32,24},{40,32},{48,40},{56,48},{64,56},{72,6... | collective-permute-start | bytes 36872 | tf_op jit(solution)/shard_map/ppermute | solution.py:17
  85.8 25.5 %all-to-all-start.2 = ((bf16[64,7,16]{2,1,0:T(8,128)(2,1)}), bf16[64,7,16]{2,1,0:T(8,128)(2,1)S(1)}, u32[]{:S(2)}, u32[]{:S(2)}) async-start(bf16[64,7,16]{2,1,0:T(8,128)(2,1)} %copy.98), calls=%async_computation.2 | async-start | bytes 262144 | tf_op jit(solution)/shard_map/all_to_all | solution.py:38
  94.9 2.2 %copy-start = (f32[224,1024]{1,0:T(8,128)S(1)}, f32[224,1024]{1,0:T(8,128)}, u32[]{:S(2)}) copy-start(f32[224,1024]{1,0:T(8,128)} %convert_element_type.133) | copy-start | bytes 2752516
  95.4 0.8 copy-start.8
  97.1 1.0 copy-start.11
  97.3 10.4 %copy-start.7 = (f32[1,351,1024]{2,1,0:T(8,128)}, f32[1,351,1024]{2,1,0:T(8,128)S(1)}, u32[]{:S(2)}) copy-start(f32[1,351,1024]{2,1,0:T(8,128)S(1)} %maximum_bitcast_fusion) | copy-start | bytes 4313092
  98.2 9.5 %copy-start.4 = (bf16[224,1024]{1,0:T(8,128)(2,1)S(1)}, bf16[224,1024]{1,0:T(8,128)(2,1)}, u32[]{:S(2)}) copy-start(bf16[224,1024]{1,0:T(8,128)(2,1)} %param.15) | copy-start | bytes 1376260
  111.3 26.6 %all-to-all-start.4 = ((bf16[64,1,16]{2,1,0:T(2,128)(2,1)}), bf16[64,1,16]{2,1,0:T(2,128)(2,1)S(1)}, u32[]{:S(2)}, u32[]{:S(2)}) async-start(bf16[64,1,16]{2,1,0:T(2,128)(2,1)} %convert_element_type.146), calls=%async_computation.4 | async-start | bytes 65536 | tf_op jit(solution)/shard_map/all_to_all | solution.py:38
  136.7 14.9 %copy-start.9 = (bf16[1,8,29,1024]{3,1,2,0:T(8,128)(2,1)S(1)}, bf16[1,8,29,1024]{3,1,2,0:T(8,128)(2,1)}, u32[]{:S(2)}) copy-start(bf16[1,8,29,1024]{3,1,2,0:T(8,128)(2,1)} %copy-done.8) | copy-start | bytes 1425412
  137.9 35.9 %all-to-all-start.3 = ((bf16[64,128,16]{1,2,0:T(8,128)(2,1)}), bf16[64,128,16]{1,2,0:T(8,128)(2,1)S(1)}, u32[]{:S(2)}, u32[]{:S(2)}) async-start(bf16[64,128,16]{1,2,0:T(8,128)(2,1)} %bitcast.15), calls=%async_computation.3 | async-start | bytes 524288 | tf_op jit(solution)/shard_map/all_to_all | solution.py:38
  152.6 1.0 copy-start.5
  152.6 1.1 copy-start.6
where the time goes:
time: 175 us; the launch traced here: 174 us
  starting transfers between devices  75.5 us (43%)
  matrix products  35.3 us (20%)
  waiting for transfers between devices  30.8 us (18%)
  local copies, waits for them, and re-layouts  16.4 us (9%)
  other arithmetic  15.3 us (9%)
    all_to_all x4, starting transfers between devices, sum_at_owner(): tiles = lax.all_to_all(in_blocks(x, dim, length), axis, 0, 0, tiled=True)  52.5 us
    conv_general_dilated x6, matrix products, depthwise(): lax.conv_general_dilated(signal[None], kernel[:, None, :], (1,), 'VALID',...  35.3 us
    all_to_all x4, waiting for transfers between devices, sum_at_owner(): tiles = lax.all_to_all(in_blocks(x, dim, length), axis, 0, 0, tiled=True)  24.3 us
    ppermute x4, starting transfers between devices, shifted(): return lax.ppermute(block, axis, route)  16.3 us
    all_to_all x2, starting transfers between devices, sent_to_all(): return lax.all_to_all(copies, axis, split_axis=0, concat_axis=0, tiled=True)  6.67 us
    all_to_all x2, waiting for transfers between devices, sent_to_all(): return lax.all_to_all(copies, axis, split_axis=0, concat_axis=0, tiled=True)  6.5 us
    convert_element_type x3, other arithmetic, rounded(): half = lax.optimization_barrier(value.astype(jnp.bfloat16))  4.02 us
    unnamed x38, local copies, waits for them, and re-layouts  3.75 us
  transfers between devices with their start and end apart: 10, of which 4 were waited for; matrix products, arithmetic and copies ran while one was open for 27% of the time, Pallas kernels for 0%

commit v1 on v0

v1 whole, which is shorter than its diff:
```python
import math

import jax
import jax.numpy as jnp
import numpy as np
from jax import lax
from jax.experimental import pallas as pl
from jax.experimental.pallas import tpu as pltpu
from jax.sharding import PartitionSpec as P

D = 8192
EPSILON = 0.1
BF = jnp.bfloat16
F32 = jnp.float32

LEN = 384
HALF = LEN // 2
ROWS = 224
EXT = ROWS + 8
HALO = 128
HEAD = 136
CB = 256
FWD = HALO + 8 + 8
BWD = HEAD + 24
CHUNK = 32


def basis(first, last):
    theta = np.pi * (2 * np.arange(HALF)[:, None] + 1) / LEN * np.arange(first, last)[None, :]
    return np.concatenate([np.cos(theta), -np.sin(theta)], 0)


def halves(matrix):
    high = matrix.astype(BF)
    low = (matrix - high.astype(np.float64)).astype(BF)
    return high, low


def dot(a, b):
    return jnp.dot(a, b, preferred_element_type=F32)


def split(x):
    high = x.astype(BF)
    return high, (x - high.astype(F32)).astype(BF)


def forward(fh, fl, data):
    return dot(fh, data) + dot(fl, data)


def inverse(th, tl, spectrum):
    high, low = split(spectrum)
    return dot(th, high) + dot(tl, high) + dot(th, low)


def wide(column):
    return jnp.concatenate([column] * (CB // 128), axis=1)


def folded(x):
    total = x[:, :128]
    for at in range(128, x.shape[1], 128):
        total = total + x[:, at : at + 128]
    return total


def sums_in_lanes(acc):
    ones = jnp.ones((8, 128), F32)
    return lax.dot_general(
        ones, acc, (((1,), (1,)), ((), ())), precision=lax.Precision.HIGHEST, preferred_element_type=F32
    )


def short_conv(ref, taps, row, count):
    total = None
    for step in range(7):
        term = taps[step : step + 1, :] * ref[pl.ds(row - step, count), :]
        total = term if total is None else total + term
    return total


def short_adjoint(ref, taps, row, count):
    total = None
    for step in range(7):
        term = taps[step : step + 1, :] * ref[pl.ds(row + step, count), :]
        total = term if total is None else total + term
    return total


def rounded(x):
    return x.astype(BF).astype(F32)


def send_kernel(kse, vse, qse, kmr, up, qmr, fse, gain, fwd, bwd, prod, acc):
    i = pl.program_id(0)
    first = ROWS - HALO - 16
    tail = rounded(kse[first:].astype(F32) * vse[first:].astype(F32))
    prod[...] = tail
    taps = fse[...]

    @pl.when(i == 0)
    def _():
        acc[...] = jnp.zeros_like(acc)

    for r in range(0, HALO, CHUNK):
        conv = short_conv(prod, taps, 16 + r, CHUNK)
        at = ROWS - HALO + r
        mixed = qse[at : at + CHUNK].astype(F32) * conv
        fwd[r : r + CHUNK] = (kmr[at : at + CHUNK].astype(F32) * mixed * gain[...]).astype(BF)
        acc[r : r + CHUNK] += folded(mixed * mixed)
    fwd[HALO : HALO + 8] = tail[HALO + 8 :].astype(BF)
    fwd[HALO + 8 :] = jnp.zeros((8, CB), BF)
    bwd[:HEAD] = (up[:HEAD].astype(F32) * qmr[:HEAD].astype(F32)).astype(BF)
    bwd[HEAD : HEAD + 8] = qse[:8]
    bwd[HEAD + 8 : HEAD + 16] = kmr[:8]
    bwd[HEAD + 16 :] = (kse[:8].astype(F32) * vse[:8].astype(F32)).astype(BF)

    @pl.when(i == pl.num_programs(0) - 1)
    def _():
        total = sums_in_lanes(acc[...])
        high = total.astype(BF).astype(F32)
        rows = lax.broadcasted_iota(jnp.int32, (8, 128), 0)
        fwd[HALO + 8 :, :128] = jnp.where(rows == 0, high, jnp.where(rows == 1, total - high, 0.0)).astype(BF)


def local_kernel(up, qmr, fmr, fxh, fxl, gloc, hspec):
    g = (up[...].astype(F32) * qmr[...].astype(F32)).astype(BF)
    gloc[...] = forward(fxh[:, HALO:], fxl[:, HALO:], g)
    high, low = split(fmr[...])
    fh = fxh[:, HALO : HALO + 128]
    hspec[...] = dot(fh, high) + dot(fxl[:, HALO : HALO + 128], high) + dot(fh, low)


def norm_kernel(
    fwd, bwd, kse, vse, qse, kmr, up, qmr, fse, gain, skip, gloc, hspec, fhh, fhl, th, tl,
    mixed_o, conv_o, gp_o, stats, prod, tail, acc_sq, acc_w
):
    i = pl.program_id(0)
    last = pl.num_programs(0) - 1

    @pl.when(i == 0)
    def _():
        acc_sq[...] = jnp.zeros_like(acc_sq)
        acc_w[...] = jnp.zeros_like(acc_w)

    prod[:8] = fwd[HALO : HALO + 8].astype(F32)
    prod[8 : 8 + ROWS] = rounded(kse[...].astype(F32) * vse[...].astype(F32))
    prod[8 + ROWS :] = bwd[HEAD + 16 :].astype(F32)
    spec = gloc[...] + forward(fhh[...], fhl[...], bwd[:HEAD])
    h = hspec[...]
    gr, gi, hr, hi = spec[:HALF], spec[HALF:], h[:HALF], h[HALF:]
    back = jnp.concatenate([gr * hr + gi * hi, gi * hr - gr * hi], 0)
    gp_o[...] = inverse(th[...], tl[...], back)
    taps = fse[...]

    def rows(at, count, query, key, g):
        conv = short_conv(prod, taps, 8 + at, count)
        conv_o[at : at + count] = conv
        mixed = query.astype(F32) * conv
        mixed_o[at : at + count] = mixed
        gp = gp_o[at : at + count] + skip[...] * g.astype(F32)
        gp_o[at : at + count] = gp
        acc_sq[at : at + count] += folded(mixed * mixed)
        acc_w[at : at + count] += folded(gp * key.astype(F32) * gain[...] * mixed)

    for at in range(0, ROWS, CHUNK):
        s = slice(at, at + CHUNK)
        rows(at, CHUNK, qse[s], kmr[s], rounded(up[s].astype(F32) * qmr[s].astype(F32)))
    rows(ROWS, 8, bwd[HEAD : HEAD + 8], bwd[HEAD + 8 : HEAD + 16], bwd[:8])

    @pl.when(i == last)
    def _():
        sq = sums_in_lanes(acc_sq[...])
        w = sums_in_lanes(acc_w[...])
        sent = fwd[HALO + 8 :, :128].astype(F32)
        tail[...] = jnp.concatenate(
            [sq[:1, :128], sq[:1, 128:], w[:1, :128], w[:1, 128:], sent[:1] + sent[1:2], jnp.zeros((3, 128), F32)], 0
        )
        for dev in range(8):
            stats[dev] = tail[...]


def column(total, row):
    pick = (lax.broadcasted_iota(jnp.int32, (8, 128), 0) == row).astype(F32)
    return lax.dot_general(
        total, pick, (((0,), (0,)), ((), ())), precision=lax.Precision.HIGHEST, preferred_element_type=F32
    )


def filter_kernel(
    stats, fwd, mixed, gp, kmr, qse, up, qmr, kse, vse, bwd, gain, gloc, fxh, fxl, th, tl,
    payload, xspec, gc_o, scale_o, coef_o, prod, halo_s, small, xin
):
    i = pl.program_id(0)
    last = pl.num_programs(0) - 1

    @pl.when(i == 0)
    def _():
        total = stats[0]
        for dev in range(1, 8):
            total = total + stats[dev]
        s0 = lax.rsqrt(column(total, 0) / D + EPSILON)
        s1 = lax.rsqrt(column(total, 1) / D + EPSILON)
        scale_o[:128] = s0
        scale_o[128:] = s1[: EXT - 128]
        coef_o[:128] = s0 * s0 * s0 * (column(total, 2) / D)
        coef_o[128:] = (s1 * s1 * s1 * (column(total, 3) / D))[: EXT - 128]
        halo_s[...] = lax.rsqrt(column(total, 4) / D + EPSILON)

    for at in range(0, HALO, CHUNK):
        s = slice(at, at + CHUNK)
        xin[s] = (fwd[s].astype(F32) * wide(halo_s[s])).astype(BF)
    prod[:8] = fwd[HALO : HALO + 8].astype(F32)
    prod[8:] = rounded(kse[...].astype(F32) * vse[...].astype(F32))

    gains = gain[...]
    sums = [jnp.zeros((8, CB), F32) for _ in range(9)]

    def eights(x):
        total = x[:8]
        for r in range(8, x.shape[0], 8):
            total = total + x[r : r + 8]
        return total

    def rows(at, count, query, key):
        scale = wide(scale_o[at : at + count])
        mix = mixed[at : at + count]
        gn = gp[at : at + count] * key.astype(F32)
        ms = mix * scale
        gm = gains * scale * gn - mix * wide(coef_o[at : at + count])
        gc = (gm * query.astype(F32)).astype(BF)
        gc_o[at : at + count] = gc
        return ms, gn, gc.astype(F32)

    for at in range(0, ROWS, CHUNK):
        s = slice(at, at + CHUNK)
        ms, gn, gc = rows(at, CHUNK, qse[s], kmr[s])
        pm = (kmr[s].astype(F32) * (ms * gains)).astype(BF)
        xin[HALO + at : HALO + at + CHUNK] = pm
        g = rounded(up[s].astype(F32) * qmr[s].astype(F32))
        for step in range(7):
            sums[step] = sums[step] + eights(gc * prod[pl.ds(8 + at - step, CHUNK), :])
        sums[7] = sums[7] + eights(g * pm.astype(F32))
        sums[8] = sums[8] + eights(gn * ms)
    rows(ROWS, 8, bwd[HEAD : HEAD + 8], bwd[HEAD + 8 : HEAD + 16])
    parts = [jnp.sum(x, axis=0, keepdims=True) for x in sums]
    small[i] = jnp.concatenate(parts + [jnp.zeros((7, CB), F32)], 0)

    x = forward(fxh[...], fxl[...], xin[...])
    xspec[...] = x
    gl = gloc[...]
    xr, xi, gr, gi = x[:HALF], x[HALF:], gl[:HALF], gl[HALF:]
    back = jnp.concatenate([gr * xr + gi * xi, gi * xr - gr * xi], 0)
    corr = inverse(th[...], tl[...], back).T.astype(BF)
    for zz in range(4):
        for yc in range(4):
            at = pl.multiple_of((4 * i + zz) * 16, 16)
            payload[yc, pl.ds(at, 16), :] = corr[zz * 64 + yc * 16 : zz * 64 + yc * 16 + 16]

    @pl.when(i == last)
    def _():
        lane = lax.broadcasted_iota(jnp.int32, (16, 128), 1)
        row = lax.broadcasted_iota(jnp.int32, (16, 128), 0)
        spread = (lane % 16 == row).astype(BF)
        chan = lax.broadcasted_iota(jnp.int32, (CB, 128), 0)
        keep = chan % 8 == lax.broadcasted_iota(jnp.int32, (CB, 128), 1) // 16
        out_row = lax.broadcasted_iota(jnp.int32, (128, CB), 0)
        out_chan = lax.broadcasted_iota(jnp.int32, (128, CB), 1)
        packed = None
        for block in range(4):
            tiled = lax.dot_general(
                small[block].astype(BF), spread, (((0,), (0,)), ((), ())), preferred_element_type=F32
            )
            masked = jnp.where(keep, tiled, 0.0).astype(BF)
            c = out_chan + block * CB
            take = (out_row // 32 == (c // 16) % 4) & ((out_row // 2) % 16 == c // 64) & (out_row % 2 == (c // 8) % 2)
            part = dot(take.astype(BF), masked)
            packed = part if packed is None else packed + part
        packed = packed.astype(BF)
        for yc in range(4):
            payload[yc, 256:] = packed[yc * 32 : yc * 32 + 32]


def rest_kernel(
    xspec, hspec, th, tl, up, kmr, mixed, conv, gp, gc, kse, vse, gain, skip, fse, scale, coef,
    gqse, gkse, gvse, gqmr, gkmr, ym, gcf
):
    x, h = xspec[...], hspec[...]
    xr, xi, hr, hi = x[:HALF], x[HALF:], h[:HALF], h[HALF:]
    spec = jnp.concatenate([xr * hr - xi * hi, xi * hr + xr * hi], 0)
    ym[...] = inverse(th[:ROWS], tl[:ROWS], spec)
    gcf[...] = gc[...].astype(F32)
    gains, taps = gain[...], fse[...]
    for at in range(0, ROWS, CHUNK):
        s = slice(at, at + CHUNK)
        sc = wide(scale[s])
        key = kmr[s].astype(F32)
        mix = mixed[s]
        grad = gp[s]
        normed = mix * sc * gains
        pm = rounded(key * normed)
        gqmr[s] = (up[s].astype(F32) * (ym[s] + skip[...] * pm)).astype(BF)
        gkmr[s] = (grad * normed).astype(BF)
        gm = gains * sc * (grad * key) - mix * wide(coef[s])
        gqse[s] = (gm * conv[s]).astype(BF)
        gps = short_adjoint(gcf, taps, at, CHUNK)
        gkse[s] = (gps * vse[s].astype(F32)).astype(BF)
        gvse[s] = (gps * kse[s].astype(F32)).astype(BF)


def merge_kernel(got, out):
    total = got[0].astype(F32)
    for k in range(1, 4):
        total = total + got[k].astype(F32)
    for z in range(16):
        out[z, :16] = total[z * 16 : z * 16 + 16].astype(BF)
        pair = total[256 + z * 2 : 256 + z * 2 + 2]
        out[z, 16:] = jnp.concatenate([pair, jnp.zeros((6, 128), F32)], 0).astype(BF)


def final_kernel(got, se_o, mr_o, skip_o, gain_o, *, factor):
    total = got[0].astype(F32)
    for k in range(1, 16):
        total = total + got[k].astype(F32)
    total = total * factor
    eye = (
        lax.broadcasted_iota(jnp.int32, (16, 16), 0) == lax.broadcasted_iota(jnp.int32, (16, 16), 1)
    ).astype(F32)
    mr_o[...] = lax.dot_general(
        total[:16], eye, (((0,), (0,)), ((), ())), precision=lax.Precision.HIGHEST, preferred_element_type=F32
    )
    chan = lax.broadcasted_iota(jnp.int32, (16, 128), 0)
    lane = lax.broadcasted_iota(jnp.int32, (16, 128), 1)
    mine = jnp.where(chan < 8, total[16:17], total[17:18])
    mine = jnp.where(lane // 16 == chan % 8, mine, 0.0)
    pick = (lane % 16 == chan).astype(F32)
    small = lax.dot_general(
        pick, mine, (((1,), (1,)), ((), ())), precision=lax.Precision.HIGHEST, preferred_element_type=F32
    )
    se_o[...] = small[:7]
    skip_o[...] = small[7:8]
    gain_o[...] = small[8:9]


def local(
    query_se, key_se, value_se, query_mr, key_mr, upstream, filter_se, filter_mr, skip_mr, norm_gain
):
    chans = query_se.shape[1]
    steps = chans // CB
    size = lax.axis_size("ctx")
    skip2, gain2 = skip_mr.reshape(1, chans), norm_gain.reshape(1, chans)
    fx = halves(basis(-HALO, ROWS))
    fhead = halves(basis(ROWS, ROWS + HEAD))
    back = halves(basis(0, EXT).T * (2.0 / LEN))

    def cols(rows):
        return pl.BlockSpec((rows, CB), lambda i: (0, i))

    def whole(*shape):
        return pl.BlockSpec(shape, lambda i: (0,) * len(shape))

    def shape(rows, dtype):
        return jax.ShapeDtypeStruct((rows, chans), dtype)

    params = pltpu.CompilerParams(dimension_semantics=("arbitrary",), vmem_limit_bytes=48 * 1024 * 1024)
    stream, one = cols(ROWS), cols(1)

    fwd, bwd = pl.pallas_call(
        send_kernel,
        grid=(steps,),
        in_specs=[stream] * 6 + [cols(7), one],
        out_specs=[cols(FWD), cols(BWD)],
        out_shape=[shape(FWD, BF), shape(BWD, BF)],
        scratch_shapes=[pltpu.VMEM((HALO + 16, CB), F32), pltpu.VMEM((HALO, 128), F32)],
        compiler_params=params,
        name="send",
    )(key_se, value_se, query_se, key_mr, upstream, query_mr, filter_se, gain2)

    down = [(k, k + 1) for k in range(size - 1)]
    upward = [(k + 1, k) for k in range(size - 1)]
    bwd = lax.ppermute(bwd, "ctx", upward)
    fwd = lax.ppermute(fwd, "ctx", down)

    spectrum = cols(LEN)
    gloc, hspec = pl.pallas_call(
        local_kernel,
        grid=(steps,),
        in_specs=[stream, stream, cols(128), whole(LEN, HALO + ROWS), whole(LEN, HALO + ROWS)],
        out_specs=[spectrum, spectrum],
        out_shape=[shape(LEN, F32), shape(LEN, F32)],
        compiler_params=params,
        name="local",
    )(upstream, query_mr, filter_mr, *fx)

    mixed, conv, gp, stats = pl.pallas_call(
        norm_kernel,
        grid=(steps,),
        in_specs=[cols(FWD), cols(BWD)] + [stream] * 6 + [cols(7), one, one, spectrum, spectrum]
        + [whole(LEN, HEAD)] * 2 + [whole(EXT, LEN)] * 2,
        out_specs=[cols(EXT), cols(EXT), cols(EXT), whole(8, 8, 128)],
        out_shape=[shape(EXT, F32), shape(EXT, F32), shape(EXT, F32), jax.ShapeDtypeStruct((8, 8, 128), F32)],
        scratch_shapes=[
            pltpu.VMEM((ROWS + 16, CB), F32), pltpu.VMEM((8, 128), F32),
            pltpu.VMEM((256, 128), F32), pltpu.VMEM((256, 128), F32),
        ],
        compiler_params=params,
        name="norm",
    )(fwd, bwd, key_se, value_se, query_se, key_mr, upstream, query_mr, filter_se, gain2, skip2, gloc, hspec,
      *fhead, *back)

    stats = lax.all_to_all(stats, "tp", 0, 0, tiled=True)

    payload, xspec, gc, scale, coef = pl.pallas_call(
        filter_kernel,
        grid=(steps,),
        in_specs=[whole(8, 8, 128), cols(FWD), cols(EXT), cols(EXT)] + [stream] * 6
        + [cols(BWD), one, spectrum] + [whole(LEN, HALO + ROWS)] * 2 + [whole(128, LEN)] * 2,
        out_specs=[whole(4, 288, 128), spectrum, cols(EXT), whole(EXT, 128), whole(EXT, 128)],
        out_shape=[jax.ShapeDtypeStruct((4, 288, 128), BF), shape(LEN, F32), shape(EXT, BF),
                   jax.ShapeDtypeStruct((EXT, 128), F32), jax.ShapeDtypeStruct((EXT, 128), F32)],
        scratch_shapes=[
            pltpu.VMEM((ROWS + 8, CB), F32), pltpu.VMEM((HALO, 128), F32),
            pltpu.VMEM((steps, 16, CB), F32), pltpu.VMEM((HALO + ROWS, CB), BF),
        ],
        compiler_params=params,
        name="filters",
    )(stats, fwd, mixed, gp, key_mr, query_se, upstream, query_mr, key_se, value_se, bwd, gain2, gloc, *fx, *back)

    near = [[4 * a + b for b in range(4)] for a in range(size // 4)]
    far = [[4 * a + b for a in range(size // 4)] for b in range(4)]
    got = lax.all_to_all(payload, "ctx", 0, 0, axis_index_groups=near, tiled=True)

    outs = pl.pallas_call(
        rest_kernel,
        grid=(steps,),
        in_specs=[spectrum, spectrum, whole(EXT, LEN), whole(EXT, LEN), stream, stream, cols(EXT), cols(EXT),
                  cols(EXT), cols(EXT), stream, stream, one, one, cols(7), whole(EXT, 128), whole(EXT, 128)],
        out_specs=[stream] * 5,
        out_shape=[shape(ROWS, BF)] * 5,
        scratch_shapes=[pltpu.VMEM((ROWS, CB), F32), pltpu.VMEM((EXT, CB), F32)],
        compiler_params=params,
        name="rest",
    )(xspec, hspec, *back, upstream, key_mr, mixed, conv, gp, gc, key_se, value_se, gain2, skip2, filter_se,
      scale, coef)

    merged = pl.pallas_call(
        merge_kernel, out_shape=jax.ShapeDtypeStruct((16, 24, 128), BF), name="merge"
    )(got)
    got = lax.all_to_all(merged, "ctx", 0, 0, axis_index_groups=far, tiled=True)
    factor = 1.0 / math.sqrt(ROWS * size)
    se, mr, sk, ga = pl.pallas_call(
        lambda *refs: final_kernel(*refs, factor=factor),
        out_shape=[jax.ShapeDtypeStruct((7, 16), F32), jax.ShapeDtypeStruct((128, 16), F32),
                   jax.ShapeDtypeStruct((1, 16), F32), jax.ShapeDtypeStruct((1, 16), F32)],
        name="final",
    )(got)
    return (*outs, se, mr, sk.reshape(16), ga.reshape(16))


def solution(mesh):
    both, part = P("ctx", "tp"), P(None, "tp")
    in_specs = (both,) * 6 + (part, part, P("tp"), P("tp"))
    split_all = ("tp", "ctx")
    out_specs = (both,) * 5 + (P(None, split_all), P(None, split_all), P(split_all), P(split_all))
    return jax.shard_map(local, mesh=mesh, in_specs=in_specs, out_specs=out_specs, check_vma=False)
```

time: 175 us -> 100 us (0.57)
  the two profiles are of different devices: /device:TPU:1 before, /device:TPU:32 now
where the time goes in v1:
time: 100 us; the launch traced here: 99 us
  Pallas kernels  28.3 us (28%)
  blocking collectives  23.7 us (24%)
  starting transfers between devices  20.8 us (21%)
  local copies, waits for them, and re-layouts  18.1 us (18%)
  waiting for transfers between devices  7.16 us (7%)
    unnamed x69, local copies, waits for them, and re-layouts  18.1 us
    all_to_all x1, starting transfers between devices, local(): got = lax.all_to_all(merged, 'ctx', 0, 0, axis_index_groups=far, tiled=True)  16.3 us
    all_to_all x1, blocking collectives, local(): stats = lax.all_to_all(stats, 'tp', 0, 0, tiled=True)  14.1 us
    all_to_all x1, blocking collectives, local(): lax.all_to_all(payload, 'ctx', 0, 0, axis_index_groups=near, tiled=True)  9.56 us
    pallas_call x1, Pallas kernels, local(): pl.pallas_call(filter_kernel, grid=(steps,), in_specs=[whole(8, 8, 128),...  8.55 us
    pallas_call x1, Pallas kernels, local(): pl.pallas_call(norm_kernel, grid=(steps,), in_specs=[cols(FWD), cols(BWD)...  7.36 us
    pallas_call x1, Pallas kernels, local(): pl.pallas_call(rest_kernel, grid=(steps,), in_specs=[spectrum, spectrum,...  5.26 us
    all_to_all x1, waiting for transfers between devices, local(): got = lax.all_to_all(merged, 'ctx', 0, 0, axis_index_groups=far, tiled=True)  4.47 us
  transfers between devices with their start and end apart: 3, of which 2 were waited for; matrix products, arithmetic and copies ran while one was open for 0% of the time, Pallas kernels for 7%

profile of v1, /device:TPU:32, one launch (start us, length us, event | category | flops | bytes accessed | tf_op | source)
XLA Modules:
  0.0 99.0 jit_solution(9446785437545168494)
XLA Ops:
  0.7 1.0 %copy-done = bf16[224,1024]{1,0:T(8,128)(2,1)S(1)} copy-done((bf16[224,1024]{1,0:T(8,128)(2,1)S(1)}, bf16[224,1024]{1,0:T(8,128)(2,1)}, u32[]{:S(2)}) %copy-start) | copy-done | bytes 458776
  1.7 1.0 %copy-done.2 = bf16[224,1024]{1,0:T(8,128)(2,1)S(1)} copy-done((bf16[224,1024]{1,0:T(8,128)(2,1)S(1)}, bf16[224,1024]{1,0:T(8,128)(2,1)}, u32[]{:S(2)}) %copy-start.2) | copy-done | bytes 458776
  2.7 1.0 %copy-done.4 = bf16[224,1024]{1,0:T(8,128)(2,1)S(1)} copy-done((bf16[224,1024]{1,0:T(8,128)(2,1)S(1)}, bf16[224,1024]{1,0:T(8,128)(2,1)}, u32[]{:S(2)}) %copy-start.4) | copy-done | bytes 458776
  3.7 1.0 %copy-done.6 = bf16[224,1024]{1,0:T(8,128)(2,1)S(1)} copy-done((bf16[224,1024]{1,0:T(8,128)(2,1)S(1)}, bf16[224,1024]{1,0:T(8,128)(2,1)}, u32[]{:S(2)}) %copy-start.6) | copy-done | bytes 458776
  4.7 1.0 %copy-done.8 = bf16[224,1024]{1,0:T(8,128)(2,1)S(1)} copy-done((bf16[224,1024]{1,0:T(8,128)(2,1)S(1)}, bf16[224,1024]{1,0:T(8,128)(2,1)}, u32[]{:S(2)}) %copy-start.8) | copy-done | bytes 458776
  5.7 1.0 %copy-done.12 = bf16[224,1024]{1,0:T(8,128)(2,1)S(1)} copy-done((bf16[224,1024]{1,0:T(8,128)(2,1)S(1)}, bf16[224,1024]{1,0:T(8,128)(2,1)}, u32[]{:S(2)}) %copy-start.12) | copy-done | bytes 458776
  6.8 0.8 copy-done.26
  7.5 0.7 copy-done.30
  8.2 1.6 %send.1 = (bf16[144,1024]{1,0:T(8,128)(2,1)S(1)}, bf16[160,1024]{1,0:T(8,128)(2,1)S(1)}) custom-call(bf16[224,1024]{1,0:T(8,128)(2,1)S(1)} %copy-done.4, bf16[224,1024]{1,0:T(8,128)(2,1)S(1)} %copy-done.6, bf16[224,1024]{1,0:T(8,128)(2,1)S(1)} %copy-done.12, bf16[224,1024]{1,0:T(8,128)(2,1)S(1)} %copy-done.8, bf16[224,1024]{1,0:T(8,128)(2,1)S(1)} %copy-done, ...), custom_call_target="tpu_custom_call" | custom-call | tf_op jit(solution)/shard_map/send/pallas_call | solution.py:369
  9.9 2.6 %collective-permute-start.1 = (bf16[160,1024]{1,0:T(8,128)(2,1)S(1)}, bf16[160,1024]{1,0:T(8,128)(2,1)S(1)}, u32[]{:S(2)}, u32[]{:S(2)}) collective-permute-start(bf16[160,1024]{1,0:T(8,128)(2,1)S(1)} %get-tuple-element.32), channel_id=1, source_target_pairs={{8,0},{16,8},{24,16},{32,24},{40,32},{48,40},{56,48},{64,56},{72,6... | collective-permute-start | bytes 983048 | tf_op jit(solution)/shard_map/ppermute | solution.py:382
  12.5 1.9 %collective-permute-start = (bf16[144,1024]{1,0:T(8,128)(2,1)S(1)}, bf16[144,1024]{1,0:T(8,128)(2,1)S(1)}, u32[]{:S(2)}, u32[]{:S(2)}) collective-permute-start(bf16[144,1024]{1,0:T(8,128)(2,1)S(1)} %get-tuple-element.31), channel_id=1, source_target_pairs={{0,8},{8,16},{16,24},{24,32},{32,40},{40,48},{48,56},{56,64},{64,7... | collective-permute-start | bytes 884744 | tf_op jit(solution)/shard_map/ppermute | solution.py:383
  14.5 2.1 %local.1 = (f32[384,1024]{1,0:T(8,128)S(1)}, f32[384,1024]{1,0:T(8,128)S(1)}) custom-call(bf16[224,1024]{1,0:T(8,128)(2,1)S(1)} %copy-done.1, bf16[224,1024]{1,0:T(8,128)(2,1)S(1)} %copy-done.3, f32[128,1024]{1,0:T(8,128)S(1)} %copy-done.23, bf16[384,352]{1,0:T(8,128)(2,1)S(1)} %copy-done.20, bf16[384,352]{1,0:T(8,128)(2,1)S(1)} %copy-done.19), custom_call_target="tpu_custom_call" | custom-call | tf_op jit(solution)/shard_map/local/pallas_call | solution.py:386
  16.6 1.2 %copy-done.10 = f32[384,1024]{1,0:T(8,128)} copy-done((f32[384,1024]{1,0:T(8,128)}, f32[384,1024]{1,0:T(8,128)S(1)}, u32[]{:S(2)}) %copy-start.10) | copy-done | bytes 1572888
  17.8 1.1 %copy-done.11 = f32[384,1024]{1,0:T(8,128)} copy-done((f32[384,1024]{1,0:T(8,128)}, f32[384,1024]{1,0:T(8,128)S(1)}, u32[]{:S(2)}) %copy-start.11) | copy-done | bytes 1572888
  18.9 2.7 %collective-permute-done.fwd = bf16[144,1024]{1,0:T(8,128)(2,1)S(1)} collective-permute-done((bf16[144,1024]{1,0:T(8,128)(2,1)S(1)}, bf16[144,1024]{1,0:T(8,128)(2,1)S(1)}, u32[]{:S(2)}, u32[]{:S(2)}) %collective-permute-start) | collective-permute-done | bytes 294944 | tf_op jit(solution)/shard_map/ppermute | solution.py:383
  21.7 7.4 %norm.1 = (f32[232,1024]{1,0:T(8,128)S(1)}, f32[232,1024]{1,0:T(8,128)S(1)}, f32[232,1024]{1,0:T(8,128)}, f32[8,8,128]{2,1,0:T(8,128)S(1)}) custom-call(bf16[144,1024]{1,0:T(8,128)(2,1)S(1)} %collective-permute-done.fwd, bf16[160,1024]{1,0:T(8,128)(2,1)S(1)} %collective-permute-done.1.bwd, bf16[224,1024]{1,0:T(8,128)(2,1)S(1)} %copy-done.4, ...), custom_call_target="tpu_custom_call" | custom-call | tf_op jit(solution)/shard_map/norm/pallas_call | solution.py:396
  29.0 0.9 copy-done.14
  30.0 1.0 copy-done.21
  30.9 14.1 %all_to_all.15.stats = f32[8,8,128]{2,1,0:T(8,128)S(1)} all-to-all(f32[8,8,128]{2,1,0:T(8,128)S(1)} %get-tuple-element.35), channel_id=1, replica_groups=mesh['ctx'=64,'tp'=8] {'tp'}, dimensions={0} | all-to-all | bytes 65536 | tf_op jit(solution)/shard_map/all_to_all | solution.py:412
  45.1 8.6 %filters.1 = (bf16[4,288,128]{2,1,0:T(8,128)(2,1)S(1)}, f32[384,1024]{1,0:T(8,128)}, bf16[232,1024]{1,0:T(8,128)(2,1)S(1)}, f32[232,128]{1,0:T(8,128)S(1)}, f32[232,128]{1,0:T(8,128)S(1)}) custom-call(f32[8,8,128]{2,1,0:T(8,128)S(1)} %all_to_all.15.stats, bf16[144,1024]{1,0:T(8,128)(2,1)S(1)} %collective-permute-done.fwd, f32[232,1024]{1,0:T(8,128)} %copy-done.14, ...), custom_call_target="tpu_custom_call" | custom-call | tf_op jit(solution)/shard_map/filters/pallas_call | solution.py:414
  53.6 0.8 copy-done.24
  54.4 9.6 %all_to_all.16.got = bf16[4,288,128]{2,1,0:T(8,128)(2,1)} all-to-all(bf16[4,288,128]{2,1,0:T(8,128)(2,1)S(1)} %get-tuple-element.48), channel_id=1, replica_groups={{0,8,16,24},{32,40,48,56},{64,72,80,88},{96,104,112,120},{128,136,144,1..., dimensions={0} | all-to-all | bytes 589824 | tf_op jit(solution)/shard_map/all_to_all | solution.py:432
  64.0 1.6 %merge.1 = bf16[16,24,128]{2,1,0:T(8,128)(2,1)} custom-call(bf16[4,288,128]{2,1,0:T(8,128)(2,1)} %all_to_all.16.got), custom_call_target="tpu_custom_call" | custom-call | tf_op jit(solution)/shard_map/merge/pallas_call | solution.py:447
  65.6 16.3 %all-to-all-start.2 = ((bf16[16,24,128]{2,1,0:T(8,128)(2,1)}), bf16[16,24,128]{2,1,0:T(8,128)(2,1)S(1)}, u32[]{:S(2)}, u32[]{:S(2)}) async-start(bf16[16,24,128]{2,1,0:T(8,128)(2,1)} %merge.1), calls=%async_computation.2 | async-start | bytes 196608 | tf_op jit(solution)/shard_map/all_to_all | solution.py:450
  81.9 1.2 %copy-done.16 = f32[232,1024]{1,0:T(8,128)S(1)} copy-done((f32[232,1024]{1,0:T(8,128)S(1)}, f32[232,1024]{1,0:T(8,128)}, u32[]{:S(2)}) %copy-start.16) | copy-done | bytes 950296
  83.1 1.2 %copy-done.22 = f32[232,1024]{1,0:T(8,128)S(1)} copy-done((f32[232,1024]{1,0:T(8,128)S(1)}, f32[232,1024]{1,0:T(8,128)}, u32[]{:S(2)}) %copy-start.22) | copy-done | bytes 950296
  84.3 1.0 %copy-done.25 = bf16[232,1024]{1,0:T(8,128)(2,1)S(1)} copy-done((bf16[232,1024]{1,0:T(8,128)(2,1)S(1)}, bf16[232,1024]{1,0:T(8,128)(2,1)}, u32[]{:S(2)}) %copy-start.25) | copy-done | bytes 475160
  85.3 5.3 %rest.1 = (bf16[224,1024]{1,0:T(8,128)(2,1)}, bf16[224,1024]{1,0:T(8,128)(2,1)}, bf16[224,1024]{1,0:T(8,128)(2,1)}, bf16[224,1024]{1,0:T(8,128)(2,1)}, bf16[224,1024]{1,0:T(8,128)(2,1)}) custom-call(f32[384,1024]{1,0:T(8,128)} %get-tuple-element.38.xspec, f32[384,1024]{1,0:T(8,128)} %copy-done.10, bf16[232,384]{1,0:T(8,128)(2,1)S(1)} %copy-done.18, ...), custom_call_target="tpu_custom_call" | custom-call | tf_op jit(solution)/shard_map/rest/pallas_call | solution.py:434
  90.6 4.5 %all-to-all-done.2.refs_0_ = bf16[16,24,128]{2,1,0:T(8,128)(2,1)S(1)} async-done(((bf16[16,24,128]{2,1,0:T(8,128)(2,1)}), bf16[16,24,128]{2,1,0:T(8,128)(2,1)S(1)}, u32[]{:S(2)}, u32[]{:S(2)}) %all-to-all-start.2) | async-done | bytes 98336 | tf_op jit(solution)/shard_map/all_to_all | solution.py:450
  95.1 0.6 copy-done.33
  95.7 1.8 %final.1 = (f32[7,16]{1,0:T(8,128)}, f32[128,16]{1,0:T(8,128)}, f32[1,16]{1,0:T(1,128)}, f32[1,16]{1,0:T(1,128)}) custom-call(bf16[16,24,128]{2,1,0:T(8,128)(2,1)} %copy-done.33), custom_call_target="tpu_custom_call" | custom-call | tf_op jit(solution)/shard_map/final/pallas_call | solution.py:452
  97.5 1.5 %copy.25 = f32[128,16]{0,1:T(8,128)} copy(f32[128,16]{1,0:T(8,128)} %get-tuple-element.59) | data formatting | bytes 16384
  (52 shorter events, 0.1 us)
Async XLA Ops:
  0.6 1.0 %copy-start = (bf16[224,1024]{1,0:T(8,128)(2,1)S(1)}, bf16[224,1024]{1,0:T(8,128)(2,1)}, u32[]{:S(2)}) copy-start(bf16[224,1024]{1,0:T(8,128)(2,1)} %up.9) | copy-start | bytes 1376260
  1.7 1.0 %copy-start.2 = (bf16[224,1024]{1,0:T(8,128)(2,1)S(1)}, bf16[224,1024]{1,0:T(8,128)(2,1)}, u32[]{:S(2)}) copy-start(bf16[224,1024]{1,0:T(8,128)(2,1)} %qmr.7) | copy-start | bytes 1376260
  2.7 1.0 %copy-start.4 = (bf16[224,1024]{1,0:T(8,128)(2,1)S(1)}, bf16[224,1024]{1,0:T(8,128)(2,1)}, u32[]{:S(2)}) copy-start(bf16[224,1024]{1,0:T(8,128)(2,1)} %kse.7) | copy-start | bytes 1376260
  3.7 1.0 %copy-start.6 = (bf16[224,1024]{1,0:T(8,128)(2,1)S(1)}, bf16[224,1024]{1,0:T(8,128)(2,1)}, u32[]{:S(2)}) copy-start(bf16[224,1024]{1,0:T(8,128)(2,1)} %vse.7) | copy-start | bytes 1376260
  4.7 1.0 %copy-start.8 = (bf16[224,1024]{1,0:T(8,128)(2,1)S(1)}, bf16[224,1024]{1,0:T(8,128)(2,1)}, u32[]{:S(2)}) copy-start(bf16[224,1024]{1,0:T(8,128)(2,1)} %kmr.7) | copy-start | bytes 1376260
  5.7 1.0 %copy-start.12 = (bf16[224,1024]{1,0:T(8,128)(2,1)S(1)}, bf16[224,1024]{1,0:T(8,128)(2,1)}, u32[]{:S(2)}) copy-start(bf16[224,1024]{1,0:T(8,128)(2,1)} %qse.5) | copy-start | bytes 1376260
  8.2 6.3 %copy-start.1 = (bf16[224,1024]{1,0:T(8,128)(2,1)S(1)}, bf16[224,1024]{1,0:T(8,128)(2,1)}, u32[]{:S(2)}) copy-start(bf16[224,1024]{1,0:T(8,128)(2,1)} %up.9) | copy-start | bytes 1376260
  8.2 6.3 %copy-start.3 = (bf16[224,1024]{1,0:T(8,128)(2,1)S(1)}, bf16[224,1024]{1,0:T(8,128)(2,1)}, u32[]{:S(2)}) copy-start(bf16[224,1024]{1,0:T(8,128)(2,1)} %qmr.7) | copy-start | bytes 1376260
  8.2 6.3 %copy-start.19 = (bf16[384,352]{1,0:T(8,128)(2,1)S(1)}, bf16[384,352]{1,0:T(8,128)(2,1)}, u32[]{:S(2)}) copy-start(bf16[384,352]{1,0:T(8,128)(2,1)} %constant.13.clone.fxl) | copy-start | bytes 811012
  8.2 6.3 %copy-start.20 = (bf16[384,352]{1,0:T(8,128)(2,1)S(1)}, bf16[384,352]{1,0:T(8,128)(2,1)}, u32[]{:S(2)}) copy-start(bf16[384,352]{1,0:T(8,128)(2,1)} %constant.12.clone.fxh) | copy-start | bytes 811012
  8.2 6.3 %copy-start.23 = (f32[128,1024]{1,0:T(8,128)S(1)}, f32[128,1024]{1,0:T(8,128)}, u32[]{:S(2)}) copy-start(f32[128,1024]{1,0:T(8,128)} %fmr.1) | copy-start | bytes 1572868
  9.8 11.8 %copy-start.9 = (bf16[224,1024]{1,0:T(8,128)(2,1)S(1)}, bf16[224,1024]{1,0:T(8,128)(2,1)}, u32[]{:S(2)}) copy-start(bf16[224,1024]{1,0:T(8,128)(2,1)} %kmr.7) | copy-start | bytes 1376260
  9.8 11.8 %copy-start.13 = (bf16[224,1024]{1,0:T(8,128)(2,1)S(1)}, bf16[224,1024]{1,0:T(8,128)(2,1)}, u32[]{:S(2)}) copy-start(bf16[224,1024]{1,0:T(8,128)(2,1)} %qse.5) | copy-start | bytes 1376260
  9.9 11.8 %copy-start.17 = (bf16[232,384]{1,0:T(8,128)(2,1)S(1)}, bf16[232,384]{1,0:T(8,128)(2,1)}, u32[]{:S(2)}) copy-start(bf16[232,384]{1,0:T(8,128)(2,1)} %constant.17.clone.tl) | copy-start | bytes 534532
  9.9 11.7 %copy-start.18 = (bf16[232,384]{1,0:T(8,128)(2,1)S(1)}, bf16[232,384]{1,0:T(8,128)(2,1)}, u32[]{:S(2)}) copy-start(bf16[232,384]{1,0:T(8,128)(2,1)} %constant.16.clone.th) | copy-start | bytes 534532
  9.9 11.7 %copy-start.27 = (f32[7,1024]{1,0:T(8,128)S(1)}, f32[7,1024]{1,0:T(8,128)}, u32[]{:S(2)}) copy-start(f32[7,1024]{1,0:T(8,128)} %fse.5) | copy-start | bytes 86020
  9.9 11.7 %copy-start.28 = (bf16[384,136]{1,0:T(8,128)(2,1)S(1)}, bf16[384,136]{1,0:T(8,128)(2,1)}, u32[]{:S(2)}) copy-start(bf16[384,136]{1,0:T(8,128)(2,1)} %constant.15.clone.fhl) | copy-start | bytes 313348
  9.9 11.7 %copy-start.29 = (bf16[384,136]{1,0:T(8,128)(2,1)S(1)}, bf16[384,136]{1,0:T(8,128)(2,1)}, u32[]{:S(2)}) copy-start(bf16[384,136]{1,0:T(8,128)(2,1)} %constant.14.clone.fhh) | copy-start | bytes 313348
  9.9 11.7 %copy-start.31 = (f32[1024]{0:T(1024)S(1)}, f32[1024]{0:T(1024)}, u32[]{:S(2)}) copy-start(f32[1024]{0:T(1024)} %param.25) | copy-start | bytes 12292
  9.9 11.7 %copy-start.32 = (f32[1024]{0:T(1024)S(1)}, f32[1024]{0:T(1024)}, u32[]{:S(2)}) copy-start(f32[1024]{0:T(1024)} %param.24) | copy-start | bytes 12292
  9.9 11.7 %collective-permute-start.1 = (bf16[160,1024]{1,0:T(8,128)(2,1)S(1)}, bf16[160,1024]{1,0:T(8,128)(2,1)S(1)}, u32[]{:S(2)}, u32[]{:S(2)}) collective-permute-start(bf16[160,1024]{1,0:T(8,128)(2,1)S(1)} %get-tuple-element.32), channel_id=1, source_target_pairs={{8,0},{16,8},{24,16},{32,24},{40,32},{48,40},{56,48},{64,56},{72,6... | collective-permute-start | bytes 983048 | tf_op jit(solution)/shard_map/ppermute | solution.py:382
  12.5 9.0 %collective-permute-start = (bf16[144,1024]{1,0:T(8,128)(2,1)S(1)}, bf16[144,1024]{1,0:T(8,128)(2,1)S(1)}, u32[]{:S(2)}, u32[]{:S(2)}) collective-permute-start(bf16[144,1024]{1,0:T(8,128)(2,1)S(1)} %get-tuple-element.31), channel_id=1, source_target_pairs={{0,8},{8,16},{16,24},{24,32},{32,40},{40,48},{48,56},{56,64},{64,7... | collective-permute-start | bytes 884744 | tf_op jit(solution)/shard_map/ppermute | solution.py:383
  16.6 1.2 %copy-start.10 = (f32[384,1024]{1,0:T(8,128)}, f32[384,1024]{1,0:T(8,128)S(1)}, u32[]{:S(2)}) copy-start(f32[384,1024]{1,0:T(8,128)S(1)} %get-tuple-element.34.hspec) | copy-start | bytes 4718596
  17.8 1.1 %copy-start.11 = (f32[384,1024]{1,0:T(8,128)}, f32[384,1024]{1,0:T(8,128)S(1)}, u32[]{:S(2)}) copy-start(f32[384,1024]{1,0:T(8,128)S(1)} %get-tuple-element.33.gloc) | copy-start | bytes 4718596
  30.0 1.0 copy-start.21
  45.1 36.8 %copy-start.5 = (bf16[224,1024]{1,0:T(8,128)(2,1)S(1)}, bf16[224,1024]{1,0:T(8,128)(2,1)}, u32[]{:S(2)}) copy-start(bf16[224,1024]{1,0:T(8,128)(2,1)} %kse.7) | copy-start | bytes 1376260
  45.1 36.8 %copy-start.7 = (bf16[224,1024]{1,0:T(8,128)(2,1)S(1)}, bf16[224,1024]{1,0:T(8,128)(2,1)}, u32[]{:S(2)}) copy-start(bf16[224,1024]{1,0:T(8,128)(2,1)} %vse.7) | copy-start | bytes 1376260
  54.4 27.5 %copy-start.15 = (f32[232,1024]{1,0:T(8,128)S(1)}, f32[232,1024]{1,0:T(8,128)}, u32[]{:S(2)}) copy-start(f32[232,1024]{1,0:T(8,128)} %copy-done.14) | copy-start | bytes 2850820
  65.6 29.5 %all-to-all-start.2 = ((bf16[16,24,128]{2,1,0:T(8,128)(2,1)}), bf16[16,24,128]{2,1,0:T(8,128)(2,1)S(1)}, u32[]{:S(2)}, u32[]{:S(2)}) async-start(bf16[16,24,128]{2,1,0:T(8,128)(2,1)} %merge.1), calls=%async_computation.2 | async-start | bytes 196608 | tf_op jit(solution)/shard_map/all_to_all | solution.py:450
  81.9 1.2 %copy-start.16 = (f32[232,1024]{1,0:T(8,128)S(1)}, f32[232,1024]{1,0:T(8,128)}, u32[]{:S(2)}) copy-start(f32[232,1024]{1,0:T(8,128)} %get-tuple-element.37.gp) | copy-start | bytes 2850820
  83.1 1.2 %copy-start.22 = (f32[232,1024]{1,0:T(8,128)S(1)}, f32[232,1024]{1,0:T(8,128)}, u32[]{:S(2)}) copy-start(f32[232,1024]{1,0:T(8,128)} %copy-done.21) | copy-start | bytes 2850820
  84.3 1.0 %copy-start.25 = (bf16[232,1024]{1,0:T(8,128)(2,1)S(1)}, bf16[232,1024]{1,0:T(8,128)(2,1)}, u32[]{:S(2)}) copy-start(bf16[232,1024]{1,0:T(8,128)(2,1)} %copy-done.24) | copy-start | bytes 1425412
  (5 other events, 3.8 us)

commit v2 on v1

v2 whole, which is shorter than its diff:
```python
import math

import jax
import jax.numpy as jnp
import numpy as np
from jax import lax
from jax.experimental import pallas as pl
from jax.experimental.pallas import tpu as pltpu
from jax.sharding import PartitionSpec as P

D = 8192
EPSILON = 0.1
BF = jnp.bfloat16
F32 = jnp.float32

LEN = 384
HALF = LEN // 2
ROWS = 224
EXT = ROWS + 8
HALO = 128
HEAD = 136
CB = 256
FWD = HALO + 8 + 8
BWD = HEAD + 24
CHUNK = 32


def basis(first, last):
    theta = np.pi * (2 * np.arange(HALF)[:, None] + 1) / LEN * np.arange(first, last)[None, :]
    return np.concatenate([np.cos(theta), -np.sin(theta)], 0)


def halves(matrix):
    high = matrix.astype(BF)
    low = (matrix - high.astype(np.float64)).astype(BF)
    return high, low


def dot(a, b):
    return jnp.dot(a, b, preferred_element_type=F32)


def split(x):
    high = x.astype(BF)
    return high, (x - high.astype(F32)).astype(BF)


def forward(fh, fl, data):
    return dot(fh, data) + dot(fl, data)


def inverse(th, tl, spectrum):
    high, low = split(spectrum)
    return dot(th, high) + dot(tl, high) + dot(th, low)


def wide(column):
    return jnp.concatenate([column] * (CB // 128), axis=1)


def folded(x):
    total = x[:, :128]
    for at in range(128, x.shape[1], 128):
        total = total + x[:, at : at + 128]
    return total


def sums_in_lanes(acc):
    ones = jnp.ones((8, 128), F32)
    return lax.dot_general(
        ones, acc, (((1,), (1,)), ((), ())), precision=lax.Precision.HIGHEST, preferred_element_type=F32
    )


def short_conv(ref, taps, row, count):
    total = None
    for step in range(7):
        term = taps[step : step + 1, :] * ref[pl.ds(row - step, count), :]
        total = term if total is None else total + term
    return total


def short_adjoint(ref, taps, row, count):
    total = None
    for step in range(7):
        term = taps[step : step + 1, :] * ref[pl.ds(row + step, count), :]
        total = term if total is None else total + term
    return total


def rounded(x):
    return x.astype(BF).astype(F32)


def block(b):
    return pl.ds(pl.multiple_of(b * CB, CB), CB)


def eights(x):
    total = x[:8]
    for r in range(8, x.shape[0], 8):
        total = total + x[r : r + 8]
    return total


def send_kernel(
    kse, vse, qse, kmr, up, qmr, fse, gain, fwd, bwd,
    kse_t, vse_t, qse_t, kmr_t, up_h, qmr_h, kse_h, vse_h, qse_h, kmr_h, taps_v, gain_v, sems, prod, acc
):
    last = ROWS - HALO
    first = last - 16
    pieces = [
        (up.at[pl.ds(0, HEAD)], up_h), (qmr.at[pl.ds(0, HEAD)], qmr_h),
        (qse.at[pl.ds(0, 8)], qse_h), (kmr.at[pl.ds(0, 8)], kmr_h),
        (kse.at[pl.ds(0, 8)], kse_h), (vse.at[pl.ds(0, 8)], vse_h),
        (kse.at[pl.ds(first, HALO + 16)], kse_t), (vse.at[pl.ds(first, HALO + 16)], vse_t), (fse, taps_v),
        (qse.at[pl.ds(last, HALO)], qse_t), (kmr.at[pl.ds(last, HALO)], kmr_t), (gain, gain_v),
    ]
    copies = [pltpu.make_async_copy(src, dst, sems.at[k]) for k, (src, dst) in enumerate(pieces)]
    for copy in copies:
        copy.start()
    acc[...] = jnp.zeros_like(acc)
    fwd[HALO + 8 :] = jnp.zeros((8, fwd.shape[1]), BF)
    for copy in copies[:6]:
        copy.wait()

    def head(b, carry):
        c = block(b)
        bwd[:HEAD, c] = (up_h[:, c].astype(F32) * qmr_h[:, c].astype(F32)).astype(BF)
        bwd[HEAD : HEAD + 8, c] = qse_h[:, c]
        bwd[HEAD + 8 : HEAD + 16, c] = kmr_h[:, c]
        bwd[HEAD + 16 :, c] = (kse_h[:, c].astype(F32) * vse_h[:, c].astype(F32)).astype(BF)
        return carry

    lax.fori_loop(0, fwd.shape[1] // CB, head, 0)
    for copy in copies[6:]:
        copy.wait()

    def tail(b, carry):
        c = block(b)
        product = rounded(kse_t[:, c].astype(F32) * vse_t[:, c].astype(F32))
        prod[...] = product
        taps, gains = taps_v[:, c], gain_v[:, c]
        for r in range(0, HALO, CHUNK):
            conv = short_conv(prod, taps, 16 + r, CHUNK)
            mixed = qse_t[r : r + CHUNK, c].astype(F32) * conv
            fwd[r : r + CHUNK, c] = (kmr_t[r : r + CHUNK, c].astype(F32) * mixed * gains).astype(BF)
            acc[r : r + CHUNK] += folded(mixed * mixed)
        fwd[HALO : HALO + 8, c] = product[HALO + 8 :].astype(BF)
        return carry

    lax.fori_loop(0, fwd.shape[1] // CB, tail, 0)
    total = sums_in_lanes(acc[...])
    high = total.astype(BF).astype(F32)
    rows = lax.broadcasted_iota(jnp.int32, (8, 128), 0)
    fwd[HALO + 8 :, :128] = jnp.where(rows == 0, high, jnp.where(rows == 1, total - high, 0.0)).astype(BF)


def local_kernel(
    up, qmr, kse, vse, qse, fmr, fse, fxh, fxl, gloc, hspec, conv_o, mixed_o, acc_o, prod
):
    acc_o[...] = jnp.zeros_like(acc_o)
    prod[:8] = jnp.zeros((8, CB), F32)

    def step(b, carry):
        c = block(b)
        g = (up[:, c].astype(F32) * qmr[:, c].astype(F32)).astype(BF)
        gloc[:, c] = forward(fxh[:, HALO:], fxl[:, HALO:], g)
        high, low = split(fmr[:, c])
        fh = fxh[:, HALO : HALO + 128]
        hspec[:, c] = dot(fh, high) + dot(fxl[:, HALO : HALO + 128], high) + dot(fh, low)
        prod[8:] = rounded(kse[:, c].astype(F32) * vse[:, c].astype(F32))
        taps = fse[:, c]
        for at in range(0, ROWS, CHUNK):
            conv = short_conv(prod, taps, 8 + at, CHUNK)
            mixed = qse[at : at + CHUNK, c].astype(F32) * conv
            conv_o[at : at + CHUNK, c] = conv
            mixed_o[at : at + CHUNK, c] = mixed
            square = folded(mixed * mixed)
            if at == 0:
                acc_o[8:CHUNK] += square[8:]
            else:
                acc_o[at : at + CHUNK] += square
        return carry

    lax.fori_loop(0, up.shape[1] // CB, step, 0)


def norm_kernel(
    fwd, bwd, kse, vse, qse, kmr, up, qmr, fse, gain, skip, gloc, hspec, mixed, acc_in, fhh, th,
    gp_o, conv_e, mixed_e, stats, prod, acc_sq, acc_w
):
    acc_sq[...] = acc_in[...]
    acc_w[...] = jnp.zeros_like(acc_w)

    def step(b, carry):
        c = block(b)
        spec = gloc[:, c] + dot(fhh[...], bwd[:HEAD, c])
        h = hspec[:, c]
        gr, gi, hr, hi = spec[:HALF], spec[HALF:], h[:HALF], h[HALF:]
        back = jnp.concatenate([(gr * hr + gi * hi).astype(BF), (gi * hr - gr * hi).astype(BF)], 0)
        gp_o[:, c] = dot(th[...], back)
        taps, gains, skips = fse[:, c], gain[:, c], skip[:, c]
        prod[:8] = fwd[HALO : HALO + 8, c].astype(F32)
        prod[8:16] = rounded(kse[:8, c].astype(F32) * vse[:8, c].astype(F32))
        prod[16:24] = rounded(kse[ROWS - 8 :, c].astype(F32) * vse[ROWS - 8 :, c].astype(F32))
        prod[24:] = bwd[HEAD + 16 :, c].astype(F32)
        edges = []
        for k, query in ((0, qse[:8, c]), (1, bwd[HEAD : HEAD + 8, c])):
            conv = short_conv(prod, taps, 8 + 16 * k, 8)
            edge = query.astype(F32) * conv
            conv_e[8 * k : 8 * k + 8, c] = conv
            mixed_e[8 * k : 8 * k + 8, c] = edge
            edges.append(edge)
            at = ROWS * k
            acc_sq[at : at + 8] += folded(edge * edge)

        def rows(at, count, mix, key, g):
            gp = gp_o[at : at + count, c] + skips * g
            gp_o[at : at + count, c] = gp
            acc_w[at : at + count] += folded(gp * key.astype(F32) * gains * mix)

        for at in range(0, ROWS, CHUNK):
            s = slice(at, at + CHUNK)
            mix = mixed[s, c]
            if at == 0:
                mix = jnp.concatenate([edges[0], mix[8:]], 0)
            rows(at, CHUNK, mix, kmr[s, c], rounded(up[s, c].astype(F32) * qmr[s, c].astype(F32)))
        rows(ROWS, 8, edges[1], bwd[HEAD + 8 : HEAD + 16, c], bwd[:8, c].astype(F32))
        return carry

    lax.fori_loop(0, gloc.shape[1] // CB, step, 0)
    sq = sums_in_lanes(acc_sq[...])
    w = sums_in_lanes(acc_w[...])
    sent = fwd[HALO + 8 :, :128].astype(F32)
    mine = jnp.concatenate(
        [sq[:1, :128], sq[:1, 128:], w[:1, :128], w[:1, 128:], sent[:1] + sent[1:2], jnp.zeros((3, 128), F32)], 0
    )
    for dev in range(8):
        stats[dev] = mine


def column(total, row):
    pick = (lax.broadcasted_iota(jnp.int32, (8, 128), 0) == row).astype(F32)
    return lax.dot_general(
        total, pick, (((0,), (0,)), ((), ())), precision=lax.Precision.HIGHEST, preferred_element_type=F32
    )


def finish_kernel(
    stats, fwd, mixed, conv, mixed_e, conv_e, gp, kmr, qse, up, qmr, kse, vse, bwd, gain, skip, fse, gloc, hspec,
    fxh, th, gqse, gkse, gvse, gqmr, gkmr, payload,
    prod, scale_s, coef_s, halo_s, small, xin, gcf, o0, o1, o2, o3, o4, sems
):
    steps = gloc.shape[1] // CB
    total = stats[0]
    for dev in range(1, 8):
        total = total + stats[dev]
    s0 = lax.rsqrt(column(total, 0) / D + EPSILON)
    s1 = lax.rsqrt(column(total, 1) / D + EPSILON)
    scale_s[:128] = s0
    scale_s[128:] = s1
    coef_s[:128] = s0 * s0 * s0 * (column(total, 2) / D)
    coef_s[128:] = s1 * s1 * s1 * (column(total, 3) / D)
    halo_s[...] = lax.rsqrt(column(total, 4) / D + EPSILON)
    outs = ((o0, gqse), (o1, gkse), (o2, gvse), (o3, gqmr), (o4, gkmr))

    def out_copies(b):
        c = block(b)
        return [pltpu.make_async_copy(src.at[:, c], dst.at[:, c], sems.at[k, b]) for k, (src, dst) in enumerate(outs)]

    def step(b, carry):
        c = block(b)
        for at in range(0, HALO, CHUNK):
            s = slice(at, at + CHUNK)
            xin[s] = (fwd[s, c].astype(F32) * wide(halo_s[s])).astype(BF)
        prod[:8] = fwd[HALO : HALO + 8, c].astype(F32)
        prod[8:] = rounded(kse[:, c].astype(F32) * vse[:, c].astype(F32))
        gains, taps, skips = gain[:, c], fse[:, c], skip[:, c]
        sums = [jnp.zeros((8, CB), F32) for _ in range(9)]

        def mix_of(at, count):
            mix, con = mixed[at : at + count, c], conv[at : at + count, c]
            if at == 0:
                mix = jnp.concatenate([mixed_e[:8, c], mix[8:]], 0)
                con = jnp.concatenate([conv_e[:8, c], con[8:]], 0)
            return mix, con

        for at in range(0, ROWS, CHUNK):
            s = slice(at, at + CHUNK)
            mix, con = mix_of(at, CHUNK)
            scale = wide(scale_s[s])
            key = kmr[s, c].astype(F32)
            grad = gp[s, c]
            gn = grad * key
            ms = mix * scale
            normed = ms * gains
            gm = gains * scale * gn - mix * wide(coef_s[s])
            gc = rounded(gm * qse[s, c].astype(F32))
            gcf[s] = gc
            o0[s, c] = (gm * con).astype(BF)
            o4[s, c] = (grad * normed).astype(BF)
            pm = (key * normed).astype(BF)
            xin[HALO + at : HALO + at + CHUNK] = pm
            g = rounded(up[s, c].astype(F32) * qmr[s, c].astype(F32))
            for tap in range(7):
                sums[tap] = sums[tap] + eights(gc * prod[pl.ds(8 + at - tap, CHUNK), :])
            sums[7] = sums[7] + eights(g * pm.astype(F32))
            sums[8] = sums[8] + eights(gn * ms)
        nxt = slice(ROWS, ROWS + 8)
        gn = gp[nxt, c] * bwd[HEAD + 8 : HEAD + 16, c].astype(F32)
        gm = gains * wide(scale_s[nxt]) * gn - mixed_e[8:, c] * wide(coef_s[nxt])
        gcf[nxt] = rounded(gm * bwd[HEAD : HEAD + 8, c].astype(F32))
        parts = [jnp.sum(x, axis=0, keepdims=True) for x in sums]
        small[b] = jnp.concatenate(parts + [jnp.zeros((7, CB), F32)], 0)

        x = dot(fxh[...], xin[...])
        gl, h = gloc[:, c], hspec[:, c]
        xr, xi, gr, gi, hr, hi = x[:HALF], x[HALF:], gl[:HALF], gl[HALF:], h[:HALF], h[HALF:]
        back = jnp.concatenate([(gr * xr + gi * xi).astype(BF), (gi * xr - gr * xi).astype(BF)], 0)
        corr = dot(th[:128], back).T.astype(BF)
        for zz in range(4):
            for yc in range(4):
                at = pl.multiple_of((4 * b + zz) * 16, 16)
                payload[yc, pl.ds(at, 16), :] = corr[zz * 64 + yc * 16 : zz * 64 + yc * 16 + 16]
        spec = jnp.concatenate([(xr * hr - xi * hi).astype(BF), (xi * hr + xr * hi).astype(BF)], 0)
        ym = dot(th[:ROWS], spec)
        for at in range(0, ROWS, CHUNK):
            s = slice(at, at + CHUNK)
            pm = xin[HALO + at : HALO + at + CHUNK].astype(F32)
            o3[s, c] = (up[s, c].astype(F32) * (ym[s] + skips * pm)).astype(BF)
            gps = short_adjoint(gcf, taps, at, CHUNK)
            o1[s, c] = (gps * vse[s, c].astype(F32)).astype(BF)
            o2[s, c] = (gps * kse[s, c].astype(F32)).astype(BF)
        for copy in out_copies(b):
            copy.start()
        return carry

    lax.fori_loop(0, steps, step, 0)

    lane = lax.broadcasted_iota(jnp.int32, (16, 128), 1)
    row = lax.broadcasted_iota(jnp.int32, (16, 128), 0)
    spread = (lane % 16 == row).astype(BF)
    chan = lax.broadcasted_iota(jnp.int32, (CB, 128), 0)
    keep = chan % 8 == lax.broadcasted_iota(jnp.int32, (CB, 128), 1) // 16
    out_row = lax.broadcasted_iota(jnp.int32, (128, CB), 0)
    out_chan = lax.broadcasted_iota(jnp.int32, (128, CB), 1)
    packed = None
    for b in range(steps):
        tiled = lax.dot_general(
            small[b].astype(BF), spread, (((0,), (0,)), ((), ())), preferred_element_type=F32
        )
        masked = jnp.where(keep, tiled, 0.0).astype(BF)
        ch = out_chan + b * CB
        take = (out_row // 32 == (ch // 16) % 4) & ((out_row // 2) % 16 == ch // 64) & (out_row % 2 == (ch // 8) % 2)
        part = dot(take.astype(BF), masked)
        packed = part if packed is None else packed + part
    packed = packed.astype(BF)
    for yc in range(4):
        payload[yc, 256:] = packed[yc * 32 : yc * 32 + 32]
    for b in range(steps):
        for copy in out_copies(b):
            copy.wait()


def merge_kernel(got, out):
    total = got[0].astype(F32)
    for k in range(1, 4):
        total = total + got[k].astype(F32)
    for z in range(16):
        out[z, :16] = total[z * 16 : z * 16 + 16].astype(BF)
        pair = total[256 + z * 2 : 256 + z * 2 + 2]
        out[z, 16:] = jnp.concatenate([pair, jnp.zeros((6, 128), F32)], 0).astype(BF)


def final_kernel(got, se_o, mr_o, skip_o, gain_o, *, factor):
    total = got[0].astype(F32)
    for k in range(1, 16):
        total = total + got[k].astype(F32)
    total = total * factor
    mr_o[...] = total[:16]
    chan = lax.broadcasted_iota(jnp.int32, (16, 128), 0)
    lane = lax.broadcasted_iota(jnp.int32, (16, 128), 1)
    mine = jnp.where(chan < 8, total[16:17], total[17:18])
    mine = jnp.where(lane // 16 == chan % 8, mine, 0.0)
    pick = (lane % 16 == chan).astype(F32)
    small = lax.dot_general(
        pick, mine, (((1,), (1,)), ((), ())), precision=lax.Precision.HIGHEST, preferred_element_type=F32
    )
    se_o[...] = small[:7]
    skip_o[...] = small[7:8]
    gain_o[...] = small[8:9]


def local(
    query_se, key_se, value_se, query_mr, key_mr, upstream, filter_se, filter_mr, skip_mr, norm_gain
):
    chans = query_se.shape[1]
    steps = chans // CB
    size = lax.axis_size("ctx")
    skip2, gain2 = skip_mr.reshape(1, chans), norm_gain.reshape(1, chans)
    fxh, fxl = halves(basis(-HALO, ROWS))
    fhead, _ = halves(basis(ROWS, ROWS + HEAD))
    back, _ = halves(basis(0, EXT).T * (2.0 / LEN))

    def shape(rows, dtype):
        return jax.ShapeDtypeStruct((rows, chans), dtype)

    def vmem(rows, width, dtype):
        return pltpu.VMEM((rows, width), dtype)

    params = pltpu.CompilerParams(vmem_limit_bytes=16 * 1024 * 1024)
    hbm = pl.BlockSpec(memory_space=pltpu.HBM)
    sent = (key_se, value_se, query_se, key_mr, upstream, query_mr, filter_se, gain2)
    fwd, bwd = pl.pallas_call(
        send_kernel,
        in_specs=[hbm] * 8,
        out_shape=[shape(FWD, BF), shape(BWD, BF)],
        scratch_shapes=[vmem(HALO + 16, chans, BF)] * 2 + [vmem(HALO, chans, BF)] * 2 + [vmem(HEAD, chans, BF)] * 2
        + [vmem(8, chans, BF)] * 4 + [vmem(7, chans, F32), vmem(1, chans, F32), pltpu.SemaphoreType.DMA((12,)),
           vmem(HALO + 16, CB, F32), vmem(HALO, 128, F32)],
        compiler_params=params,
        name="send",
    )(*(pltpu.with_memory_space_constraint(x, pltpu.HBM) for x in sent))

    down = [(k, k + 1) for k in range(size - 1)]
    upward = [(k + 1, k) for k in range(size - 1)]
    bwd = lax.ppermute(bwd, "ctx", upward)
    fwd = lax.ppermute(fwd, "ctx", down)

    gloc, hspec, conv, mixed, acc = pl.pallas_call(
        local_kernel,
        out_shape=[shape(LEN, F32), shape(LEN, F32), shape(ROWS, F32), shape(ROWS, F32),
                   jax.ShapeDtypeStruct((256, 128), F32)],
        scratch_shapes=[vmem(ROWS + 8, CB, F32)],
        compiler_params=params,
        name="local",
    )(upstream, query_mr, key_se, value_se, query_se, filter_mr, filter_se, fxh, fxl)

    gp, conv_e, mixed_e, stats = pl.pallas_call(
        norm_kernel,
        out_shape=[shape(EXT, F32), shape(16, F32), shape(16, F32), jax.ShapeDtypeStruct((8, 8, 128), F32)],
        scratch_shapes=[vmem(32, CB, F32), vmem(256, 128, F32), vmem(256, 128, F32)],
        compiler_params=params,
        name="norm",
    )(fwd, bwd, key_se, value_se, query_se, key_mr, upstream, query_mr, filter_se, gain2, skip2, gloc, hspec,
      mixed, acc, fhead, back)

    stats = lax.all_to_all(stats, "tp", 0, 0, tiled=True)

    *outs, payload = pl.pallas_call(
        finish_kernel,
        out_specs=[hbm] * 5 + [pl.BlockSpec(memory_space=pltpu.VMEM)],
        out_shape=[shape(ROWS, BF)] * 5 + [jax.ShapeDtypeStruct((4, 288, 128), BF)],
        scratch_shapes=[
            vmem(ROWS + 8, CB, F32), vmem(256, 128, F32), vmem(256, 128, F32), vmem(HALO, 128, F32),
            pltpu.VMEM((steps, 16, CB), F32), vmem(HALO + ROWS, CB, BF), vmem(EXT, CB, F32),
        ] + [vmem(ROWS, chans, BF)] * 5 + [pltpu.SemaphoreType.DMA((5, steps))],
        compiler_params=params,
        name="finish",
    )(stats, fwd, mixed, conv, mixed_e, conv_e, gp, key_mr, query_se, upstream, query_mr, key_se, value_se, bwd,
      gain2, skip2, filter_se, gloc, hspec, fxh, back)

    near = [[4 * a + b for b in range(4)] for a in range(size // 4)]
    far = [[4 * a + b for a in range(size // 4)] for b in range(4)]
    got = lax.all_to_all(payload, "ctx", 0, 0, axis_index_groups=near, tiled=True)
    merged = pl.pallas_call(
        merge_kernel, out_shape=jax.ShapeDtypeStruct((16, 24, 128), BF), compiler_params=params, name="merge"
    )(got)
    got = lax.all_to_all(merged, "ctx", 0, 0, axis_index_groups=far, tiled=True)
    factor = 1.0 / math.sqrt(ROWS * size)
    se, mr, sk, ga = pl.pallas_call(
        lambda *refs: final_kernel(*refs, factor=factor),
        out_shape=[jax.ShapeDtypeStruct((7, 16), F32), jax.ShapeDtypeStruct((16, 128), F32),
                   jax.ShapeDtypeStruct((1, 16), F32), jax.ShapeDtypeStruct((1, 16), F32)],
        compiler_params=params,
        name="final",
    )(got)
    return (*outs, se, mr.T, sk.reshape(16), ga.reshape(16))


def solution(mesh):
    both, part = P("ctx", "tp"), P(None, "tp")
    in_specs = (both,) * 6 + (part, part, P("tp"), P("tp"))
    split_all = ("tp", "ctx")
    out_specs = (both,) * 5 + (P(None, split_all), P(None, split_all), P(split_all), P(split_all))
    return jax.shard_map(local, mesh=mesh, in_specs=in_specs, out_specs=out_specs, check_vma=False)
```

time: 100 us -> 77.7 us (0.78)
  blocking collectives: 23.7 us -> 52.2 us
  starting transfers between devices: 20.8 us -> 4.52 us
  local copies, waits for them, and re-layouts: 18.1 us -> 2.05 us
  Pallas kernels: 28.3 us -> 15.6 us
  waiting for transfers between devices: 7.16 us -> 2.18 us
    all_to_all x0 -> x1, blocking collectives: none -> 28.8 us  [local(): got = lax.all_to_all(merged, 'ctx', 0, 0, axis_index_groups=far, tiled=True)]
    all_to_all x1 -> x0, starting transfers between devices: 16.3 us -> none  [local(): got = lax.all_to_all(merged, 'ctx', 0, 0, axis_index_groups=far, tiled=True)]
    unnamed x69 -> x28, local copies, waits for them, and re-layouts: 18.1 us -> 2.05 us
    pallas_call x5 -> x4, Pallas kernels: 24.8 us -> 14.8 us  [the longest x1 6.97 us: local(): pl.pallas_call(finish_kernel, out_specs=[hbm] * 5 + [pl.BlockSpec(memory_...]
    all_to_all x1 -> x0, waiting for transfers between devices: 4.47 us -> none  [local(): got = lax.all_to_all(merged, 'ctx', 0, 0, axis_index_groups=far, tiled=True)]
    pallas_call x1, Pallas kernels: 1.65 us -> 0.05 us  [local(): pl.pallas_call(merge_kernel, out_shape=jax.ShapeDtypeStruct((16, 24, 128)...]
    pallas_call x1, Pallas kernels: 1.8 us -> 0.75 us  [local(): pl.pallas_call(lambda *refs: final_kernel(*refs, factor=factor), out_shap...]
  transfers between devices with their start and end apart: 3 -> 2, of which waited for: 2 -> 1; matrix products, arithmetic and copies ran while one was open for 0% -> 0% of each run, Pallas kernels for 7% -> 4%
where the time goes in v2:
time: 77.7 us; the launch traced here: 77.4 us
  blocking collectives  52.2 us (67%)
  Pallas kernels  15.6 us (20%)
  starting transfers between devices  4.52 us (6%)
  waiting for transfers between devices  2.18 us (3%)
  local copies, waits for them, and re-layouts  2.05 us (3%)
  between operations  0.85 us (1%)
    all_to_all x1, blocking collectives, local(): got = lax.all_to_all(merged, 'ctx', 0, 0, axis_index_groups=far, tiled=True)  28.8 us
    all_to_all x1, blocking collectives, local(): stats = lax.all_to_all(stats, 'tp', 0, 0, tiled=True)  14.2 us
    all_to_all x1, blocking collectives, local(): lax.all_to_all(payload, 'ctx', 0, 0, axis_index_groups=near, tiled=True)  9.19 us
    pallas_call x1, Pallas kernels, local(): pl.pallas_call(finish_kernel, out_specs=[hbm] * 5 + [pl.BlockSpec(memory_...  6.97 us
    pallas_call x1, Pallas kernels, local(): pl.pallas_call(local_kernel, out_shape=[shape(LEN, F32), shape(LEN, F32),...  2.85 us
    pallas_call x1, Pallas kernels, local(): pl.pallas_call(send_kernel, in_specs=[hbm] * 8, out_shape=[shape(FWD, BF)...  2.63 us
    ppermute x1, starting transfers between devices, local(): bwd = lax.ppermute(bwd, 'ctx', upward)  2.47 us
    pallas_call x1, Pallas kernels, local(): pl.pallas_call(norm_kernel, out_shape=[shape(EXT, F32), shape(16, F32), s...  2.38 us
  transfers between devices with their start and end apart: 2, of which 1 were waited for; matrix products, arithmetic and copies ran while one was open for 0% of the time, Pallas kernels for 4%

profile of v2, /device:TPU:32, one launch (start us, length us, event | category | flops | bytes accessed | tf_op | source)
XLA Modules:
  0.0 77.4 jit_solution(6099847788726159348)
XLA Ops:
  0.6 0.0 copy-start.6
  0.7 0.0 copy-start.8
  0.7 0.0 copy-start.3
  0.7 0.0 copy-start.4
  0.7 0.0 copy-start.1
  0.7 0.0 copy-start
  0.7 0.0 copy-start.2
  0.7 2.6 %send.1 = (bf16[144,1024]{1,0:T(8,128)(2,1)S(1)}, bf16[160,1024]{1,0:T(8,128)(2,1)S(1)}) custom-call(bf16[224,1024]{1,0:T(8,128)(2,1)} %kse.7, bf16[224,1024]{1,0:T(8,128)(2,1)} %vse.7, bf16[224,1024]{1,0:T(8,128)(2,1)} %qse.7, bf16[224,1024]{1,0:T(8,128)(2,1)} %kmr.5, bf16[224,1024]{1,0:T(8,128)(2,1)} %up.7, bf16[224,1024]{1,0:T(8,128)(2,1)} %qmr.7, ...), custom_call_target="tpu_custom_call" | custom-call | tf_op jit(solution)/shard_map/send/pallas_call | solution.py:415
  3.4 2.5 %collective-permute-start.1 = (bf16[160,1024]{1,0:T(8,128)(2,1)S(1)}, bf16[160,1024]{1,0:T(8,128)(2,1)S(1)}, u32[]{:S(2)}, u32[]{:S(2)}) collective-permute-start(bf16[160,1024]{1,0:T(8,128)(2,1)S(1)} %get-tuple-element.31), channel_id=1, source_target_pairs={{8,0},{16,8},{24,16},{32,24},{40,32},{48,40},{56,48},{64,56},{72,6... | collective-permute-start | bytes 983048 | tf_op jit(solution)/shard_map/ppermute | solution.py:428
  5.8 0.0 copy-start.5
  5.8 0.0 copy-start.7
  5.9 2.1 %collective-permute-start = (bf16[144,1024]{1,0:T(8,128)(2,1)S(1)}, bf16[144,1024]{1,0:T(8,128)(2,1)S(1)}, u32[]{:S(2)}, u32[]{:S(2)}) collective-permute-start(bf16[144,1024]{1,0:T(8,128)(2,1)S(1)} %get-tuple-element.30), channel_id=1, source_target_pairs={{0,8},{8,16},{16,24},{24,32},{32,40},{40,48},{48,56},{56,64},{64,7... | collective-permute-start | bytes 884744 | tf_op jit(solution)/shard_map/ppermute | solution.py:429
  7.9 0.0 copy-done.6
  7.9 0.0 copy-done.8
  7.9 0.0 copy-done.3
  7.9 0.0 copy-done.4
  8.0 0.0 copy-done.1
  8.0 0.0 copy-done
  8.0 0.0 copy-done.2
  8.0 0.0 copy-start.9
  8.0 1.0 %copy-done.9 = f32[128,1024]{1,0:T(8,128)S(1)} copy-done((f32[128,1024]{1,0:T(8,128)S(1)}, f32[128,1024]{1,0:T(8,128)}, u32[]{:S(2)}) %copy-start.9) | copy-done | bytes 524312
  9.0 1.0 %copy-done.10 = bf16[384,352]{1,0:T(8,128)(2,1)S(1)} copy-done((bf16[384,352]{1,0:T(8,128)(2,1)S(1)}, bf16[384,352]{1,0:T(8,128)(2,1)}, u32[]{:S(2)}) %copy-start.10) | copy-done | bytes 270360
  10.0 2.8 %local.1 = (f32[384,1024]{1,0:T(8,128)S(1)}, f32[384,1024]{1,0:T(8,128)S(1)}, f32[224,1024]{1,0:T(8,128)S(1)}, f32[224,1024]{1,0:T(8,128)S(1)}, f32[256,128]{1,0:T(8,128)S(1)}) custom-call(bf16[224,1024]{1,0:T(8,128)(2,1)S(1)} %copy-done.3, bf16[224,1024]{1,0:T(8,128)(2,1)S(1)} %copy-done.4, bf16[224,1024]{1,0:T(8,128)(2,1)S(1)} %copy-done, ...), custom_call_target="tpu_custom_call" | custom-call | tf_op jit(solution)/shard_map/local/pallas_call | solution.py:431
  12.9 2.2 %collective-permute-done.fwd = bf16[144,1024]{1,0:T(8,128)(2,1)S(1)} collective-permute-done((bf16[144,1024]{1,0:T(8,128)(2,1)S(1)}, bf16[144,1024]{1,0:T(8,128)(2,1)S(1)}, u32[]{:S(2)}, u32[]{:S(2)}) %collective-permute-start) | collective-permute-done | bytes 294944 | tf_op jit(solution)/shard_map/ppermute | solution.py:429
  15.0 0.0 collective-permute-done.1.bwd
  15.0 0.0 copy-done.5
  15.1 2.4 %norm.1 = (f32[232,1024]{1,0:T(8,128)S(1)}, f32[16,1024]{1,0:T(8,128)S(1)}, f32[16,1024]{1,0:T(8,128)S(1)}, f32[8,8,128]{2,1,0:T(8,128)S(1)}) custom-call(bf16[144,1024]{1,0:T(8,128)(2,1)S(1)} %collective-permute-done.fwd, bf16[160,1024]{1,0:T(8,128)(2,1)S(1)} %collective-permute-done.1.bwd, bf16[224,1024]{1,0:T(8,128)(2,1)S(1)} %copy-done, ...), custom_call_target="tpu_custom_call" | custom-call | tf_op jit(solution)/shard_map/norm/pallas_call | solution.py:440
  17.4 14.2 %all_to_all.15.stats = f32[8,8,128]{2,1,0:T(8,128)S(1)} all-to-all(f32[8,8,128]{2,1,0:T(8,128)S(1)} %get-tuple-element.36), channel_id=1, replica_groups=mesh['ctx'=64,'tp'=8] {'tp'}, dimensions={0} | all-to-all | bytes 65536 | tf_op jit(solution)/shard_map/all_to_all | solution.py:449
  31.6 7.0 %finish.1 = (bf16[224,1024]{1,0:T(8,128)(2,1)}, bf16[224,1024]{1,0:T(8,128)(2,1)}, bf16[224,1024]{1,0:T(8,128)(2,1)}, bf16[224,1024]{1,0:T(8,128)(2,1)}, bf16[22...) custom-call(f32[8,8,128]{2,1,0:T(8,128)S(1)} %all_to_all.15.stats, bf16[144,1024]{1,0:T(8,128)(2,1)S(1)} %collective-permute-done.fwd, ...), custom_call_target="tpu_custom_call" | custom-call | tf_op jit(solution)/shard_map/finish/pallas_call | solution.py:451
  38.6 9.2 %all_to_all.16.got = bf16[4,288,128]{2,1,0:T(8,128)(2,1)S(1)} all-to-all(bf16[4,288,128]{2,1,0:T(8,128)(2,1)S(1)} %get-tuple-element.46), channel_id=1, replica_groups={{0,8,16,24},{32,40,48,56},{64,72,80,88},{96,104,112,120},{128,136,144,1..., dimensions={0} | all-to-all | bytes 589824 | tf_op jit(solution)/shard_map/all_to_all | solution.py:466
  47.8 28.8 %all_to_all.17.refs_0_ = bf16[16,24,128]{2,1,0:T(8,128)(2,1)S(1)} all-to-all(bf16[16,24,128]{2,1,0:T(8,128)(2,1)S(1)} %merge.1), channel_id=1, replica_groups={{0,32,64,96,128,160,192,224,256,288,320,352,384,416,448,480},{8,40,72,1..., dimensions={0} | all-to-all | bytes 196608 | tf_op jit(solution)/shard_map/all_to_all | solution.py:470
  76.6 0.8 final.1
  (9 shorter events, 0.1 us)
Async XLA Ops:
  0.6 7.3 %copy-start.6 = (bf16[384,352]{1,0:T(8,128)(2,1)S(1)}, bf16[384,352]{1,0:T(8,128)(2,1)}, u32[]{:S(2)}) copy-start(bf16[384,352]{1,0:T(8,128)(2,1)} %constant.8.clone.fxh) | copy-start | bytes 811012
  0.7 7.3 %copy-start.8 = (f32[7,1024]{1,0:T(8,128)S(1)}, f32[7,1024]{1,0:T(8,128)}, u32[]{:S(2)}) copy-start(f32[7,1024]{1,0:T(8,128)} %fse.7) | copy-start | bytes 86020
  0.7 7.3 %copy-start.3 = (bf16[224,1024]{1,0:T(8,128)(2,1)S(1)}, bf16[224,1024]{1,0:T(8,128)(2,1)}, u32[]{:S(2)}) copy-start(bf16[224,1024]{1,0:T(8,128)(2,1)} %up.7) | copy-start | bytes 1376260
  0.7 7.3 %copy-start.4 = (bf16[224,1024]{1,0:T(8,128)(2,1)S(1)}, bf16[224,1024]{1,0:T(8,128)(2,1)}, u32[]{:S(2)}) copy-start(bf16[224,1024]{1,0:T(8,128)(2,1)} %qmr.7) | copy-start | bytes 1376260
  0.7 7.3 %copy-start.1 = (bf16[224,1024]{1,0:T(8,128)(2,1)S(1)}, bf16[224,1024]{1,0:T(8,128)(2,1)}, u32[]{:S(2)}) copy-start(bf16[224,1024]{1,0:T(8,128)(2,1)} %vse.7) | copy-start | bytes 1376260
  0.7 7.3 %copy-start = (bf16[224,1024]{1,0:T(8,128)(2,1)S(1)}, bf16[224,1024]{1,0:T(8,128)(2,1)}, u32[]{:S(2)}) copy-start(bf16[224,1024]{1,0:T(8,128)(2,1)} %kse.7) | copy-start | bytes 1376260
  0.7 7.3 %copy-start.2 = (bf16[224,1024]{1,0:T(8,128)(2,1)S(1)}, bf16[224,1024]{1,0:T(8,128)(2,1)}, u32[]{:S(2)}) copy-start(bf16[224,1024]{1,0:T(8,128)(2,1)} %qse.7) | copy-start | bytes 1376260
  3.4 11.7 %collective-permute-start.1 = (bf16[160,1024]{1,0:T(8,128)(2,1)S(1)}, bf16[160,1024]{1,0:T(8,128)(2,1)S(1)}, u32[]{:S(2)}, u32[]{:S(2)}) collective-permute-start(bf16[160,1024]{1,0:T(8,128)(2,1)S(1)} %get-tuple-element.31), channel_id=1, source_target_pairs={{8,0},{16,8},{24,16},{32,24},{40,32},{48,40},{56,48},{64,56},{72,6... | collective-permute-start | bytes 983048 | tf_op jit(solution)/shard_map/ppermute | solution.py:428
  5.8 9.2 %copy-start.5 = (bf16[224,1024]{1,0:T(8,128)(2,1)S(1)}, bf16[224,1024]{1,0:T(8,128)(2,1)}, u32[]{:S(2)}) copy-start(bf16[224,1024]{1,0:T(8,128)(2,1)} %kmr.5) | copy-start | bytes 1376260
  5.8 9.2 %copy-start.7 = (bf16[232,384]{1,0:T(8,128)(2,1)S(1)}, bf16[232,384]{1,0:T(8,128)(2,1)}, u32[]{:S(2)}) copy-start(bf16[232,384]{1,0:T(8,128)(2,1)} %constant.11.clone.th) | copy-start | bytes 534532
  5.9 9.2 %collective-permute-start = (bf16[144,1024]{1,0:T(8,128)(2,1)S(1)}, bf16[144,1024]{1,0:T(8,128)(2,1)S(1)}, u32[]{:S(2)}, u32[]{:S(2)}) collective-permute-start(bf16[144,1024]{1,0:T(8,128)(2,1)S(1)} %get-tuple-element.30), channel_id=1, source_target_pairs={{0,8},{8,16},{16,24},{24,32},{32,40},{40,48},{48,56},{56,64},{64,7... | collective-permute-start | bytes 884744 | tf_op jit(solution)/shard_map/ppermute | solution.py:429
  8.0 1.0 %copy-start.9 = (f32[128,1024]{1,0:T(8,128)S(1)}, f32[128,1024]{1,0:T(8,128)}, u32[]{:S(2)}) copy-start(f32[128,1024]{1,0:T(8,128)} %fmr.1) | copy-start | bytes 1572868
  9.0 1.0 %copy-start.10 = (bf16[384,352]{1,0:T(8,128)(2,1)S(1)}, bf16[384,352]{1,0:T(8,128)(2,1)}, u32[]{:S(2)}) copy-start(bf16[384,352]{1,0:T(8,128)(2,1)} %constant.9.clone.fxl) | copy-start | bytes 811012
  10.0 5.0 %copy-start.11 = (bf16[384,136]{1,0:T(8,128)(2,1)S(1)}, bf16[384,136]{1,0:T(8,128)(2,1)}, u32[]{:S(2)}) copy-start(bf16[384,136]{1,0:T(8,128)(2,1)} %constant.10.clone.fhh) | copy-start | bytes 313348
  10.0 5.1 %copy-start.12 = (f32[1024]{0:T(1024)S(1)}, f32[1024]{0:T(1024)}, u32[]{:S(2)}) copy-start(f32[1024]{0:T(1024)} %param.23) | copy-start | bytes 12292
  10.0 5.1 %copy-start.13 = (f32[1024]{0:T(1024)S(1)}, f32[1024]{0:T(1024)}, u32[]{:S(2)}) copy-start(f32[1024]{0:T(1024)} %param.22) | copy-start | bytes 12292

commit v3 on v2

v3 whole, which is shorter than its diff:
```python
import math

import jax
import jax.numpy as jnp
import numpy as np
from jax import lax
from jax.experimental import pallas as pl
from jax.experimental.pallas import tpu as pltpu
from jax.sharding import PartitionSpec as P

D = 8192
EPSILON = 0.1
BF = jnp.bfloat16
F32 = jnp.float32

LEN = 384
HALF = LEN // 2
ROWS = 224
EXT = ROWS + 8
HALO = 128
HEAD = 136
CB = 256
BWD = HEAD + 24
CHUNK = 32


def basis(first, last):
    theta = np.pi * (2 * np.arange(HALF)[:, None] + 1) / LEN * np.arange(first, last)[None, :]
    return np.concatenate([np.cos(theta), -np.sin(theta)], 0)


def halves(matrix):
    high = matrix.astype(BF)
    low = (matrix - high.astype(np.float64)).astype(BF)
    return high, low


def dot(a, b):
    return jnp.dot(a, b, preferred_element_type=F32)


def split(x):
    high = x.astype(BF)
    return high, (x - high.astype(F32)).astype(BF)


def forward(fh, fl, data):
    return dot(fh, data) + dot(fl, data)


def wide(column):
    return jnp.concatenate([column] * (CB // 128), axis=1)


def folded(x):
    total = x[:, :128]
    for at in range(128, x.shape[1], 128):
        total = total + x[:, at : at + 128]
    return total


def sums_in_lanes(acc):
    ones = jnp.ones((8, 128), F32)
    return lax.dot_general(
        ones, acc, (((1,), (1,)), ((), ())), precision=lax.Precision.HIGHEST, preferred_element_type=F32
    )


def short_conv(ref, taps, row, count):
    total = None
    for step in range(7):
        term = taps[step : step + 1, :] * ref[pl.ds(row - step, count), :]
        total = term if total is None else total + term
    return total


def rounded(x):
    return x.astype(BF).astype(F32)


def block(b):
    return pl.ds(pl.multiple_of(b * CB, CB), CB)


def eights(x):
    total = x[:8]
    for r in range(8, x.shape[0], 8):
        total = total + x[r : r + 8]
    return total


def send_kernel(
    kse, vse, qse, kmr, up, qmr, fwd, bwd, up_h, qmr_h, kse_h, vse_h, qse_h, kmr_h, kse_t, vse_t, sems
):
    tail = pl.ds(ROWS - 8, 8)
    head = pl.ds(0, 8)
    pieces = [
        (up.at[pl.ds(0, HEAD)], up_h), (qmr.at[pl.ds(0, HEAD)], qmr_h), (qse.at[head], qse_h), (kmr.at[head], kmr_h),
        (kse.at[head], kse_h), (vse.at[head], vse_h), (kse.at[tail], kse_t), (vse.at[tail], vse_t),
    ]
    copies = [pltpu.make_async_copy(src, dst, sems.at[k]) for k, (src, dst) in enumerate(pieces)]
    for copy in copies:
        copy.start()
    for copy in copies:
        copy.wait()

    def step(b, carry):
        c = block(b)
        bwd[:HEAD, c] = (up_h[:, c].astype(F32) * qmr_h[:, c].astype(F32)).astype(BF)
        bwd[HEAD : HEAD + 8, c] = qse_h[:, c]
        bwd[HEAD + 8 : HEAD + 16, c] = kmr_h[:, c]
        bwd[HEAD + 16 :, c] = (kse_h[:, c].astype(F32) * vse_h[:, c].astype(F32)).astype(BF)
        fwd[:, c] = (kse_t[:, c].astype(F32) * vse_t[:, c].astype(F32)).astype(BF)
        return carry

    lax.fori_loop(0, fwd.shape[1] // CB, step, 0)


def local_kernel(
    up, qmr, kse, vse, qse, fse, fmr_in, fxh_in, fxl_in, gloc, hspec, conv_o, mixed_o, acc_o,
    prod, fmr, fxh, fxl, sems
):
    pieces = ((fmr_in, fmr), (fxh_in, fxh), (fxl_in, fxl))
    copies = [pltpu.make_async_copy(src, dst, sems.at[k]) for k, (src, dst) in enumerate(pieces)]
    for copy in copies:
        copy.start()
    acc_o[...] = jnp.zeros_like(acc_o)
    prod[:8] = jnp.zeros((8, CB), F32)
    steps = up.shape[1] // CB

    def short(b, carry):
        c = block(b)
        prod[8:] = rounded(kse[:, c].astype(F32) * vse[:, c].astype(F32))
        taps = fse[:, c]
        for at in range(0, ROWS, CHUNK):
            conv = short_conv(prod, taps, 8 + at, CHUNK)
            mixed = qse[at : at + CHUNK, c].astype(F32) * conv
            conv_o[at : at + CHUNK, c] = conv
            mixed_o[at : at + CHUNK, c] = mixed
            square = folded(mixed * mixed)
            if at == 0:
                acc_o[8:CHUNK] += square[8:]
            else:
                acc_o[at : at + CHUNK] += square
        return carry

    lax.fori_loop(0, steps, short, 0)
    for copy in copies:
        copy.wait()

    def spectra(b, carry):
        c = block(b)
        g = (up[:, c].astype(F32) * qmr[:, c].astype(F32)).astype(BF)
        gloc[:, c] = forward(fxh[...], fxl[...], g)
        high, low = split(fmr[:, c])
        fh = fxh[:, :128]
        hspec[:, c] = dot(fh, high) + dot(fxl[:, :128], high) + dot(fh, low)
        return carry

    lax.fori_loop(0, steps, spectra, 0)


def norm_kernel(
    fwd, bwd, kse, vse, qse, kmr, up, qmr, fse, gain, skip, gloc, hspec, mixed, acc_in, fhh, th,
    gp_o, gext_o, conv_e, mixed_e, stats, prod, acc_sq, acc_w
):
    acc_sq[...] = acc_in[...]
    acc_w[...] = jnp.zeros_like(acc_w)

    def step(b, carry):
        c = block(b)
        spec = gloc[:, c] + dot(fhh[...], bwd[:HEAD, c])
        gext_o[:, c] = spec
        h = hspec[:, c]
        gr, gi, hr, hi = spec[:HALF], spec[HALF:], h[:HALF], h[HALF:]
        back = jnp.concatenate([(gr * hr + gi * hi).astype(BF), (gi * hr - gr * hi).astype(BF)], 0)
        gp_o[:, c] = dot(th[...], back)
        taps, gains, skips = fse[:, c], gain[:, c], skip[:, c]
        prod[:8] = fwd[:, c].astype(F32)
        prod[8:16] = rounded(kse[:8, c].astype(F32) * vse[:8, c].astype(F32))
        prod[16:24] = rounded(kse[ROWS - 8 :, c].astype(F32) * vse[ROWS - 8 :, c].astype(F32))
        prod[24:] = bwd[HEAD + 16 :, c].astype(F32)
        edges = []
        for k, query in ((0, qse[:8, c]), (1, bwd[HEAD : HEAD + 8, c])):
            conv = short_conv(prod, taps, 8 + 16 * k, 8)
            edge = query.astype(F32) * conv
            conv_e[8 * k : 8 * k + 8, c] = conv
            mixed_e[8 * k : 8 * k + 8, c] = edge
            edges.append(edge)
            at = ROWS * k
            acc_sq[at : at + 8] += folded(edge * edge)

        def rows(at, count, mix, key, g):
            gp = gp_o[at : at + count, c] + skips * g
            gp_o[at : at + count, c] = gp
            acc_w[at : at + count] += folded(gp * key.astype(F32) * gains * mix)

        for at in range(0, ROWS, CHUNK):
            s = slice(at, at + CHUNK)
            mix = mixed[s, c]
            if at == 0:
                mix = jnp.concatenate([edges[0], mix[8:]], 0)
            rows(at, CHUNK, mix, kmr[s, c], rounded(up[s, c].astype(F32) * qmr[s, c].astype(F32)))
        rows(ROWS, 8, edges[1], bwd[HEAD + 8 : HEAD + 16, c], bwd[:8, c].astype(F32))
        return carry

    lax.fori_loop(0, gloc.shape[1] // CB, step, 0)
    sq = sums_in_lanes(acc_sq[...])
    w = sums_in_lanes(acc_w[...])
    mine = jnp.concatenate([sq[:1, :128], sq[:1, 128:], w[:1, :128], w[:1, 128:], jnp.zeros((4, 128), F32)], 0)
    for dev in range(8):
        stats[dev] = mine


def column(total, row):
    pick = (lax.broadcasted_iota(jnp.int32, (8, 128), 0) == row).astype(F32)
    return lax.dot_general(
        total, pick, (((0,), (0,)), ((), ())), precision=lax.Precision.HIGHEST, preferred_element_type=F32
    )


def merged_rows(body, edge, at, count, c=slice(None)):
    rows = body[at : at + count, c]
    return jnp.concatenate([edge[:8, c], rows[8:]], 0) if at == 0 else rows


def scales(stats, scale_s, coef_s):
    total = stats[0]
    for dev in range(1, 8):
        total = total + stats[dev]
    s0 = lax.rsqrt(column(total, 0) / D + EPSILON)
    s1 = lax.rsqrt(column(total, 1) / D + EPSILON)
    scale_s[:128] = s0
    scale_s[128:] = s1
    coef_s[:128] = s0 * s0 * s0 * (column(total, 2) / D)
    coef_s[128:] = s1 * s1 * s1 * (column(total, 3) / D)


def filter_kernel(
    stats, fwd, mixed, mixed_e, gp, kmr, qse, up, qmr, kse, vse, gain, gext, fxh, th,
    payload, halo, prod, small, scale_s, coef_s, pms
):
    steps = gext.shape[1] // CB
    scales(stats, scale_s, coef_s)

    def step(b, carry):
        c = block(b)
        prod[:8] = fwd[:, c].astype(F32)
        prod[8:] = rounded(kse[:, c].astype(F32) * vse[:, c].astype(F32))
        gains = gain[:, c]
        sums = [jnp.zeros((8, CB), F32) for _ in range(9)]
        for at in range(0, ROWS, CHUNK):
            s = slice(at, at + CHUNK)
            mix = merged_rows(mixed, mixed_e, at, CHUNK, c)
            scale = wide(scale_s[s])
            key = kmr[s, c].astype(F32)
            gn = gp[s, c] * key
            ms = mix * scale
            pm = (key * (ms * gains)).astype(BF)
            pms[s] = pm
            if at >= ROWS - HALO:
                halo[at - (ROWS - HALO) : at - (ROWS - HALO) + CHUNK, c] = pm
            gm = gains * scale * gn - mix * wide(coef_s[s])
            gc = rounded(gm * qse[s, c].astype(F32))
            g = rounded(up[s, c].astype(F32) * qmr[s, c].astype(F32))
            for tap in range(7):
                sums[tap] = sums[tap] + eights(gc * prod[pl.ds(8 + at - tap, CHUNK), :])
            sums[7] = sums[7] + eights(g * pm.astype(F32))
            sums[8] = sums[8] + eights(gn * ms)
        parts = [jnp.sum(x, axis=0, keepdims=True) for x in sums]
        small[b] = jnp.concatenate(parts + [jnp.zeros((7, CB), F32)], 0)

        x = dot(fxh[...], pms[...])
        ge = gext[:, c]
        xr, xi, gr, gi = x[:HALF], x[HALF:], ge[:HALF], ge[HALF:]
        back = jnp.concatenate([(gr * xr + gi * xi).astype(BF), (gi * xr - gr * xi).astype(BF)], 0)
        corr = dot(th[:128], back).T.astype(BF)
        for zz in range(4):
            for yc in range(4):
                at = pl.multiple_of((4 * b + zz) * 16, 16)
                payload[yc, pl.ds(at, 16), :] = corr[zz * 64 + yc * 16 : zz * 64 + yc * 16 + 16]
        return carry

    lax.fori_loop(0, steps, step, 0)

    lane = lax.broadcasted_iota(jnp.int32, (16, 128), 1)
    row = lax.broadcasted_iota(jnp.int32, (16, 128), 0)
    spread = (lane % 16 == row).astype(BF)
    chan = lax.broadcasted_iota(jnp.int32, (CB, 128), 0)
    keep = chan % 8 == lax.broadcasted_iota(jnp.int32, (CB, 128), 1) // 16
    out_row = lax.broadcasted_iota(jnp.int32, (128, CB), 0)
    out_chan = lax.broadcasted_iota(jnp.int32, (128, CB), 1)
    packed = None
    for b in range(steps):
        tiled = lax.dot_general(
            small[b].astype(BF), spread, (((0,), (0,)), ((), ())), preferred_element_type=F32
        )
        masked = jnp.where(keep, tiled, 0.0).astype(BF)
        ch = out_chan + b * CB
        take = (out_row // 32 == (ch // 16) % 4) & ((out_row // 2) % 16 == ch // 64) & (out_row % 2 == (ch // 8) % 2)
        part = dot(take.astype(BF), masked)
        packed = part if packed is None else packed + part
    packed = packed.astype(BF)
    for yc in range(4):
        payload[yc, 256:] = packed[yc * 32 : yc * 32 + 32]


def rest_kernel(
    stats, halo, hspec, mixed, conv, mixed_e, conv_e, gp, bwd, up, kmr, kse, vse, qse, gain, skip, fse, fxh, fhalo, th,
    gqse, gkse, gvse, gqmr, gkmr, scale_s, coef_s, gcs, pms
):
    @pl.when(pl.program_id(0) == 0)
    def _():
        scales(stats, scale_s, coef_s)

    gains, taps, skips = gain[...], fse[...], skip[...]
    for at in range(0, ROWS, CHUNK):
        s = slice(at, at + CHUNK)
        mix = merged_rows(mixed, mixed_e, at, CHUNK)
        con = merged_rows(conv, conv_e, at, CHUNK)
        scale, key, grad = wide(scale_s[s]), kmr[s].astype(F32), gp[s]
        normed = mix * scale * gains
        pms[s] = (key * normed).astype(BF)
        gkmr[s] = (grad * normed).astype(BF)
        gm = gains * scale * (grad * key) - mix * wide(coef_s[s])
        gqse[s] = (gm * con).astype(BF)
        gcs[s] = rounded(gm * qse[s].astype(F32))
    nxt = slice(ROWS, ROWS + 8)
    gn = gp[nxt] * bwd[HEAD + 8 : HEAD + 16].astype(F32)
    gm = gains * wide(scale_s[nxt]) * gn - mixed_e[8:] * wide(coef_s[nxt])
    gcs[nxt] = rounded(gm * bwd[HEAD : HEAD + 8].astype(F32))
    x, h = dot(fxh[...], pms[...]) + dot(fhalo[...], halo[...]), hspec[...]
    xr, xi, hr, hi = x[:HALF], x[HALF:], h[:HALF], h[HALF:]
    spec = jnp.concatenate([(xr * hr - xi * hi).astype(BF), (xi * hr + xr * hi).astype(BF)], 0)
    ym = dot(th[:ROWS], spec)
    for at in range(0, ROWS, CHUNK):
        s = slice(at, at + CHUNK)
        gqmr[s] = (up[s].astype(F32) * (ym[s] + skips * pms[s].astype(F32))).astype(BF)
        gps = None
        for tap in range(7):
            term = taps[tap : tap + 1, :] * gcs[pl.ds(at + tap, CHUNK), :]
            gps = term if gps is None else gps + term
        gkse[s] = (gps * vse[s].astype(F32)).astype(BF)
        gvse[s] = (gps * kse[s].astype(F32)).astype(BF)


def merge_kernel(got, out):
    total = got[0].astype(F32)
    for k in range(1, 4):
        total = total + got[k].astype(F32)
    for z in range(16):
        out[z, :16] = total[z * 16 : z * 16 + 16].astype(BF)
        pair = total[256 + z * 2 : 256 + z * 2 + 2]
        out[z, 16:] = jnp.concatenate([pair, jnp.zeros((6, 128), F32)], 0).astype(BF)


def final_kernel(got, se_o, mr_o, skip_o, gain_o, *, factor):
    total = got[0].astype(F32)
    for k in range(1, 16):
        total = total + got[k].astype(F32)
    total = total * factor
    mr_o[...] = total[:16]
    chan = lax.broadcasted_iota(jnp.int32, (16, 128), 0)
    lane = lax.broadcasted_iota(jnp.int32, (16, 128), 1)
    mine = jnp.where(chan < 8, total[16:17], total[17:18])
    mine = jnp.where(lane // 16 == chan % 8, mine, 0.0)
    pick = (lane % 16 == chan).astype(F32)
    small = lax.dot_general(
        pick, mine, (((1,), (1,)), ((), ())), precision=lax.Precision.HIGHEST, preferred_element_type=F32
    )
    se_o[...] = small[:7]
    skip_o[...] = small[7:8]
    gain_o[...] = small[8:9]


def local(
    query_se, key_se, value_se, query_mr, key_mr, upstream, filter_se, filter_mr, skip_mr, norm_gain
):
    chans = query_se.shape[1]
    steps = chans // CB
    size = lax.axis_size("ctx")
    skip2, gain2 = skip_mr.reshape(1, chans), norm_gain.reshape(1, chans)
    fxh, fxl = halves(basis(0, ROWS))
    fhead, _ = halves(basis(ROWS, ROWS + HEAD))
    fhalo, _ = halves(basis(-HALO, 0))
    back, _ = halves(basis(0, EXT).T * (2.0 / LEN))

    def shape(rows, dtype):
        return jax.ShapeDtypeStruct((rows, chans), dtype)

    def vmem(rows, width, dtype):
        return pltpu.VMEM((rows, width), dtype)

    def kept(x):
        return pltpu.with_memory_space_constraint(x, pltpu.HBM)

    params = pltpu.CompilerParams(vmem_limit_bytes=16 * 1024 * 1024)
    hbm = pl.BlockSpec(memory_space=pltpu.HBM)
    here = pl.BlockSpec(memory_space=pltpu.VMEM)
    fwd, bwd = pl.pallas_call(
        send_kernel,
        in_specs=[hbm] * 6,
        out_shape=[shape(8, BF), shape(BWD, BF)],
        scratch_shapes=[vmem(HEAD, chans, BF)] * 2 + [vmem(8, chans, BF)] * 6 + [pltpu.SemaphoreType.DMA((8,))],
        compiler_params=params,
        name="send",
    )(*(kept(x) for x in (key_se, value_se, query_se, key_mr, upstream, query_mr)))

    down = [(k, k + 1) for k in range(size - 1)]
    upward = [(k + 1, k) for k in range(size - 1)]
    bwd = lax.ppermute(bwd, "ctx", upward)
    fwd = lax.ppermute(fwd, "ctx", down)

    gloc, hspec, conv, mixed, acc = pl.pallas_call(
        local_kernel,
        in_specs=[here] * 6 + [hbm] * 3,
        out_shape=[shape(LEN, F32), shape(LEN, F32), shape(ROWS, F32), shape(ROWS, F32),
                   jax.ShapeDtypeStruct((256, 128), F32)],
        scratch_shapes=[vmem(ROWS + 8, CB, F32), vmem(filter_mr.shape[0], chans, F32), vmem(LEN, ROWS, BF),
                        vmem(LEN, ROWS, BF), pltpu.SemaphoreType.DMA((3,))],
        compiler_params=params,
        name="local",
    )(upstream, query_mr, key_se, value_se, query_se, filter_se, kept(filter_mr), kept(fxh), kept(fxl))

    gp, gext, conv_e, mixed_e, stats = pl.pallas_call(
        norm_kernel,
        out_shape=[shape(EXT, F32), shape(LEN, F32), shape(16, F32), shape(16, F32),
                   jax.ShapeDtypeStruct((8, 8, 128), F32)],
        scratch_shapes=[vmem(32, CB, F32), vmem(256, 128, F32), vmem(256, 128, F32)],
        compiler_params=params,
        name="norm",
    )(fwd, bwd, key_se, value_se, query_se, key_mr, upstream, query_mr, filter_se, gain2, skip2, gloc, hspec,
      mixed, acc, fhead, back)

    stats = lax.all_to_all(stats, "tp", 0, 0, tiled=True)

    payload, halo = pl.pallas_call(
        filter_kernel,
        out_shape=[jax.ShapeDtypeStruct((4, 288, 128), BF), shape(HALO, BF)],
        scratch_shapes=[vmem(ROWS + 8, CB, F32), pltpu.VMEM((steps, 16, CB), F32), vmem(256, 128, F32),
                        vmem(256, 128, F32), vmem(ROWS, CB, BF)],
        compiler_params=params,
        name="filters",
    )(stats, fwd, mixed, mixed_e, gp, key_mr, query_se, upstream, query_mr, key_se, value_se, gain2, gext, fxh, back)
    halo = lax.ppermute(halo, "ctx", down)

    def cols(rows):
        return pl.BlockSpec((rows, CB), lambda i: (0, i))

    def whole(*dims):
        return pl.BlockSpec(dims, lambda i: (0,) * len(dims))

    late = (stats, halo, hspec, mixed, conv, mixed_e, conv_e, gp, bwd, upstream, key_mr, key_se, value_se, query_se,
            gain2, skip2, filter_se, fxh, fhalo, back)
    outs = pl.pallas_call(
        rest_kernel,
        grid=(steps,),
        in_specs=[whole(8, 8, 128)] + [cols(x.shape[0]) for x in late[1:17]] + [whole(*x.shape) for x in late[17:]],
        out_specs=[cols(ROWS)] * 5,
        out_shape=[shape(ROWS, BF)] * 5,
        scratch_shapes=[vmem(256, 128, F32), vmem(256, 128, F32), vmem(EXT, CB, F32), vmem(ROWS, CB, BF)],
        compiler_params=params,
        name="rest",
    )(*(kept(x) for x in late))

    near = [[4 * a + b for b in range(4)] for a in range(size // 4)]
    far = [[4 * a + b for a in range(size // 4)] for b in range(4)]
    got = lax.all_to_all(payload, "ctx", 0, 0, axis_index_groups=near, tiled=True)
    merged = pl.pallas_call(
        merge_kernel, out_shape=jax.ShapeDtypeStruct((16, 24, 128), BF), compiler_params=params, name="merge"
    )(got)
    got = lax.all_to_all(merged, "ctx", 0, 0, axis_index_groups=far, tiled=True)
    factor = 1.0 / math.sqrt(ROWS * size)
    se, mr, sk, ga = pl.pallas_call(
        lambda *refs: final_kernel(*refs, factor=factor),
        out_shape=[jax.ShapeDtypeStruct((7, 16), F32), jax.ShapeDtypeStruct((16, 128), F32),
                   jax.ShapeDtypeStruct((1, 16), F32), jax.ShapeDtypeStruct((1, 16), F32)],
        compiler_params=params,
        name="final",
    )(got)
    return (*outs, se, mr.T, sk.reshape(16), ga.reshape(16))


def solution(mesh):
    both, part = P("ctx", "tp"), P(None, "tp")
    in_specs = (both,) * 6 + (part, part, P("tp"), P("tp"))
    split_all = ("tp", "ctx")
    out_specs = (both,) * 5 + (P(None, split_all), P(None, split_all), P(split_all), P(split_all))
    return jax.shard_map(local, mesh=mesh, in_specs=in_specs, out_specs=out_specs, check_vma=False)
```

time: 77.7 us -> 77.1 us (level)
  blocking collectives: 52.2 us -> 23.3 us
  starting transfers between devices: 4.52 us -> 22.3 us
  waiting for transfers between devices: 2.18 us -> 8.98 us
  Pallas kernels: 15.6 us -> 20.3 us
  local copies, waits for them, and re-layouts: 2.05 us -> 0.84 us
    all_to_all x1 -> x0, blocking collectives: 28.8 us -> none  [local(): got = lax.all_to_all(merged, 'ctx', 0, 0, axis_index_groups=far, tiled=True)]
    all_to_all x0 -> x1, starting transfers between devices: none -> 15.9 us  [local(): got = lax.all_to_all(merged, 'ctx', 0, 0, axis_index_groups=far, tiled=True)]
    ppermute x0 -> x1, waiting for transfers between devices: none -> 7.91 us  [local(): halo = lax.ppermute(halo, 'ctx', down)]
    pallas_call x4 -> x5, Pallas kernels: 14.8 us -> 18.8 us  [the longest x1 7.33 us: local(): pl.pallas_call(rest_kernel, grid=(steps,), in_specs=[whole(8, 8, 128)] +...]
    ppermute x0 -> x1, starting transfers between devices: none -> 1.91 us  [local(): halo = lax.ppermute(halo, 'ctx', down)]
    unnamed x28 -> x44, local copies, waits for them, and re-layouts: 2.05 us -> 0.84 us
    ppermute x1, waiting for transfers between devices: 2.17 us -> 1.07 us  [local(): fwd = lax.ppermute(fwd, 'ctx', down)]
  transfers between devices with their start and end apart: 2 -> 4, of which waited for: 1 -> 2; matrix products, arithmetic and copies ran while one was open for 0% -> 0% of each run, Pallas kernels for 4% -> 13%
where the time goes in v3:
time: 77.1 us; the launch traced here: 76.7 us
  blocking collectives  23.3 us (30%)
  starting transfers between devices  22.3 us (29%)
  Pallas kernels  20.3 us (26%)
  waiting for transfers between devices  8.98 us (12%)
  between operations  0.99 us (1%)
  local copies, waits for them, and re-layouts  0.84 us (1%)
    all_to_all x1, starting transfers between devices, local(): got = lax.all_to_all(merged, 'ctx', 0, 0, axis_index_groups=far, tiled=True)  15.9 us
    all_to_all x1, blocking collectives, local(): stats = lax.all_to_all(stats, 'tp', 0, 0, tiled=True)  14.2 us
    all_to_all x1, blocking collectives, local(): lax.all_to_all(payload, 'ctx', 0, 0, axis_index_groups=near, tiled=True)  9.15 us
    ppermute x1, waiting for transfers between devices, local(): halo = lax.ppermute(halo, 'ctx', down)  7.91 us
    pallas_call x1, Pallas kernels, local(): pl.pallas_call(rest_kernel, grid=(steps,), in_specs=[whole(8, 8, 128)] +...  7.33 us
    pallas_call x1, Pallas kernels, local(): pl.pallas_call(filter_kernel, out_shape=[jax.ShapeDtypeStruct((4, 288, 12...  4.83 us
    pallas_call x1, Pallas kernels, local(): pl.pallas_call(local_kernel, in_specs=[here] * 6 + [hbm] * 3, out_shape=[...  2.94 us
    ppermute x1, starting transfers between devices, local(): bwd = lax.ppermute(bwd, 'ctx', upward)  2.47 us
  transfers between devices with their start and end apart: 4, of which 2 were waited for; matrix products, arithmetic and copies ran while one was open for 0% of the time, Pallas kernels for 13%

profile of v3, /device:TPU:32, one launch (start us, length us, event | category | flops | bytes accessed | tf_op | source)
XLA Modules:
  0.0 76.7 jit_solution(13265887003589899671)
XLA Ops:
  0.6 0.0 copy-start.3
  0.7 0.0 copy-start.1
  0.7 0.0 copy-start
  0.7 0.0 copy-start.2
  0.7 0.0 copy-start.13
  0.7 1.4 %send.1 = (bf16[8,1024]{1,0:T(8,128)(2,1)S(1)}, bf16[160,1024]{1,0:T(8,128)(2,1)S(1)}) custom-call(bf16[224,1024]{1,0:T(8,128)(2,1)} %kse.9, bf16[224,1024]{1,0:T(8,128)(2,1)} %vse.9, bf16[224,1024]{1,0:T(8,128)(2,1)} %qse.9, bf16[224,1024]{1,0:T(8,128)(2,1)} %kmr.7, bf16[224,1024]{1,0:T(8,128)(2,1)} %up.9, bf16[224,1024]{1,0:T(8,128)(2,1)} %qmr.7), custom_call_target="tpu_custom_call" | custom-call | tf_op jit(solution)/shard_map/send/pallas_call | solution.py:400
  2.1 2.5 %collective-permute-start.1 = (bf16[160,1024]{1,0:T(8,128)(2,1)S(1)}, bf16[160,1024]{1,0:T(8,128)(2,1)S(1)}, u32[]{:S(2)}, u32[]{:S(2)}) collective-permute-start(bf16[160,1024]{1,0:T(8,128)(2,1)S(1)} %get-tuple-element.33), channel_id=1, source_target_pairs={{8,0},{16,8},{24,16},{32,24},{40,32},{48,40},{56,48},{64,56},{72,6... | collective-permute-start | bytes 983048 | tf_op jit(solution)/shard_map/ppermute | solution.py:411
  4.6 0.0 copy-start.6
  4.6 0.0 copy-start.10
  4.6 0.0 copy-start.16
  4.6 0.0 copy-start.18
  4.6 0.0 copy-start.19
  4.6 2.1 %collective-permute-start = (bf16[8,1024]{1,0:T(8,128)(2,1)S(1)}, bf16[8,1024]{1,0:T(8,128)(2,1)S(1)}, u32[]{:S(2)}, u32[]{:S(2)}) collective-permute-start(bf16[8,1024]{1,0:T(8,128)(2,1)S(1)} %get-tuple-element.32), channel_id=1, source_target_pairs={{0,8},{8,16},{16,24},{24,32},{32,40},{40,48},{48,56},{56,64},{64,7... | collective-permute-start | bytes 49160 | tf_op jit(solution)/shard_map/ppermute | solution.py:412
  6.7 2.9 %local.1 = (f32[384,1024]{1,0:T(8,128)S(1)}, f32[384,1024]{1,0:T(8,128)S(1)}, f32[224,1024]{1,0:T(8,128)S(1)}, f32[224,1024]{1,0:T(8,128)S(1)}, f32[256,128]{1,0:T(8,128)S(1)}) custom-call(bf16[224,1024]{1,0:T(8,128)(2,1)S(1)} %copy-done.3, bf16[224,1024]{1,0:T(8,128)(2,1)S(1)} %copy-done.5, bf16[224,1024]{1,0:T(8,128)(2,1)S(1)} %copy-done, ...), custom_call_target="tpu_custom_call" | custom-call | tf_op jit(solution)/shard_map/local/pallas_call | solution.py:414
  9.7 1.1 %collective-permute-done.fwd = bf16[8,1024]{1,0:T(8,128)(2,1)S(1)} collective-permute-done((bf16[8,1024]{1,0:T(8,128)(2,1)S(1)}, bf16[8,1024]{1,0:T(8,128)(2,1)S(1)}, u32[]{:S(2)}, u32[]{:S(2)}) %collective-permute-start) | collective-permute-done | bytes 16416 | tf_op jit(solution)/shard_map/ppermute | solution.py:412
  10.8 0.0 collective-permute-done.1.bwd
  10.8 0.0 copy-start.9
  10.9 2.4 %norm.1 = (f32[232,1024]{1,0:T(8,128)S(1)}, f32[384,1024]{1,0:T(8,128)S(1)}, f32[16,1024]{1,0:T(8,128)S(1)}, f32[16,1024]{1,0:T(8,128)S(1)}, f32[8,8,128]{2,1,0:T(8,128)S(1)}) custom-call(bf16[8,1024]{1,0:T(8,128)(2,1)S(1)} %collective-permute-done.fwd, bf16[160,1024]{1,0:T(8,128)(2,1)S(1)} %collective-permute-done.1.bwd, bf16[224,1024]{1,0:T(8,128)(2,1)S(1)} %copy-done, ...), custom_call_target="tpu_custom_call" | custom-call | tf_op jit(solution)/shard_map/norm/pallas_call | solution.py:425
  13.2 0.0 copy-done.12
  13.3 14.2 %all_to_all.15.stats = f32[8,8,128]{2,1,0:T(8,128)S(1)} all-to-all(f32[8,8,128]{2,1,0:T(8,128)S(1)} %get-tuple-element.38), channel_id=1, replica_groups=mesh['ctx'=64,'tp'=8] {'tp'}, dimensions={0} | all-to-all | bytes 65536 | tf_op jit(solution)/shard_map/all_to_all | solution.py:435
  27.5 0.0 copy-done.9
  27.5 4.8 %filters.1 = (bf16[4,288,128]{2,1,0:T(8,128)(2,1)S(1)}, bf16[128,1024]{1,0:T(8,128)(2,1)S(1)}) custom-call(f32[8,8,128]{2,1,0:T(8,128)S(1)} %all_to_all.15.stats, bf16[8,1024]{1,0:T(8,128)(2,1)S(1)} %collective-permute-done.fwd, f32[224,1024]{1,0:T(8,128)S(1)} %get-tuple-element.36.mixed, f32[16,1024]{1,0:T(8,128)S(1)} %get-tuple-element.39.mixed_e, ...), custom_call_target="tpu_custom_call" | custom-call | tf_op jit(solution)/shard_map/filters/pallas_call | solution.py:437
  32.3 0.0 copy-start.20
  32.4 9.1 %all_to_all.16.got = bf16[4,288,128]{2,1,0:T(8,128)(2,1)S(1)} all-to-all(bf16[4,288,128]{2,1,0:T(8,128)(2,1)S(1)} %get-tuple-element.50), channel_id=1, replica_groups={{0,8,16,24},{32,40,48,56},{64,72,80,88},{96,104,112,120},{128,136,144,1..., dimensions={0} | all-to-all | bytes 589824 | tf_op jit(solution)/shard_map/all_to_all | solution.py:468
  41.5 0.7 merge.1
  42.2 15.9 %all-to-all-start.2 = ((bf16[16,24,128]{2,1,0:T(8,128)(2,1)}), bf16[16,24,128]{2,1,0:T(8,128)(2,1)S(1)}, u32[]{:S(2)}, u32[]{:S(2)}) async-start(bf16[16,24,128]{2,1,0:T(8,128)(2,1)} %merge.1), calls=%async_computation.2 | async-start | bytes 196608 | tf_op jit(solution)/shard_map/all_to_all | solution.py:472
  58.1 1.9 %collective-permute-start.2 = (bf16[128,1024]{1,0:T(8,128)(2,1)}, bf16[128,1024]{1,0:T(8,128)(2,1)S(1)}, u32[]{:S(2)}, u32[]{:S(2)}) collective-permute-start(bf16[128,1024]{1,0:T(8,128)(2,1)} %copy-done.20), channel_id=1, source_target_pairs={{0,8},{8,16},{16,24},{24,32},{32,40},{40,48},{48,56},{56,64},{64,7... | collective-permute-start | bytes 786440 | tf_op jit(solution)/shard_map/ppermute | solution.py:445
  60.0 7.9 %collective-permute-done.2.halo = bf16[128,1024]{1,0:T(8,128)(2,1)S(1)} collective-permute-done((bf16[128,1024]{1,0:T(8,128)(2,1)}, bf16[128,1024]{1,0:T(8,128)(2,1)S(1)}, u32[]{:S(2)}, u32[]{:S(2)}) %collective-permute-start.2) | collective-permute-done | bytes 262176 | tf_op jit(solution)/shard_map/ppermute | solution.py:445
  67.9 0.7 copy-done.21
  68.6 7.3 %rest.1 = (bf16[224,1024]{1,0:T(8,128)(2,1)}, bf16[224,1024]{1,0:T(8,128)(2,1)}, bf16[224,1024]{1,0:T(8,128)(2,1)}, bf16[224,1024]{1,0:T(8,128)(2,1)}, bf16[224,1024]{1,0:T(8,128)(2,1)}) custom-call(f32[8,8,128]{2,1,0:T(8,128)} %copy-done.14, bf16[128,1024]{1,0:T(8,128)(2,1)} %copy-done.21, f32[384,1024]{1,0:T(8,128)} %copy-done.7, f32[224,1024]{1,0:T(8,128)} %copy-done.4, ...), custom_call_target="tpu_custom_call" | custom-call | tf_op jit(solution)/shard_map/rest/pallas_call | solution.py:455
  75.9 0.0 all-to-all-done.2.refs_0_
  76.0 0.8 final.1
  (29 shorter events, 0.1 us)
Async XLA Ops:
  0.6 6.0 %copy-start.3 = (bf16[224,1024]{1,0:T(8,128)(2,1)S(1)}, bf16[224,1024]{1,0:T(8,128)(2,1)}, u32[]{:S(2)}) copy-start(bf16[224,1024]{1,0:T(8,128)(2,1)} %up.9) | copy-start | bytes 1376260
  0.7 6.0 %copy-start.1 = (bf16[224,1024]{1,0:T(8,128)(2,1)S(1)}, bf16[224,1024]{1,0:T(8,128)(2,1)}, u32[]{:S(2)}) copy-start(bf16[224,1024]{1,0:T(8,128)(2,1)} %vse.9) | copy-start | bytes 1376260
  0.7 6.0 %copy-start = (bf16[224,1024]{1,0:T(8,128)(2,1)S(1)}, bf16[224,1024]{1,0:T(8,128)(2,1)}, u32[]{:S(2)}) copy-start(bf16[224,1024]{1,0:T(8,128)(2,1)} %kse.9) | copy-start | bytes 1376260
  0.7 6.0 %copy-start.2 = (bf16[224,1024]{1,0:T(8,128)(2,1)S(1)}, bf16[224,1024]{1,0:T(8,128)(2,1)}, u32[]{:S(2)}) copy-start(bf16[224,1024]{1,0:T(8,128)(2,1)} %qse.9) | copy-start | bytes 1376260
  0.7 6.0 %copy-start.5 = (bf16[224,1024]{1,0:T(8,128)(2,1)S(1)}, bf16[224,1024]{1,0:T(8,128)(2,1)}, u32[]{:S(2)}) copy-start(bf16[224,1024]{1,0:T(8,128)(2,1)} %qmr.7) | copy-start | bytes 1376260
  0.7 6.0 %copy-start.13 = (f32[7,1024]{1,0:T(8,128)S(1)}, f32[7,1024]{1,0:T(8,128)}, u32[]{:S(2)}) copy-start(f32[7,1024]{1,0:T(8,128)} %fse.5) | copy-start | bytes 86020
  2.1 8.7 %collective-permute-start.1 = (bf16[160,1024]{1,0:T(8,128)(2,1)S(1)}, bf16[160,1024]{1,0:T(8,128)(2,1)S(1)}, u32[]{:S(2)}, u32[]{:S(2)}) collective-permute-start(bf16[160,1024]{1,0:T(8,128)(2,1)S(1)} %get-tuple-element.33), channel_id=1, source_target_pairs={{8,0},{16,8},{24,16},{32,24},{40,32},{48,40},{56,48},{64,56},{72,6... | collective-permute-start | bytes 983048 | tf_op jit(solution)/shard_map/ppermute | solution.py:411
  4.6 6.2 %copy-start.6 = (bf16[224,1024]{1,0:T(8,128)(2,1)S(1)}, bf16[224,1024]{1,0:T(8,128)(2,1)}, u32[]{:S(2)}) copy-start(bf16[224,1024]{1,0:T(8,128)(2,1)} %kmr.7) | copy-start | bytes 1376260
  4.6 6.2 %copy-start.10 = (bf16[232,384]{1,0:T(8,128)(2,1)S(1)}, bf16[232,384]{1,0:T(8,128)(2,1)}, u32[]{:S(2)}) copy-start(bf16[232,384]{1,0:T(8,128)(2,1)} %constant.13.clone.th) | copy-start | bytes 534532
  4.6 6.2 %copy-start.16 = (bf16[384,136]{1,0:T(8,128)(2,1)S(1)}, bf16[384,136]{1,0:T(8,128)(2,1)}, u32[]{:S(2)}) copy-start(bf16[384,136]{1,0:T(8,128)(2,1)} %constant.12.clone.fhh) | copy-start | bytes 313348
  4.6 6.2 %copy-start.18 = (f32[1024]{0:T(1024)S(1)}, f32[1024]{0:T(1024)}, u32[]{:S(2)}) copy-start(f32[1024]{0:T(1024)} %param.24) | copy-start | bytes 12292
  4.6 6.2 %copy-start.19 = (f32[1024]{0:T(1024)S(1)}, f32[1024]{0:T(1024)}, u32[]{:S(2)}) copy-start(f32[1024]{0:T(1024)} %param.23) | copy-start | bytes 12292
  4.6 6.2 %collective-permute-start = (bf16[8,1024]{1,0:T(8,128)(2,1)S(1)}, bf16[8,1024]{1,0:T(8,128)(2,1)S(1)}, u32[]{:S(2)}, u32[]{:S(2)}) collective-permute-start(bf16[8,1024]{1,0:T(8,128)(2,1)S(1)} %get-tuple-element.32), channel_id=1, source_target_pairs={{0,8},{8,16},{16,24},{24,32},{32,40},{40,48},{48,56},{56,64},{64,7... | collective-permute-start | bytes 49160 | tf_op jit(solution)/shard_map/ppermute | solution.py:412
  9.7 3.5 %copy-start.7 = (f32[384,1024]{1,0:T(8,128)}, f32[384,1024]{1,0:T(8,128)S(1)}, u32[]{:S(2)}) copy-start(f32[384,1024]{1,0:T(8,128)S(1)} %get-tuple-element.35.hspec) | copy-start | bytes 4718596
  9.7 3.5 %copy-start.12 = (f32[224,1024]{1,0:T(8,128)}, f32[224,1024]{1,0:T(8,128)S(1)}, u32[]{:S(2)}) copy-start(f32[224,1024]{1,0:T(8,128)S(1)} %get-tuple-element.43.conv) | copy-start | bytes 2752516
  9.7 17.7 %copy-start.4 = (f32[224,1024]{1,0:T(8,128)}, f32[224,1024]{1,0:T(8,128)S(1)}, u32[]{:S(2)}) copy-start(f32[224,1024]{1,0:T(8,128)S(1)} %get-tuple-element.36.mixed) | copy-start | bytes 2752516
  10.8 2.4 %copy-start.11 = (bf16[160,1024]{1,0:T(8,128)(2,1)}, bf16[160,1024]{1,0:T(8,128)(2,1)S(1)}, u32[]{:S(2)}) copy-start(bf16[160,1024]{1,0:T(8,128)(2,1)S(1)} %collective-permute-done.1.bwd) | copy-start | bytes 983044
  10.8 16.6 %copy-start.9 = (bf16[384,224]{1,0:T(8,128)(2,1)S(1)}, bf16[384,224]{1,0:T(8,128)(2,1)}, u32[]{:S(2)}) copy-start(bf16[384,224]{1,0:T(8,128)(2,1)} %constant.10.clone.fxh_in.fxh) | copy-start | bytes 516100
  13.2 19.1 %copy-start.8 = (f32[232,1024]{1,0:T(8,128)}, f32[232,1024]{1,0:T(8,128)S(1)}, u32[]{:S(2)}) copy-start(f32[232,1024]{1,0:T(8,128)S(1)} %get-tuple-element.40.gp) | copy-start | bytes 2850820
  13.3 19.1 %copy-start.15 = (f32[16,1024]{1,0:T(8,128)}, f32[16,1024]{1,0:T(8,128)S(1)}, u32[]{:S(2)}) copy-start(f32[16,1024]{1,0:T(8,128)S(1)} %get-tuple-element.39.mixed_e) | copy-start | bytes 196612
  13.3 19.1 %copy-start.17 = (f32[16,1024]{1,0:T(8,128)}, f32[16,1024]{1,0:T(8,128)S(1)}, u32[]{:S(2)}) copy-start(f32[16,1024]{1,0:T(8,128)S(1)} %get-tuple-element.44.conv_e) | copy-start | bytes 196612
  27.5 4.9 %copy-start.14 = (f32[8,8,128]{2,1,0:T(8,128)}, f32[8,8,128]{2,1,0:T(8,128)S(1)}, u32[]{:S(2)}) copy-start(f32[8,8,128]{2,1,0:T(8,128)S(1)} %all_to_all.15.stats) | copy-start | bytes 98308
  32.3 9.2 %copy-start.20 = (bf16[128,1024]{1,0:T(8,128)(2,1)}, bf16[128,1024]{1,0:T(8,128)(2,1)S(1)}, u32[]{:S(2)}) copy-start(bf16[128,1024]{1,0:T(8,128)(2,1)S(1)} %get-tuple-element.42) | copy-start | bytes 786436
  42.2 33.8 %all-to-all-start.2 = ((bf16[16,24,128]{2,1,0:T(8,128)(2,1)}), bf16[16,24,128]{2,1,0:T(8,128)(2,1)S(1)}, u32[]{:S(2)}, u32[]{:S(2)}) async-start(bf16[16,24,128]{2,1,0:T(8,128)(2,1)} %merge.1), calls=%async_computation.2 | async-start | bytes 196608 | tf_op jit(solution)/shard_map/all_to_all | solution.py:472
  58.1 9.8 %collective-permute-start.2 = (bf16[128,1024]{1,0:T(8,128)(2,1)}, bf16[128,1024]{1,0:T(8,128)(2,1)S(1)}, u32[]{:S(2)}, u32[]{:S(2)}) collective-permute-start(bf16[128,1024]{1,0:T(8,128)(2,1)} %copy-done.20), channel_id=1, source_target_pairs={{0,8},{8,16},{16,24},{24,32},{32,40},{40,48},{48,56},{56,64},{64,7... | collective-permute-start | bytes 786440 | tf_op jit(solution)/shard_map/ppermute | solution.py:445
  67.9 0.7 copy-start.21

commit v4 on v3

--- a/solution.py
+++ b/solution.py
@@ -70,6 +70,14 @@
     total = None
     for step in range(7):
         term = taps[step : step + 1, :] * ref[pl.ds(row - step, count), :]
+        total = term if total is None else total + term
+    return total
+
+
+def short_adjoint(ref, taps, row, count):
+    total = None
+    for step in range(7):
+        term = taps[step : step + 1, :] * ref[pl.ds(row + step, count), :]
         total = term if total is None else total + term
     return total
 
@@ -237,11 +245,16 @@
 
 
 def filter_kernel(
-    stats, fwd, mixed, mixed_e, gp, kmr, qse, up, qmr, kse, vse, gain, gext, fxh, th,
-    payload, halo, prod, small, scale_s, coef_s, pms
+    stats, fwd, bwd, mixed, mixed_e, conv, conv_e, gp, kmr, qse, up, qmr, kse, vse, gain, fse, gext, fxh, th,
+    gqse, gkse, gvse, gkmr, pm_o, payload, halo, prod, small, scale_s, coef_s, gcs, o0, o1, o2, o3, pms, sems
 ):
     steps = gext.shape[1] // CB
     scales(stats, scale_s, coef_s)
+    outs = ((pms, pm_o), (o0, gqse), (o3, gkmr), (o1, gkse), (o2, gvse))
+
+    def out_copies(b):
+        c = block(b)
+        return [pltpu.make_async_copy(src.at[:, c], dst.at[:, c], sems.at[k, b]) for k, (src, dst) in enumerate(outs)]
 
     def step(b, carry):
         c = block(b)
@@ -254,23 +267,32 @@
             mix = merged_rows(mixed, mixed_e, at, CHUNK, c)
             scale = wide(scale_s[s])
             key = kmr[s, c].astype(F32)
-            gn = gp[s, c] * key
+            grad = gp[s, c]
+            gn = grad * key
             ms = mix * scale
-            pm = (key * (ms * gains)).astype(BF)
-            pms[s] = pm
+            normed = ms * gains
+            pm = (key * normed).astype(BF)
+            pms[s, c] = pm
+            o3[s, c] = (grad * normed).astype(BF)
             if at >= ROWS - HALO:
                 halo[at - (ROWS - HALO) : at - (ROWS - HALO) + CHUNK, c] = pm
             gm = gains * scale * gn - mix * wide(coef_s[s])
+            o0[s, c] = (gm * merged_rows(conv, conv_e, at, CHUNK, c)).astype(BF)
             gc = rounded(gm * qse[s, c].astype(F32))
+            gcs[s] = gc
             g = rounded(up[s, c].astype(F32) * qmr[s, c].astype(F32))
             for tap in range(7):
                 sums[tap] = sums[tap] + eights(gc * prod[pl.ds(8 + at - tap, CHUNK), :])
             sums[7] = sums[7] + eights(g * pm.astype(F32))
             sums[8] = sums[8] + eights(gn * ms)
+        nxt = slice(ROWS, ROWS + 8)
+        gn = gp[nxt, c] * bwd[HEAD + 8 : HEAD + 16, c].astype(F32)
+        gm = gains * wide(scale_s[nxt]) * gn - mixed_e[8:, c] * wide(coef_s[nxt])
+        gcs[nxt] = rounded(gm * bwd[HEAD : HEAD + 8, c].astype(F32))
         parts = [jnp.sum(x, axis=0, keepdims=True) for x in sums]
         small[b] = jnp.concatenate(parts + [jnp.zeros((7, CB), F32)], 0)
 
-        x = dot(fxh[...], pms[...])
+        x = dot(fxh[...], pms[:, c])
         ge = gext[:, c]
         xr, xi, gr, gi = x[:HALF], x[HALF:], ge[:HALF], ge[HALF:]
         back = jnp.concatenate([(gr * xr + gi * xi).astype(BF), (gi * xr - gr * xi).astype(BF)], 0)
@@ -279,6 +301,14 @@
             for yc in range(4):
                 at = pl.multiple_of((4 * b + zz) * 16, 16)
                 payload[yc, pl.ds(at, 16), :] = corr[zz * 64 + yc * 16 : zz * 64 + yc * 16 + 16]
+        taps = fse[:, c]
+        for at in range(0, ROWS, CHUNK):
+            s = slice(at, at + CHUNK)
+            gps = short_adjoint(gcs, taps, at, CHUNK)
+            o1[s, c] = (gps * vse[s, c].astype(F32)).astype(BF)
+            o2[s, c] = (gps * kse[s, c].astype(F32)).astype(BF)
+        for copy in out_copies(b):
+            copy.start()
         return carry
 
     lax.fori_loop(0, steps, step, 0)
@@ -303,45 +333,19 @@
     packed = packed.astype(BF)
     for yc in range(4):
         payload[yc, 256:] = packed[yc * 32 : yc * 32 + 32]
-
-
-def rest_kernel(
-    stats, halo, hspec, mixed, conv, mixed_e, conv_e, gp, bwd, up, kmr, kse, vse, qse, gain, skip, fse, fxh, fhalo, th,
-    gqse, gkse, gvse, gqmr, gkmr, scale_s, coef_s, gcs, pms
-):
-    @pl.when(pl.program_id(0) == 0)
-    def _():
-        scales(stats, scale_s, coef_s)
-
-    gains, taps, skips = gain[...], fse[...], skip[...]
+    for b in range(steps):
+        for copy in out_copies(b):
+            copy.wait()
+
+
+def query_kernel(halo, pm, hspec, up, skip, fxh, fhalo, th, gqmr):
+    x, h = dot(fxh[...], pm[...]) + dot(fhalo[...], halo[...]), hspec[...]
+    xr, xi, hr, hi = x[:HALF], x[HALF:], h[:HALF], h[HALF:]
+    spec = jnp.concatenate([(xr * hr - xi * hi).astype(BF), (xi * hr + xr * hi).astype(BF)], 0)
+    ym = dot(th[...], spec)[:ROWS]
     for at in range(0, ROWS, CHUNK):
         s = slice(at, at + CHUNK)
-        mix = merged_rows(mixed, mixed_e, at, CHUNK)
-        con = merged_rows(conv, conv_e, at, CHUNK)
-        scale, key, grad = wide(scale_s[s]), kmr[s].astype(F32), gp[s]
-        normed = mix * scale * gains
-        pms[s] = (key * normed).astype(BF)
-        gkmr[s] = (grad * normed).astype(BF)
-        gm = gains * scale * (grad * key) - mix * wide(coef_s[s])
-        gqse[s] = (gm * con).astype(BF)
-        gcs[s] = rounded(gm * qse[s].astype(F32))
-    nxt = slice(ROWS, ROWS + 8)
-    gn = gp[nxt] * bwd[HEAD + 8 : HEAD + 16].astype(F32)
-    gm = gains * wide(scale_s[nxt]) * gn - mixed_e[8:] * wide(coef_s[nxt])
-    gcs[nxt] = rounded(gm * bwd[HEAD : HEAD + 8].astype(F32))
-    x, h = dot(fxh[...], pms[...]) + dot(fhalo[...], halo[...]), hspec[...]
-    xr, xi, hr, hi = x[:HALF], x[HALF:], h[:HALF], h[HALF:]
-    spec = jnp.concatenate([(xr * hr - xi * hi).astype(BF), (xi * hr + xr * hi).astype(BF)], 0)
-    ym = dot(th[:ROWS], spec)
-    for at in range(0, ROWS, CHUNK):
-        s = slice(at, at + CHUNK)
-        gqmr[s] = (up[s].astype(F32) * (ym[s] + skips * pms[s].astype(F32))).astype(BF)
-        gps = None
-        for tap in range(7):
-            term = taps[tap : tap + 1, :] * gcs[pl.ds(at + tap, CHUNK), :]
-            gps = term if gps is None else gps + term
-        gkse[s] = (gps * vse[s].astype(F32)).astype(BF)
-        gvse[s] = (gps * kse[s].astype(F32)).astype(BF)
+        gqmr[s] = (up[s].astype(F32) * (ym[s] + skip[...] * pm[s].astype(F32))).astype(BF)
 
 
 def merge_kernel(got, out):
@@ -434,14 +438,17 @@
 
     stats = lax.all_to_all(stats, "tp", 0, 0, tiled=True)
 
-    payload, halo = pl.pallas_call(
+    gqse, gkse, gvse, gkmr, pm, payload, halo = pl.pallas_call(
         filter_kernel,
-        out_shape=[jax.ShapeDtypeStruct((4, 288, 128), BF), shape(HALO, BF)],
+        out_specs=[hbm] * 5 + [here] * 2,
+        out_shape=[shape(ROWS, BF)] * 5 + [jax.ShapeDtypeStruct((4, 288, 128), BF), shape(HALO, BF)],
         scratch_shapes=[vmem(ROWS + 8, CB, F32), pltpu.VMEM((steps, 16, CB), F32), vmem(256, 128, F32),
-                        vmem(256, 128, F32), vmem(ROWS, CB, BF)],
+                        vmem(256, 128, F32), vmem(EXT, CB, F32)] + [vmem(ROWS, chans, BF)] * 5
+        + [pltpu.SemaphoreType.DMA((5, steps))],
         compiler_params=params,
         name="filters",
-    )(stats, fwd, mixed, mixed_e, gp, key_mr, query_se, upstream, query_mr, key_se, value_se, gain2, gext, fxh, back)
+    )(stats, fwd, bwd, mixed, mixed_e, conv, conv_e, gp, key_mr, query_se, upstream, query_mr, key_se, value_se, gain2,
+      filter_se, gext, fxh, back)
     halo = lax.ppermute(halo, "ctx", down)
 
     def cols(rows):
@@ -450,18 +457,16 @@
     def whole(*dims):
         return pl.BlockSpec(dims, lambda i: (0,) * len(dims))
 
-    late = (stats, halo, hspec, mixed, conv, mixed_e, conv_e, gp, bwd, upstream, key_mr, key_se, value_se, query_se,
-            gain2, skip2, filter_se, fxh, fhalo, back)
-    outs = pl.pallas_call(
-        rest_kernel,
+    gqmr = pl.pallas_call(
+        query_kernel,
         grid=(steps,),
-        in_specs=[whole(8, 8, 128)] + [cols(x.shape[0]) for x in late[1:17]] + [whole(*x.shape) for x in late[17:]],
-        out_specs=[cols(ROWS)] * 5,
-        out_shape=[shape(ROWS, BF)] * 5,
-        scratch_shapes=[vmem(256, 128, F32), vmem(256, 128, F32), vmem(EXT, CB, F32), vmem(ROWS, CB, BF)],
-        compiler_params=params,
-        name="rest",
-    )(*(kept(x) for x in late))
+        in_specs=[cols(HALO), cols(ROWS), cols(LEN), cols(ROWS), cols(1), whole(LEN, ROWS), whole(LEN, HALO),
+                  whole(EXT, LEN)],
+        out_specs=cols(ROWS),
+        out_shape=shape(ROWS, BF),
+        compiler_params=params,
+        name="query",
+    )(halo, *(kept(x) for x in (pm, hspec, upstream, skip2, fxh, fhalo, back)))
 
     near = [[4 * a + b for b in range(4)] for a in range(size // 4)]
     far = [[4 * a + b for a in range(size // 4)] for b in range(4)]
@@ -478,7 +483,7 @@
         compiler_params=params,
         name="final",
     )(got)
-    return (*outs, se, mr.T, sk.reshape(16), ga.reshape(16))
+    return (gqse, gkse, gvse, gqmr, gkmr, se, mr.T, sk.reshape(16), ga.reshape(16))
 
 
 def solution(mesh):

time: 77.1 us -> 76.1 us (0.987)
  Pallas kernels: 20.3 us -> 19.4 us
    pallas_call x2, Pallas kernels: 12.2 us -> 11.3 us  [the longest x1 6.46 us: local(): pl.pallas_call(filter_kernel, out_specs=[hbm] * 5 + [here] * 2, out_shape...]
  transfers between devices with their start and end apart: 4 -> 4, of which waited for: 2 -> 2; matrix products, arithmetic and copies ran while one was open for 0% -> 0% of each run, Pallas kernels for 13% -> 10%
where the time goes in v4:
time: 76.1 us; the launch traced here: 75.7 us
  blocking collectives  23.3 us (31%)
  starting transfers between devices  22.3 us (29%)
  Pallas kernels  19.4 us (25%)
  waiting for transfers between devices  8.89 us (12%)
  between operations  0.88 us (1%)
  local copies, waits for them, and re-layouts  0.87 us (1%)
    all_to_all x1, starting transfers between devices, local(): got = lax.all_to_all(merged, 'ctx', 0, 0, axis_index_groups=far, tiled=True)  15.9 us
    all_to_all x1, blocking collectives, local(): stats = lax.all_to_all(stats, 'tp', 0, 0, tiled=True)  14.2 us
    all_to_all x1, blocking collectives, local(): lax.all_to_all(payload, 'ctx', 0, 0, axis_index_groups=near, tiled=True)  9.13 us
    ppermute x1, waiting for transfers between devices, local(): halo = lax.ppermute(halo, 'ctx', down)  7.8 us
    pallas_call x1, Pallas kernels, local(): pl.pallas_call(filter_kernel, out_specs=[hbm] * 5 + [here] * 2, out_shape...  6.46 us
    pallas_call x1, Pallas kernels, local(): pl.pallas_call(query_kernel, grid=(steps,), in_specs=[cols(HALO), cols(RO...  4.84 us
    pallas_call x1, Pallas kernels, local(): pl.pallas_call(local_kernel, in_specs=[here] * 6 + [hbm] * 3, out_shape=[...  2.94 us
    ppermute x1, starting transfers between devices, local(): bwd = lax.ppermute(bwd, 'ctx', upward)  2.47 us
  transfers between devices with their start and end apart: 4, of which 2 were waited for; matrix products, arithmetic and copies ran while one was open for 0% of the time, Pallas kernels for 10%

profile of v4, /device:TPU:32, one launch (start us, length us, event | category | flops | bytes accessed | tf_op | source)
XLA Modules:
  0.0 75.7 jit_solution(16260934436781275986)
XLA Ops:
  0.6 0.0 copy-start
  0.7 0.0 copy-start.4
  0.7 0.0 copy-start.2
  0.7 0.0 copy-start.1
  0.7 0.0 copy-start.3
  0.7 0.0 copy-start.10
  0.7 1.4 %send.1 = (bf16[8,1024]{1,0:T(8,128)(2,1)S(1)}, bf16[160,1024]{1,0:T(8,128)(2,1)S(1)}) custom-call(bf16[224,1024]{1,0:T(8,128)(2,1)} %kse.7, bf16[224,1024]{1,0:T(8,128)(2,1)} %vse.7, bf16[224,1024]{1,0:T(8,128)(2,1)} %qse.7, bf16[224,1024]{1,0:T(8,128)(2,1)} %kmr.5, bf16[224,1024]{1,0:T(8,128)(2,1)} %up.9, bf16[224,1024]{1,0:T(8,128)(2,1)} %qmr.7), custom_call_target="tpu_custom_call" | custom-call | tf_op jit(solution)/shard_map/send/pallas_call | solution.py:404
  2.1 2.5 %collective-permute-start.1 = (bf16[160,1024]{1,0:T(8,128)(2,1)S(1)}, bf16[160,1024]{1,0:T(8,128)(2,1)S(1)}, u32[]{:S(2)}, u32[]{:S(2)}) collective-permute-start(bf16[160,1024]{1,0:T(8,128)(2,1)S(1)} %get-tuple-element.33), channel_id=1, source_target_pairs={{8,0},{16,8},{24,16},{32,24},{40,32},{48,40},{56,48},{64,56},{72,6... | collective-permute-start | bytes 983048 | tf_op jit(solution)/shard_map/ppermute | solution.py:415
  4.6 0.0 copy-start.6
  4.6 0.0 copy-start.8
  4.6 0.0 copy-start.11
  4.6 0.0 copy-start.12
  4.6 0.0 copy-start.13
  4.6 2.1 %collective-permute-start = (bf16[8,1024]{1,0:T(8,128)(2,1)S(1)}, bf16[8,1024]{1,0:T(8,128)(2,1)S(1)}, u32[]{:S(2)}, u32[]{:S(2)}) collective-permute-start(bf16[8,1024]{1,0:T(8,128)(2,1)S(1)} %get-tuple-element.32), channel_id=1, source_target_pairs={{0,8},{8,16},{16,24},{24,32},{32,40},{40,48},{48,56},{56,64},{64,7... | collective-permute-start | bytes 49160 | tf_op jit(solution)/shard_map/ppermute | solution.py:416
  6.7 0.0 copy-done
  6.7 0.0 copy-done.4
  6.7 2.9 %local.1 = (f32[384,1024]{1,0:T(8,128)S(1)}, f32[384,1024]{1,0:T(8,128)S(1)}, f32[224,1024]{1,0:T(8,128)S(1)}, f32[224,1024]{1,0:T(8,128)S(1)}, f32[256,128]{1,0:T(8,128)S(1)}) custom-call(bf16[224,1024]{1,0:T(8,128)(2,1)S(1)} %copy-done, bf16[224,1024]{1,0:T(8,128)(2,1)S(1)} %copy-done.4, bf16[224,1024]{1,0:T(8,128)(2,1)S(1)} %copy-done.1, ...), custom_call_target="tpu_custom_call" | custom-call | tf_op jit(solution)/shard_map/local/pallas_call | solution.py:418
  9.7 1.1 %collective-permute-done.fwd = bf16[8,1024]{1,0:T(8,128)(2,1)S(1)} collective-permute-done((bf16[8,1024]{1,0:T(8,128)(2,1)S(1)}, bf16[8,1024]{1,0:T(8,128)(2,1)S(1)}, u32[]{:S(2)}, u32[]{:S(2)}) %collective-permute-start) | collective-permute-done | bytes 16416 | tf_op jit(solution)/shard_map/ppermute | solution.py:416
  10.8 0.0 collective-permute-done.1.bwd
  10.8 0.0 copy-start.7
  10.8 2.4 %norm.1 = (f32[232,1024]{1,0:T(8,128)S(1)}, f32[384,1024]{1,0:T(8,128)S(1)}, f32[16,1024]{1,0:T(8,128)S(1)}, f32[16,1024]{1,0:T(8,128)S(1)}, f32[8,8,128]{2,1,0:T(8,128)S(1)}) custom-call(bf16[8,1024]{1,0:T(8,128)(2,1)S(1)} %collective-permute-done.fwd, bf16[160,1024]{1,0:T(8,128)(2,1)S(1)} %collective-permute-done.1.bwd, bf16[224,1024]{1,0:T(8,128)(2,1)S(1)} %copy-done.1, ...), custom_call_target="tpu_custom_call" | custom-call | tf_op jit(solution)/shard_map/norm/pallas_call | solution.py:429
  13.2 14.2 %all_to_all.15.stats = f32[8,8,128]{2,1,0:T(8,128)S(1)} all-to-all(f32[8,8,128]{2,1,0:T(8,128)S(1)} %get-tuple-element.38), channel_id=1, replica_groups=mesh['ctx'=64,'tp'=8] {'tp'}, dimensions={0} | all-to-all | bytes 65536 | tf_op jit(solution)/shard_map/all_to_all | solution.py:439
  27.4 6.5 %filters.1 = (bf16[224,1024]{1,0:T(8,128)(2,1)}, bf16[224,1024]{1,0:T(8,128)(2,1)}, bf16[224,1024]{1,0:T(8,128)(2,1)}, bf16[224,1024]{1,0:T(8,128)(2,1)}, bf16[2...) custom-call(f32[8,8,128]{2,1,0:T(8,128)S(1)} %all_to_all.15.stats, ...), custom_call_target="tpu_custom_call" | custom-call | tf_op jit(solution)/shard_map/filters/pallas_call | solution.py:441
  33.9 0.8 %copy-done.9 = bf16[224,1024]{1,0:T(8,128)(2,1)} copy-done((bf16[224,1024]{1,0:T(8,128)(2,1)}, bf16[224,1024]{1,0:T(8,128)(2,1)S(1)}, u32[]{:S(2)}) %copy-start.9) | copy-done | bytes 458776
  34.7 9.1 %all_to_all.16.got = bf16[4,288,128]{2,1,0:T(8,128)(2,1)S(1)} all-to-all(bf16[4,288,128]{2,1,0:T(8,128)(2,1)S(1)} %get-tuple-element.50), channel_id=1, replica_groups={{0,8,16,24},{32,40,48,56},{64,72,80,88},{96,104,112,120},{128,136,144,1..., dimensions={0} | all-to-all | bytes 589824 | tf_op jit(solution)/shard_map/all_to_all | solution.py:473
  43.8 0.7 merge.1
  44.5 15.9 %all-to-all-start.2 = ((bf16[16,24,128]{2,1,0:T(8,128)(2,1)}), bf16[16,24,128]{2,1,0:T(8,128)(2,1)S(1)}, u32[]{:S(2)}, u32[]{:S(2)}) async-start(bf16[16,24,128]{2,1,0:T(8,128)(2,1)} %merge.1), calls=%async_computation.2 | async-start | bytes 196608 | tf_op jit(solution)/shard_map/all_to_all | solution.py:477
  60.4 1.9 %collective-permute-start.2 = (bf16[128,1024]{1,0:T(8,128)(2,1)S(1)}, bf16[128,1024]{1,0:T(8,128)(2,1)S(1)}, u32[]{:S(2)}, u32[]{:S(2)}) collective-permute-start(bf16[128,1024]{1,0:T(8,128)(2,1)S(1)} %get-tuple-element.47), channel_id=1, source_target_pairs={{0,8},{8,16},{16,24},{24,32},{32,40},{40,48},{48,56},{56,64},{64,7... | collective-permute-start | bytes 786440 | tf_op jit(solution)/shard_map/ppermute | solution.py:452
  62.3 7.8 %collective-permute-done.2.halo = bf16[128,1024]{1,0:T(8,128)(2,1)S(1)} collective-permute-done((bf16[128,1024]{1,0:T(8,128)(2,1)S(1)}, bf16[128,1024]{1,0:T(8,128)(2,1)S(1)}, u32[]{:S(2)}, u32[]{:S(2)}) %collective-permute-start.2) | collective-permute-done | bytes 262176 | tf_op jit(solution)/shard_map/ppermute | solution.py:452
  70.1 4.8 %query.1 = bf16[224,1024]{1,0:T(8,128)(2,1)} custom-call(bf16[128,1024]{1,0:T(8,128)(2,1)S(1)} %collective-permute-done.2.halo, bf16[224,1024]{1,0:T(8,128)(2,1)} %copy-done.9, f32[384,1024]{1,0:T(8,128)} %copy-done.5, bf16[224,1024]{1,0:T(8,128)(2,1)} %up.9, f32[1,1024]{1,0:T(1,128)} %bitcast.7, bf16[384,224]{1,0:T(8,128)(2,1)} %constant.10.clone.fxh_in.fxh, ...), custom_call_target="tpu_custom_call" | custom-call | tf_op jit(solution)/shard_map/query/pallas_call | solution.py:460
  74.9 0.0 all-to-all-done.2.refs_0_
  74.9 0.8 final.1
  (13 shorter events, 0.0 us)
Async XLA Ops:
  0.6 6.0 %copy-start = (bf16[224,1024]{1,0:T(8,128)(2,1)S(1)}, bf16[224,1024]{1,0:T(8,128)(2,1)}, u32[]{:S(2)}) copy-start(bf16[224,1024]{1,0:T(8,128)(2,1)} %up.9) | copy-start | bytes 1376260
  0.7 6.0 %copy-start.4 = (bf16[224,1024]{1,0:T(8,128)(2,1)S(1)}, bf16[224,1024]{1,0:T(8,128)(2,1)}, u32[]{:S(2)}) copy-start(bf16[224,1024]{1,0:T(8,128)(2,1)} %qmr.7) | copy-start | bytes 1376260
  0.7 6.0 %copy-start.2 = (bf16[224,1024]{1,0:T(8,128)(2,1)S(1)}, bf16[224,1024]{1,0:T(8,128)(2,1)}, u32[]{:S(2)}) copy-start(bf16[224,1024]{1,0:T(8,128)(2,1)} %vse.7) | copy-start | bytes 1376260
  0.7 6.0 %copy-start.1 = (bf16[224,1024]{1,0:T(8,128)(2,1)S(1)}, bf16[224,1024]{1,0:T(8,128)(2,1)}, u32[]{:S(2)}) copy-start(bf16[224,1024]{1,0:T(8,128)(2,1)} %kse.7) | copy-start | bytes 1376260
  0.7 6.0 %copy-start.3 = (bf16[224,1024]{1,0:T(8,128)(2,1)S(1)}, bf16[224,1024]{1,0:T(8,128)(2,1)}, u32[]{:S(2)}) copy-start(bf16[224,1024]{1,0:T(8,128)(2,1)} %qse.7) | copy-start | bytes 1376260
  0.7 6.0 %copy-start.10 = (f32[7,1024]{1,0:T(8,128)S(1)}, f32[7,1024]{1,0:T(8,128)}, u32[]{:S(2)}) copy-start(f32[7,1024]{1,0:T(8,128)} %fse.5) | copy-start | bytes 86020
  2.1 8.7 %collective-permute-start.1 = (bf16[160,1024]{1,0:T(8,128)(2,1)S(1)}, bf16[160,1024]{1,0:T(8,128)(2,1)S(1)}, u32[]{:S(2)}, u32[]{:S(2)}) collective-permute-start(bf16[160,1024]{1,0:T(8,128)(2,1)S(1)} %get-tuple-element.33), channel_id=1, source_target_pairs={{8,0},{16,8},{24,16},{32,24},{40,32},{48,40},{56,48},{64,56},{72,6... | collective-permute-start | bytes 983048 | tf_op jit(solution)/shard_map/ppermute | solution.py:415
  4.6 6.2 %copy-start.6 = (bf16[224,1024]{1,0:T(8,128)(2,1)S(1)}, bf16[224,1024]{1,0:T(8,128)(2,1)}, u32[]{:S(2)}) copy-start(bf16[224,1024]{1,0:T(8,128)(2,1)} %kmr.5) | copy-start | bytes 1376260
  4.6 6.2 %copy-start.8 = (bf16[232,384]{1,0:T(8,128)(2,1)S(1)}, bf16[232,384]{1,0:T(8,128)(2,1)}, u32[]{:S(2)}) copy-start(bf16[232,384]{1,0:T(8,128)(2,1)} %constant.13.clone.th) | copy-start | bytes 534532
  4.6 6.2 %copy-start.11 = (bf16[384,136]{1,0:T(8,128)(2,1)S(1)}, bf16[384,136]{1,0:T(8,128)(2,1)}, u32[]{:S(2)}) copy-start(bf16[384,136]{1,0:T(8,128)(2,1)} %constant.12.clone.fhh) | copy-start | bytes 313348
  4.6 6.2 %copy-start.12 = (f32[1024]{0:T(1024)S(1)}, f32[1024]{0:T(1024)}, u32[]{:S(2)}) copy-start(f32[1024]{0:T(1024)} %param.24) | copy-start | bytes 12292
  4.6 6.2 %copy-start.13 = (f32[1024]{0:T(1024)S(1)}, f32[1024]{0:T(1024)}, u32[]{:S(2)}) copy-start(f32[1024]{0:T(1024)} %param.23) | copy-start | bytes 12292
  4.6 6.2 %collective-permute-start = (bf16[8,1024]{1,0:T(8,128)(2,1)S(1)}, bf16[8,1024]{1,0:T(8,128)(2,1)S(1)}, u32[]{:S(2)}, u32[]{:S(2)}) collective-permute-start(bf16[8,1024]{1,0:T(8,128)(2,1)S(1)} %get-tuple-element.32), channel_id=1, source_target_pairs={{0,8},{8,16},{16,24},{24,32},{32,40},{40,48},{48,56},{56,64},{64,7... | collective-permute-start | bytes 49160 | tf_op jit(solution)/shard_map/ppermute | solution.py:416
  9.7 3.5 %copy-start.5 = (f32[384,1024]{1,0:T(8,128)}, f32[384,1024]{1,0:T(8,128)S(1)}, u32[]{:S(2)}) copy-start(f32[384,1024]{1,0:T(8,128)S(1)} %get-tuple-element.35.hspec) | copy-start | bytes 4718596
  10.8 16.6 %copy-start.7 = (bf16[384,224]{1,0:T(8,128)(2,1)S(1)}, bf16[384,224]{1,0:T(8,128)(2,1)}, u32[]{:S(2)}) copy-start(bf16[384,224]{1,0:T(8,128)(2,1)} %constant.10.clone.fxh_in.fxh) | copy-start | bytes 516100
  33.9 0.8 %copy-start.9 = (bf16[224,1024]{1,0:T(8,128)(2,1)}, bf16[224,1024]{1,0:T(8,128)(2,1)S(1)}, u32[]{:S(2)}) copy-start(bf16[224,1024]{1,0:T(8,128)(2,1)S(1)} %get-tuple-element.48.pm) | copy-start | bytes 1376260
  44.5 30.5 %all-to-all-start.2 = ((bf16[16,24,128]{2,1,0:T(8,128)(2,1)}), bf16[16,24,128]{2,1,0:T(8,128)(2,1)S(1)}, u32[]{:S(2)}, u32[]{:S(2)}) async-start(bf16[16,24,128]{2,1,0:T(8,128)(2,1)} %merge.1), calls=%async_computation.2 | async-start | bytes 196608 | tf_op jit(solution)/shard_map/all_to_all | solution.py:477
  60.4 9.7 %collective-permute-start.2 = (bf16[128,1024]{1,0:T(8,128)(2,1)S(1)}, bf16[128,1024]{1,0:T(8,128)(2,1)S(1)}, u32[]{:S(2)}, u32[]{:S(2)}) collective-permute-start(bf16[128,1024]{1,0:T(8,128)(2,1)S(1)} %get-tuple-element.47), channel_id=1, source_target_pairs={{0,8},{8,16},{16,24},{24,32},{32,40},{40,48},{48,56},{56,64},{64,7... | collective-permute-start | bytes 786440 | tf_op jit(solution)/shard_map/ppermute | solution.py:452

commit v5 on v4

--- a/solution.py
+++ b/solution.py
@@ -7,6 +7,7 @@
 from jax.experimental import pallas as pl
 from jax.experimental.pallas import tpu as pltpu
 from jax.sharding import PartitionSpec as P
+
 
 D = 8192
 EPSILON = 0.1
@@ -29,6 +30,12 @@
     return np.concatenate([np.cos(theta), -np.sin(theta)], 0)
 
 
+def owner_rows(chans):
+    row, chan = np.arange(128)[:, None], np.arange(chans)[None, :]
+    near = row // 32 == (chan // 16) % 4
+    return near & ((row // 2) % 16 == chan // 64) & (row % 2 == (chan // 8) % 2)
+
+
 def halves(matrix):
     high = matrix.astype(BF)
     low = (matrix - high.astype(np.float64)).astype(BF)
@@ -66,10 +73,19 @@
     )
 
 
+def shifted(ref, row, count):
+    return jnp.concatenate([ref[half, pl.ds(row, count), :] for half in range(CB // 128)], 1)
+
+
+def keep(ref, rows, value):
+    for half in range(CB // 128):
+        ref[half, rows] = value[:, half * 128 : half * 128 + 128]
+
+
 def short_conv(ref, taps, row, count):
     total = None
     for step in range(7):
-        term = taps[step : step + 1, :] * ref[pl.ds(row - step, count), :]
+        term = taps[step : step + 1, :] * shifted(ref, row - step, count)
         total = term if total is None else total + term
     return total
 
@@ -77,7 +93,7 @@
 def short_adjoint(ref, taps, row, count):
     total = None
     for step in range(7):
-        term = taps[step : step + 1, :] * ref[pl.ds(row + step, count), :]
+        term = taps[step : step + 1, :] * shifted(ref, row + step, count)
         total = term if total is None else total + term
     return total
 
@@ -125,7 +141,7 @@
 
 
 def local_kernel(
-    up, qmr, kse, vse, qse, fse, fmr_in, fxh_in, fxl_in, gloc, hspec, conv_o, mixed_o, acc_o,
+    up, qmr, kse, vse, qse, fse, fmr_in, fxh_in, fxl_in, gloc, hspec, conv_o, mixed_o, acc_o, p_o, g_o,
     prod, fmr, fxh, fxl, sems
 ):
     pieces = ((fmr_in, fmr), (fxh_in, fxh), (fxl_in, fxl))
@@ -133,12 +149,14 @@
     for copy in copies:
         copy.start()
     acc_o[...] = jnp.zeros_like(acc_o)
-    prod[:8] = jnp.zeros((8, CB), F32)
+    prod[:, :8] = jnp.zeros((CB // 128, 8, 128), F32)
     steps = up.shape[1] // CB
 
     def short(b, carry):
         c = block(b)
-        prod[8:] = rounded(kse[:, c].astype(F32) * vse[:, c].astype(F32))
+        product = rounded(kse[:, c].astype(F32) * vse[:, c].astype(F32))
+        keep(prod, slice(8, None), product)
+        p_o[:, c] = product
         taps = fse[:, c]
         for at in range(0, ROWS, CHUNK):
             conv = short_conv(prod, taps, 8 + at, CHUNK)
@@ -159,6 +177,7 @@
     def spectra(b, carry):
         c = block(b)
         g = (up[:, c].astype(F32) * qmr[:, c].astype(F32)).astype(BF)
+        g_o[:, c] = g.astype(F32)
         gloc[:, c] = forward(fxh[...], fxl[...], g)
         high, low = split(fmr[:, c])
         fh = fxh[:, :128]
@@ -169,7 +188,7 @@
 
 
 def norm_kernel(
-    fwd, bwd, kse, vse, qse, kmr, up, qmr, fse, gain, skip, gloc, hspec, mixed, acc_in, fhh, th,
+    fwd, bwd, p, g_in, qse, kmr, fse, gain, skip, gloc, hspec, mixed, acc_in, fhh, th,
     gp_o, gext_o, conv_e, mixed_e, stats, prod, acc_sq, acc_w
 ):
     acc_sq[...] = acc_in[...]
@@ -184,10 +203,10 @@
         back = jnp.concatenate([(gr * hr + gi * hi).astype(BF), (gi * hr - gr * hi).astype(BF)], 0)
         gp_o[:, c] = dot(th[...], back)
         taps, gains, skips = fse[:, c], gain[:, c], skip[:, c]
-        prod[:8] = fwd[:, c].astype(F32)
-        prod[8:16] = rounded(kse[:8, c].astype(F32) * vse[:8, c].astype(F32))
-        prod[16:24] = rounded(kse[ROWS - 8 :, c].astype(F32) * vse[ROWS - 8 :, c].astype(F32))
-        prod[24:] = bwd[HEAD + 16 :, c].astype(F32)
+        keep(prod, slice(0, 8), fwd[:, c].astype(F32))
+        keep(prod, slice(8, 16), p[:8, c])
+        keep(prod, slice(16, 24), p[ROWS - 8 :, c])
+        keep(prod, slice(24, 32), bwd[HEAD + 16 :, c].astype(F32))
         edges = []
         for k, query in ((0, qse[:8, c]), (1, bwd[HEAD : HEAD + 8, c])):
             conv = short_conv(prod, taps, 8 + 16 * k, 8)
@@ -208,7 +227,7 @@
             mix = mixed[s, c]
             if at == 0:
                 mix = jnp.concatenate([edges[0], mix[8:]], 0)
-            rows(at, CHUNK, mix, kmr[s, c], rounded(up[s, c].astype(F32) * qmr[s, c].astype(F32)))
+            rows(at, CHUNK, mix, kmr[s, c], g_in[s, c])
         rows(ROWS, 8, edges[1], bwd[HEAD + 8 : HEAD + 16, c], bwd[:8, c].astype(F32))
         return carry
 
@@ -245,7 +264,7 @@
 
 
 def filter_kernel(
-    stats, fwd, bwd, mixed, mixed_e, conv, conv_e, gp, kmr, qse, up, qmr, kse, vse, gain, fse, gext, fxh, th,
+    stats, fwd, bwd, p, g_in, mixed, mixed_e, conv, conv_e, gp, kmr, qse, kse, vse, gain, fse, gext, fxh, th, spots,
     gqse, gkse, gvse, gkmr, pm_o, payload, halo, prod, small, scale_s, coef_s, gcs, o0, o1, o2, o3, pms, sems
 ):
     steps = gext.shape[1] // CB
@@ -258,8 +277,8 @@
 
     def step(b, carry):
         c = block(b)
-        prod[:8] = fwd[:, c].astype(F32)
-        prod[8:] = rounded(kse[:, c].astype(F32) * vse[:, c].astype(F32))
+        keep(prod, slice(0, 8), fwd[:, c].astype(F32))
+        keep(prod, slice(8, None), p[:, c])
         gains = gain[:, c]
         sums = [jnp.zeros((8, CB), F32) for _ in range(9)]
         for at in range(0, ROWS, CHUNK):
@@ -279,16 +298,15 @@
             gm = gains * scale * gn - mix * wide(coef_s[s])
             o0[s, c] = (gm * merged_rows(conv, conv_e, at, CHUNK, c)).astype(BF)
             gc = rounded(gm * qse[s, c].astype(F32))
-            gcs[s] = gc
-            g = rounded(up[s, c].astype(F32) * qmr[s, c].astype(F32))
+            keep(gcs, s, gc)
             for tap in range(7):
-                sums[tap] = sums[tap] + eights(gc * prod[pl.ds(8 + at - tap, CHUNK), :])
-            sums[7] = sums[7] + eights(g * pm.astype(F32))
+                sums[tap] = sums[tap] + eights(gc * shifted(prod, 8 + at - tap, CHUNK))
+            sums[7] = sums[7] + eights(g_in[s, c] * pm.astype(F32))
             sums[8] = sums[8] + eights(gn * ms)
         nxt = slice(ROWS, ROWS + 8)
         gn = gp[nxt, c] * bwd[HEAD + 8 : HEAD + 16, c].astype(F32)
         gm = gains * wide(scale_s[nxt]) * gn - mixed_e[8:, c] * wide(coef_s[nxt])
-        gcs[nxt] = rounded(gm * bwd[HEAD : HEAD + 8, c].astype(F32))
+        keep(gcs, nxt, rounded(gm * bwd[HEAD : HEAD + 8, c].astype(F32)))
         parts = [jnp.sum(x, axis=0, keepdims=True) for x in sums]
         small[b] = jnp.concatenate(parts + [jnp.zeros((7, CB), F32)], 0)
 
@@ -317,18 +335,14 @@
     row = lax.broadcasted_iota(jnp.int32, (16, 128), 0)
     spread = (lane % 16 == row).astype(BF)
     chan = lax.broadcasted_iota(jnp.int32, (CB, 128), 0)
-    keep = chan % 8 == lax.broadcasted_iota(jnp.int32, (CB, 128), 1) // 16
-    out_row = lax.broadcasted_iota(jnp.int32, (128, CB), 0)
-    out_chan = lax.broadcasted_iota(jnp.int32, (128, CB), 1)
+    own = chan % 8 == lax.broadcasted_iota(jnp.int32, (CB, 128), 1) // 16
     packed = None
     for b in range(steps):
         tiled = lax.dot_general(
             small[b].astype(BF), spread, (((0,), (0,)), ((), ())), preferred_element_type=F32
         )
-        masked = jnp.where(keep, tiled, 0.0).astype(BF)
-        ch = out_chan + b * CB
-        take = (out_row // 32 == (ch // 16) % 4) & ((out_row // 2) % 16 == ch // 64) & (out_row % 2 == (ch // 8) % 2)
-        part = dot(take.astype(BF), masked)
+        masked = jnp.where(own, tiled, 0.0).astype(BF)
+        part = dot(spots[:, b * CB : b * CB + CB], masked)
         packed = part if packed is None else packed + part
     packed = packed.astype(BF)
     for yc in range(4):
@@ -338,14 +352,50 @@
             copy.wait()
 
 
-def query_kernel(halo, pm, hspec, up, skip, fxh, fhalo, th, gqmr):
-    x, h = dot(fxh[...], pm[...]) + dot(fhalo[...], halo[...]), hspec[...]
-    xr, xi, hr, hi = x[:HALF], x[HALF:], h[:HALF], h[HALF:]
-    spec = jnp.concatenate([(xr * hr - xi * hi).astype(BF), (xi * hr + xr * hi).astype(BF)], 0)
-    ym = dot(th[...], spec)[:ROWS]
-    for at in range(0, ROWS, CHUNK):
-        s = slice(at, at + CHUNK)
-        gqmr[s] = (up[s].astype(F32) * (ym[s] + skip[...] * pm[s].astype(F32))).astype(BF)
+def query_kernel(
+    halo, pm_in, hspec_in, up_in, skip, fxh_in, fhalo_in, th_in, gqmr,
+    pm, hspec, up, fxh, fhalo, th, out, sems, fixed_sems
+):
+    steps = pm.shape[1] // CB
+
+    def copies(b):
+        c = block(b)
+        pairs = ((pm_in, pm), (hspec_in, hspec), (up_in, up))
+        return [pltpu.make_async_copy(src.at[:, c], dst.at[:, c], sems.at[k, b]) for k, (src, dst) in enumerate(pairs)]
+
+    def out_copy(b):
+        c = block(b)
+        return pltpu.make_async_copy(out.at[:, c], gqmr.at[:, c], sems.at[3, b])
+
+    bases = [
+        pltpu.make_async_copy(src, dst, fixed_sems.at[k])
+        for k, (src, dst) in enumerate(((fxh_in, fxh), (fhalo_in, fhalo), (th_in, th)))
+    ]
+    for copy in bases:
+        copy.start()
+    for b in range(steps):
+        for copy in copies(b):
+            copy.start()
+    for copy in bases:
+        copy.wait()
+
+    def step(b, carry):
+        for copy in copies(b):
+            copy.wait()
+        c = block(b)
+        x, h = dot(fxh[...], pm[:, c]) + dot(fhalo[...], halo[:, c]), hspec[:, c]
+        xr, xi, hr, hi = x[:HALF], x[HALF:], h[:HALF], h[HALF:]
+        spec = jnp.concatenate([(xr * hr - xi * hi).astype(BF), (xi * hr + xr * hi).astype(BF)], 0)
+        ym = dot(th[...], spec)
+        for at in range(0, ROWS, CHUNK):
+            s = slice(at, at + CHUNK)
+            out[s, c] = (up[s, c].astype(F32) * (ym[s] + skip[:, c] * pm[s, c].astype(F32))).astype(BF)
+        out_copy(b).start()
+        return carry
+
+    lax.fori_loop(0, steps, step, 0)
+    for b in range(steps):
+        out_copy(b).wait()
 
 
 def merge_kernel(got, out):
@@ -353,15 +403,16 @@
     for k in range(1, 4):
         total = total + got[k].astype(F32)
     for z in range(16):
-        out[z, :16] = total[z * 16 : z * 16 + 16].astype(BF)
-        pair = total[256 + z * 2 : 256 + z * 2 + 2]
-        out[z, 16:] = jnp.concatenate([pair, jnp.zeros((6, 128), F32)], 0).astype(BF)
+        for k in range(9):
+            at = z * 16 + 2 * k if k < 8 else 256 + 2 * z
+            out[z, :, 128 * k : 128 * k + 128] = total[at : at + 2].astype(BF)
 
 
 def final_kernel(got, se_o, mr_o, skip_o, gain_o, *, factor):
-    total = got[0].astype(F32)
+    packed = got[0].astype(F32)
     for k in range(1, 16):
-        total = total + got[k].astype(F32)
+        packed = packed + got[k].astype(F32)
+    total = jnp.concatenate([packed[:, 128 * k : 128 * k + 128] for k in range(9)], 0)
     total = total * factor
     mr_o[...] = total[:16]
     chan = lax.broadcasted_iota(jnp.int32, (16, 128), 0)
@@ -395,6 +446,9 @@
     def vmem(rows, width, dtype):
         return pltpu.VMEM((rows, width), dtype)
 
+    def shifts(rows):
+        return pltpu.VMEM((CB // 128, rows, 128), F32)
+
     def kept(x):
         return pltpu.with_memory_space_constraint(x, pltpu.HBM)
 
@@ -415,12 +469,12 @@
     bwd = lax.ppermute(bwd, "ctx", upward)
     fwd = lax.ppermute(fwd, "ctx", down)
 
-    gloc, hspec, conv, mixed, acc = pl.pallas_call(
+    gloc, hspec, conv, mixed, acc, p, g = pl.pallas_call(
         local_kernel,
         in_specs=[here] * 6 + [hbm] * 3,
         out_shape=[shape(LEN, F32), shape(LEN, F32), shape(ROWS, F32), shape(ROWS, F32),
-                   jax.ShapeDtypeStruct((256, 128), F32)],
-        scratch_shapes=[vmem(ROWS + 8, CB, F32), vmem(filter_mr.shape[0], chans, F32), vmem(LEN, ROWS, BF),
+                   jax.ShapeDtypeStruct((256, 128), F32), shape(ROWS, F32), shape(ROWS, F32)],
+        scratch_shapes=[shifts(ROWS + 8), vmem(filter_mr.shape[0], chans, F32), vmem(LEN, ROWS, BF),
                         vmem(LEN, ROWS, BF), pltpu.SemaphoreType.DMA((3,))],
         compiler_params=params,
         name="local",
@@ -430,10 +484,10 @@
         norm_kernel,
         out_shape=[shape(EXT, F32), shape(LEN, F32), shape(16, F32), shape(16, F32),
                    jax.ShapeDtypeStruct((8, 8, 128), F32)],
-        scratch_shapes=[vmem(32, CB, F32), vmem(256, 128, F32), vmem(256, 128, F32)],
+        scratch_shapes=[shifts(32), vmem(256, 128, F32), vmem(256, 128, F32)],
         compiler_params=params,
         name="norm",
-    )(fwd, bwd, key_se, value_se, query_se, key_mr, upstream, query_mr, filter_se, gain2, skip2, gloc, hspec,
+    )(fwd, bwd, p, g, query_se, key_mr, filter_se, gain2, skip2, gloc, hspec,
       mixed, acc, fhead, back)
 
     stats = lax.all_to_all(stats, "tp", 0, 0, tiled=True)
@@ -441,38 +495,34 @@
     gqse, gkse, gvse, gkmr, pm, payload, halo = pl.pallas_call(
         filter_kernel,
         out_specs=[hbm] * 5 + [here] * 2,
-        out_shape=[shape(ROWS, BF)] * 5 + [jax.ShapeDtypeStruct((4, 288, 128), BF), shape(HALO, BF)],
-        scratch_shapes=[vmem(ROWS + 8, CB, F32), pltpu.VMEM((steps, 16, CB), F32), vmem(256, 128, F32),
-                        vmem(256, 128, F32), vmem(EXT, CB, F32)] + [vmem(ROWS, chans, BF)] * 5
+        out_shape=[shape(ROWS, BF)] * 4
+        + [pltpu.HBM((ROWS, chans), BF), jax.ShapeDtypeStruct((4, 288, 128), BF), shape(HALO, BF)],
+        scratch_shapes=[shifts(ROWS + 8), pltpu.VMEM((steps, 16, CB), F32), vmem(256, 128, F32),
+                        vmem(256, 128, F32), shifts(EXT)] + [vmem(ROWS, chans, BF)] * 5
         + [pltpu.SemaphoreType.DMA((5, steps))],
         compiler_params=params,
         name="filters",
-    )(stats, fwd, bwd, mixed, mixed_e, conv, conv_e, gp, key_mr, query_se, upstream, query_mr, key_se, value_se, gain2,
-      filter_se, gext, fxh, back)
+    )(stats, fwd, bwd, p, g, mixed, mixed_e, conv, conv_e, gp, key_mr, query_se, key_se, value_se, gain2, filter_se, gext,
+      fxh, back, owner_rows(chans).astype(BF))
     halo = lax.ppermute(halo, "ctx", down)
-
-    def cols(rows):
-        return pl.BlockSpec((rows, CB), lambda i: (0, i))
-
-    def whole(*dims):
-        return pl.BlockSpec(dims, lambda i: (0,) * len(dims))
 
     gqmr = pl.pallas_call(
         query_kernel,
-        grid=(steps,),
-        in_specs=[cols(HALO), cols(ROWS), cols(LEN), cols(ROWS), cols(1), whole(LEN, ROWS), whole(LEN, HALO),
-                  whole(EXT, LEN)],
-        out_specs=cols(ROWS),
+        in_specs=[here] + [hbm] * 3 + [here] + [hbm] * 3,
+        out_specs=hbm,
         out_shape=shape(ROWS, BF),
+        scratch_shapes=[vmem(ROWS, chans, BF), vmem(LEN, chans, F32), vmem(ROWS, chans, BF), vmem(LEN, ROWS, BF),
+                        vmem(LEN, HALO, BF), vmem(EXT, LEN, BF), vmem(ROWS, chans, BF),
+                        pltpu.SemaphoreType.DMA((4, steps)), pltpu.SemaphoreType.DMA((3,))],
         compiler_params=params,
         name="query",
-    )(halo, *(kept(x) for x in (pm, hspec, upstream, skip2, fxh, fhalo, back)))
+    )(halo, kept(pm), kept(hspec), kept(upstream), skip2, kept(fxh), kept(fhalo), kept(back))
 
     near = [[4 * a + b for b in range(4)] for a in range(size // 4)]
     far = [[4 * a + b for a in range(size // 4)] for b in range(4)]
     got = lax.all_to_all(payload, "ctx", 0, 0, axis_index_groups=near, tiled=True)
     merged = pl.pallas_call(
-        merge_kernel, out_shape=jax.ShapeDtypeStruct((16, 24, 128), BF), compiler_params=params, name="merge"
+        merge_kernel, out_shape=jax.ShapeDtypeStruct((16, 2, 1152), BF), compiler_params=params, name="merge"
     )(got)
     got = lax.all_to_all(merged, "ctx", 0, 0, axis_index_groups=far, tiled=True)
     factor = 1.0 / math.sqrt(ROWS * size)

time: 76.1 us -> 73.8 us (0.970)
  Pallas kernels: 19.4 us -> 18.1 us
  local copies, waits for them, and re-layouts: 0.87 us -> 0.08 us
    pallas_call x1, Pallas kernels: 6.46 us -> 5.2 us  [local(): pl.pallas_call(filter_kernel, out_specs=[hbm] * 5 + [here] * 2, out_shape...]
    unnamed x28, local copies, waits for them, and re-layouts: 0.87 us -> 0.08 us
  transfers between devices with their start and end apart: 4 -> 4, of which waited for: 2 -> 2; matrix products, arithmetic and copies ran while one was open for 0% -> 0% of each run, Pallas kernels for 10% -> 11%
where the time goes in v5:
time: 73.8 us; the launch traced here: 73.4 us
  blocking collectives  23.3 us (32%)
  starting transfers between devices  22.3 us (30%)
  Pallas kernels  18.1 us (25%)
  waiting for transfers between devices  8.66 us (12%)
  between operations  0.9 us (1%)
    all_to_all x1, starting transfers between devices, local(): got = lax.all_to_all(merged, 'ctx', 0, 0, axis_index_groups=far, tiled=True)  15.9 us
    all_to_all x1, blocking collectives, local(): stats = lax.all_to_all(stats, 'tp', 0, 0, tiled=True)  14.2 us
    all_to_all x1, blocking collectives, local(): lax.all_to_all(payload, 'ctx', 0, 0, axis_index_groups=near, tiled=True)  9.15 us
    ppermute x1, waiting for transfers between devices, local(): halo = lax.ppermute(halo, 'ctx', down)  7.46 us
    pallas_call x1, Pallas kernels, local(): pl.pallas_call(filter_kernel, out_specs=[hbm] * 5 + [here] * 2, out_shape...  5.2 us
    pallas_call x1, Pallas kernels, local(): pl.pallas_call(query_kernel, in_specs=[here] + [hbm] * 3 + [here] + [hbm]...  4.88 us
    pallas_call x1, Pallas kernels, local(): pl.pallas_call(local_kernel, in_specs=[here] * 6 + [hbm] * 3, out_shape=[...  2.84 us
    ppermute x1, starting transfers between devices, local(): bwd = lax.ppermute(bwd, 'ctx', upward)  2.47 us
  transfers between devices with their start and end apart: 4, of which 2 were waited for; matrix products, arithmetic and copies ran while one was open for 0% of the time, Pallas kernels for 11%

profile of v5, /device:TPU:32, one launch (start us, length us, event | category | flops | bytes accessed | tf_op | source)
XLA Modules:
  0.0 73.4 jit_solution(6427964092637180727)
XLA Ops:
  0.7 0.0 copy-start.2
  0.7 0.0 copy-start.4
  0.7 0.0 copy-start.3
  0.7 0.0 copy-start.6
  0.7 0.0 copy-start.9
  0.7 1.4 %send.1 = (bf16[8,1024]{1,0:T(8,128)(2,1)S(1)}, bf16[160,1024]{1,0:T(8,128)(2,1)S(1)}) custom-call(bf16[224,1024]{1,0:T(8,128)(2,1)} %kse.5, bf16[224,1024]{1,0:T(8,128)(2,1)} %vse.5, bf16[224,1024]{1,0:T(8,128)(2,1)} %qse.7, bf16[224,1024]{1,0:T(8,128)(2,1)} %kmr.5, bf16[224,1024]{1,0:T(8,128)(2,1)} %up_in.1, bf16[224,1024]{1,0:T(8,128)(2,1)} %qmr.3), custom_call_target="tpu_custom_call" | custom-call | tf_op jit(solution)/shard_map/send/pallas_call | solution.py:458
  2.1 2.5 %collective-permute-start.1 = (bf16[160,1024]{1,0:T(8,128)(2,1)S(1)}, bf16[160,1024]{1,0:T(8,128)(2,1)S(1)}, u32[]{:S(2)}, u32[]{:S(2)}) collective-permute-start(bf16[160,1024]{1,0:T(8,128)(2,1)S(1)} %get-tuple-element.35), channel_id=1, source_target_pairs={{8,0},{16,8},{24,16},{32,24},{40,32},{48,40},{56,48},{64,56},{72,6... | collective-permute-start | bytes 983048 | tf_op jit(solution)/shard_map/ppermute | solution.py:469
  4.6 0.0 copy-start.5
  4.6 0.0 copy-start.8
  4.6 0.0 copy-start.11
  4.6 0.0 copy-start.12
  4.6 0.0 copy-start.13
  4.6 2.1 %collective-permute-start = (bf16[8,1024]{1,0:T(8,128)(2,1)S(1)}, bf16[8,1024]{1,0:T(8,128)(2,1)S(1)}, u32[]{:S(2)}, u32[]{:S(2)}) collective-permute-start(bf16[8,1024]{1,0:T(8,128)(2,1)S(1)} %get-tuple-element.34), channel_id=1, source_target_pairs={{0,8},{8,16},{16,24},{24,32},{32,40},{40,48},{48,56},{56,64},{64,7... | collective-permute-start | bytes 49160 | tf_op jit(solution)/shard_map/ppermute | solution.py:470
  6.7 2.8 %local.1 = (f32[384,1024]{1,0:T(8,128)S(1)}, f32[384,1024]{1,0:T(8,128)S(1)}, f32[224,1024]{1,0:T(8,128)S(1)}, f32[224,1024]{1,0:T(8,128)S(1)}, f32[256,128]{1,0...) custom-call(bf16[224,1024]{1,0:T(8,128)(2,1)S(1)} %copy-done.2, bf16[224,1024]{1,0:T(8,128)(2,1)S(1)} %copy-done.6, ...), custom_call_target="tpu_custom_call" | custom-call | tf_op jit(solution)/shard_map/local/pallas_call | solution.py:472
  9.6 0.0 copy-start.1
  9.6 1.2 %collective-permute-done.fwd = bf16[8,1024]{1,0:T(8,128)(2,1)S(1)} collective-permute-done((bf16[8,1024]{1,0:T(8,128)(2,1)S(1)}, bf16[8,1024]{1,0:T(8,128)(2,1)S(1)}, u32[]{:S(2)}, u32[]{:S(2)}) %collective-permute-start) | collective-permute-done | bytes 16416 | tf_op jit(solution)/shard_map/ppermute | solution.py:470
  10.8 0.0 collective-permute-done.1.bwd
  10.8 0.0 copy-done.8
  10.8 0.0 copy-start.7
  10.8 0.0 copy-start.10
  10.9 2.3 %norm.1 = (f32[232,1024]{1,0:T(8,128)S(1)}, f32[384,1024]{1,0:T(8,128)S(1)}, f32[16,1024]{1,0:T(8,128)S(1)}, f32[16,1024]{1,0:T(8,128)S(1)}, f32[8,8,128]{2,1,0:T(8,128)S(1)}) custom-call(bf16[8,1024]{1,0:T(8,128)(2,1)S(1)} %collective-permute-done.fwd, bf16[160,1024]{1,0:T(8,128)(2,1)S(1)} %collective-permute-done.1.bwd, ...), custom_call_target="tpu_custom_call" | custom-call | tf_op jit(solution)/shard_map/norm/pallas_call | solution.py:483
  13.2 14.2 %all_to_all.15.stats = f32[8,8,128]{2,1,0:T(8,128)S(1)} all-to-all(f32[8,8,128]{2,1,0:T(8,128)S(1)} %get-tuple-element.42), channel_id=1, replica_groups=mesh['ctx'=64,'tp'=8] {'tp'}, dimensions={0} | all-to-all | bytes 65536 | tf_op jit(solution)/shard_map/all_to_all | solution.py:493
  27.4 0.0 copy-done.7
  27.4 5.2 %filters.1 = (bf16[224,1024]{1,0:T(8,128)(2,1)}, bf16[224,1024]{1,0:T(8,128)(2,1)}, bf16[224,1024]{1,0:T(8,128)(2,1)}, bf16[224,1024]{1,0:T(8,128)(2,1)}, bf16[2...) custom-call(f32[8,8,128]{2,1,0:T(8,128)S(1)} %all_to_all.15.stats, ...), custom_call_target="tpu_custom_call" | custom-call | tf_op jit(solution)/shard_map/filters/pallas_call | solution.py:495
  32.6 9.1 %all_to_all.16.got = bf16[4,288,128]{2,1,0:T(8,128)(2,1)S(1)} all-to-all(bf16[4,288,128]{2,1,0:T(8,128)(2,1)S(1)} %get-tuple-element.54), channel_id=1, replica_groups={{0,8,16,24},{32,40,48,56},{64,72,80,88},{96,104,112,120},{128,136,144,1..., dimensions={0} | all-to-all | bytes 589824 | tf_op jit(solution)/shard_map/all_to_all | solution.py:523
  41.8 0.7 merge.1
  42.5 15.9 %all-to-all-start.2 = ((bf16[16,2,1152]{2,1,0:T(2,128)(2,1)}), bf16[16,2,1152]{2,1,0:T(2,128)(2,1)S(1)}, u32[]{:S(2)}, u32[]{:S(2)}) async-start(bf16[16,2,1152]{2,1,0:T(2,128)(2,1)} %merge.1), calls=%async_computation.2 | async-start | bytes 147456 | tf_op jit(solution)/shard_map/all_to_all | solution.py:527
  58.3 1.9 %collective-permute-start.2 = (bf16[128,1024]{1,0:T(8,128)(2,1)S(1)}, bf16[128,1024]{1,0:T(8,128)(2,1)S(1)}, u32[]{:S(2)}, u32[]{:S(2)}) collective-permute-start(bf16[128,1024]{1,0:T(8,128)(2,1)S(1)} %get-tuple-element.51), channel_id=1, source_target_pairs={{0,8},{8,16},{16,24},{24,32},{32,40},{40,48},{48,56},{56,64},{64,7... | collective-permute-start | bytes 786440 | tf_op jit(solution)/shard_map/ppermute | solution.py:507
  60.3 7.5 %collective-permute-done.2.halo = bf16[128,1024]{1,0:T(8,128)(2,1)S(1)} collective-permute-done((bf16[128,1024]{1,0:T(8,128)(2,1)S(1)}, bf16[128,1024]{1,0:T(8,128)(2,1)S(1)}, u32[]{:S(2)}, u32[]{:S(2)}) %collective-permute-start.2) | collective-permute-done | bytes 262176 | tf_op jit(solution)/shard_map/ppermute | solution.py:507
  67.7 4.9 %query.1 = bf16[224,1024]{1,0:T(8,128)(2,1)} custom-call(bf16[128,1024]{1,0:T(8,128)(2,1)S(1)} %collective-permute-done.2.halo, bf16[224,1024]{1,0:T(8,128)(2,1)} %get-tuple-element.52.pm_in, f32[384,1024]{1,0:T(8,128)} %copy-done.1, bf16[224,1024]{1,0:T(8,128)(2,1)} %up_in.1, f32[1,1024]{1,0:T(1,128)S(1)} %bitcast.8, ...), custom_call_target="tpu_custom_call" | custom-call | tf_op jit(solution)/shard_map/query/pallas_call | solution.py:509
  72.6 0.0 all-to-all-done.2.refs_0_
  72.6 0.8 %final.1 = (f32[7,16]{1,0:T(8,128)}, f32[16,128]{1,0:T(8,128)}, f32[1,16]{1,0:T(1,128)}, f32[1,16]{1,0:T(1,128)}) custom-call(bf16[16,2,1152]{2,1,0:T(2,128)(2,1)S(1)} %all-to-all-done.2.refs_0_), custom_call_target="tpu_custom_call" | custom-call | tf_op jit(solution)/shard_map/final/pallas_call | solution.py:529
  (13 shorter events, 0.0 us)
Async XLA Ops:
  0.6 6.0 %copy-start = (bf16[224,1024]{1,0:T(8,128)(2,1)S(1)}, bf16[224,1024]{1,0:T(8,128)(2,1)}, u32[]{:S(2)}) copy-start(bf16[224,1024]{1,0:T(8,128)(2,1)} %qse.7) | copy-start | bytes 1376260
  0.7 6.0 %copy-start.2 = (bf16[224,1024]{1,0:T(8,128)(2,1)S(1)}, bf16[224,1024]{1,0:T(8,128)(2,1)}, u32[]{:S(2)}) copy-start(bf16[224,1024]{1,0:T(8,128)(2,1)} %up_in.1) | copy-start | bytes 1376260
  0.7 6.0 %copy-start.4 = (bf16[224,1024]{1,0:T(8,128)(2,1)S(1)}, bf16[224,1024]{1,0:T(8,128)(2,1)}, u32[]{:S(2)}) copy-start(bf16[224,1024]{1,0:T(8,128)(2,1)} %vse.5) | copy-start | bytes 1376260
  0.7 6.0 %copy-start.3 = (bf16[224,1024]{1,0:T(8,128)(2,1)S(1)}, bf16[224,1024]{1,0:T(8,128)(2,1)}, u32[]{:S(2)}) copy-start(bf16[224,1024]{1,0:T(8,128)(2,1)} %kse.5) | copy-start | bytes 1376260
  0.7 6.0 %copy-start.6 = (bf16[224,1024]{1,0:T(8,128)(2,1)S(1)}, bf16[224,1024]{1,0:T(8,128)(2,1)}, u32[]{:S(2)}) copy-start(bf16[224,1024]{1,0:T(8,128)(2,1)} %qmr.3) | copy-start | bytes 1376260
  0.7 6.0 %copy-start.9 = (f32[7,1024]{1,0:T(8,128)S(1)}, f32[7,1024]{1,0:T(8,128)}, u32[]{:S(2)}) copy-start(f32[7,1024]{1,0:T(8,128)} %fse.5) | copy-start | bytes 86020
  2.1 8.7 %collective-permute-start.1 = (bf16[160,1024]{1,0:T(8,128)(2,1)S(1)}, bf16[160,1024]{1,0:T(8,128)(2,1)S(1)}, u32[]{:S(2)}, u32[]{:S(2)}) collective-permute-start(bf16[160,1024]{1,0:T(8,128)(2,1)S(1)} %get-tuple-element.35), channel_id=1, source_target_pairs={{8,0},{16,8},{24,16},{32,24},{40,32},{48,40},{56,48},{64,56},{72,6... | collective-permute-start | bytes 983048 | tf_op jit(solution)/shard_map/ppermute | solution.py:469
  4.6 6.2 %copy-start.5 = (bf16[224,1024]{1,0:T(8,128)(2,1)S(1)}, bf16[224,1024]{1,0:T(8,128)(2,1)}, u32[]{:S(2)}) copy-start(bf16[224,1024]{1,0:T(8,128)(2,1)} %kmr.5) | copy-start | bytes 1376260
  4.6 6.2 %copy-start.8 = (bf16[232,384]{1,0:T(8,128)(2,1)S(1)}, bf16[232,384]{1,0:T(8,128)(2,1)}, u32[]{:S(2)}) copy-start(bf16[232,384]{1,0:T(8,128)(2,1)} %constant.15.clone.th.th_in) | copy-start | bytes 534532
  4.6 6.2 %copy-start.11 = (bf16[384,136]{1,0:T(8,128)(2,1)S(1)}, bf16[384,136]{1,0:T(8,128)(2,1)}, u32[]{:S(2)}) copy-start(bf16[384,136]{1,0:T(8,128)(2,1)} %constant.14.clone.fhh) | copy-start | bytes 313348
  4.6 6.2 %copy-start.12 = (f32[1024]{0:T(1024)S(1)}, f32[1024]{0:T(1024)}, u32[]{:S(2)}) copy-start(f32[1024]{0:T(1024)} %param.25) | copy-start | bytes 12292
  4.6 6.2 %copy-start.13 = (f32[1024]{0:T(1024)S(1)}, f32[1024]{0:T(1024)}, u32[]{:S(2)}) copy-start(f32[1024]{0:T(1024)} %param.24) | copy-start | bytes 12292
  4.6 6.2 %collective-permute-start = (bf16[8,1024]{1,0:T(8,128)(2,1)S(1)}, bf16[8,1024]{1,0:T(8,128)(2,1)S(1)}, u32[]{:S(2)}, u32[]{:S(2)}) collective-permute-start(bf16[8,1024]{1,0:T(8,128)(2,1)S(1)} %get-tuple-element.34), channel_id=1, source_target_pairs={{0,8},{8,16},{16,24},{24,32},{32,40},{40,48},{48,56},{56,64},{64,7... | collective-permute-start | bytes 49160 | tf_op jit(solution)/shard_map/ppermute | solution.py:470
  9.6 3.6 %copy-start.1 = (f32[384,1024]{1,0:T(8,128)}, f32[384,1024]{1,0:T(8,128)S(1)}, u32[]{:S(2)}) copy-start(f32[384,1024]{1,0:T(8,128)S(1)} %get-tuple-element.39.hspec.hspec_in) | copy-start | bytes 4718596
  10.8 16.6 %copy-start.7 = (bf16[384,224]{1,0:T(8,128)(2,1)S(1)}, bf16[384,224]{1,0:T(8,128)(2,1)}, u32[]{:S(2)}) copy-start(bf16[384,224]{1,0:T(8,128)(2,1)} %constant.12.clone.fxh_in.fxh) | copy-start | bytes 516100
  10.8 16.5 %copy-start.10 = (bf16[128,1024]{1,0:T(8,128)(2,1)S(1)}, bf16[128,1024]{1,0:T(8,128)(2,1)}, u32[]{:S(2)}) copy-start(bf16[128,1024]{1,0:T(8,128)(2,1)} %constant.16.clone.spots) | copy-start | bytes 786436
  42.5 30.2 %all-to-all-start.2 = ((bf16[16,2,1152]{2,1,0:T(2,128)(2,1)}), bf16[16,2,1152]{2,1,0:T(2,128)(2,1)S(1)}, u32[]{:S(2)}, u32[]{:S(2)}) async-start(bf16[16,2,1152]{2,1,0:T(2,128)(2,1)} %merge.1), calls=%async_computation.2 | async-start | bytes 147456 | tf_op jit(solution)/shard_map/all_to_all | solution.py:527
  58.3 9.4 %collective-permute-start.2 = (bf16[128,1024]{1,0:T(8,128)(2,1)S(1)}, bf16[128,1024]{1,0:T(8,128)(2,1)S(1)}, u32[]{:S(2)}, u32[]{:S(2)}) collective-permute-start(bf16[128,1024]{1,0:T(8,128)(2,1)S(1)} %get-tuple-element.51), channel_id=1, source_target_pairs={{0,8},{8,16},{16,24},{24,32},{32,40},{40,48},{48,56},{56,64},{64,7... | collective-permute-start | bytes 786440 | tf_op jit(solution)/shard_map/ppermute | solution.py:507

commit v6 on v3

--- a/solution.py
+++ b/solution.py
@@ -7,6 +7,7 @@
 from jax.experimental import pallas as pl
 from jax.experimental.pallas import tpu as pltpu
 from jax.sharding import PartitionSpec as P
+
 
 D = 8192
 EPSILON = 0.1
@@ -29,6 +30,12 @@
     return np.concatenate([np.cos(theta), -np.sin(theta)], 0)
 
 
+def owner_rows(chans):
+    row, chan = np.arange(128)[:, None], np.arange(chans)[None, :]
+    near = row // 32 == (chan // 16) % 4
+    return near & ((row // 2) % 16 == chan // 64) & (row % 2 == (chan // 8) % 2)
+
+
 def halves(matrix):
     high = matrix.astype(BF)
     low = (matrix - high.astype(np.float64)).astype(BF)
@@ -66,10 +73,27 @@
     )
 
 
+def shifted(ref, row, count):
+    return jnp.concatenate([ref[half, pl.ds(row, count), :] for half in range(CB // 128)], 1)
+
+
+def keep(ref, rows, value):
+    for half in range(CB // 128):
+        ref[half, rows] = value[:, half * 128 : half * 128 + 128]
+
+
 def short_conv(ref, taps, row, count):
     total = None
     for step in range(7):
-        term = taps[step : step + 1, :] * ref[pl.ds(row - step, count), :]
+        term = taps[step : step + 1, :] * shifted(ref, row - step, count)
+        total = term if total is None else total + term
+    return total
+
+
+def short_adjoint(ref, taps, row, count):
+    total = None
+    for step in range(7):
+        term = taps[step : step + 1, :] * shifted(ref, row + step, count)
         total = term if total is None else total + term
     return total
 
@@ -117,7 +141,7 @@
 
 
 def local_kernel(
-    up, qmr, kse, vse, qse, fse, fmr_in, fxh_in, fxl_in, gloc, hspec, conv_o, mixed_o, acc_o,
+    up, qmr, kse, vse, qse, fse, fmr_in, fxh_in, fxl_in, gloc, hspec, conv_o, mixed_o, acc_o, p_o, g_o,
     prod, fmr, fxh, fxl, sems
 ):
     pieces = ((fmr_in, fmr), (fxh_in, fxh), (fxl_in, fxl))
@@ -125,12 +149,14 @@
     for copy in copies:
         copy.start()
     acc_o[...] = jnp.zeros_like(acc_o)
-    prod[:8] = jnp.zeros((8, CB), F32)
+    prod[:, :8] = jnp.zeros((CB // 128, 8, 128), F32)
     steps = up.shape[1] // CB
 
     def short(b, carry):
         c = block(b)
-        prod[8:] = rounded(kse[:, c].astype(F32) * vse[:, c].astype(F32))
+        product = rounded(kse[:, c].astype(F32) * vse[:, c].astype(F32))
+        keep(prod, slice(8, None), product)
+        p_o[:, c] = product
         taps = fse[:, c]
         for at in range(0, ROWS, CHUNK):
             conv = short_conv(prod, taps, 8 + at, CHUNK)
@@ -151,6 +177,7 @@
     def spectra(b, carry):
         c = block(b)
         g = (up[:, c].astype(F32) * qmr[:, c].astype(F32)).astype(BF)
+        g_o[:, c] = g.astype(F32)
         gloc[:, c] = forward(fxh[...], fxl[...], g)
         high, low = split(fmr[:, c])
         fh = fxh[:, :128]
@@ -161,7 +188,7 @@
 
 
 def norm_kernel(
-    fwd, bwd, kse, vse, qse, kmr, up, qmr, fse, gain, skip, gloc, hspec, mixed, acc_in, fhh, th,
+    fwd, bwd, p, g_in, qse, kmr, fse, gain, skip, gloc, hspec, mixed, acc_in, fhh, th,
     gp_o, gext_o, conv_e, mixed_e, stats, prod, acc_sq, acc_w
 ):
     acc_sq[...] = acc_in[...]
@@ -176,10 +203,10 @@
         back = jnp.concatenate([(gr * hr + gi * hi).astype(BF), (gi * hr - gr * hi).astype(BF)], 0)
         gp_o[:, c] = dot(th[...], back)
         taps, gains, skips = fse[:, c], gain[:, c], skip[:, c]
-        prod[:8] = fwd[:, c].astype(F32)
-        prod[8:16] = rounded(kse[:8, c].astype(F32) * vse[:8, c].astype(F32))
-        prod[16:24] = rounded(kse[ROWS - 8 :, c].astype(F32) * vse[ROWS - 8 :, c].astype(F32))
-        prod[24:] = bwd[HEAD + 16 :, c].astype(F32)
+        keep(prod, slice(0, 8), fwd[:, c].astype(F32))
+        keep(prod, slice(8, 16), p[:8, c])
+        keep(prod, slice(16, 24), p[ROWS - 8 :, c])
+        keep(prod, slice(24, 32), bwd[HEAD + 16 :, c].astype(F32))
         edges = []
         for k, query in ((0, qse[:8, c]), (1, bwd[HEAD : HEAD + 8, c])):
             conv = short_conv(prod, taps, 8 + 16 * k, 8)
@@ -200,7 +227,7 @@
             mix = mixed[s, c]
             if at == 0:
                 mix = jnp.concatenate([edges[0], mix[8:]], 0)
-            rows(at, CHUNK, mix, kmr[s, c], rounded(up[s, c].astype(F32) * qmr[s, c].astype(F32)))
+            rows(at, CHUNK, mix, kmr[s, c], g_in[s, c])
         rows(ROWS, 8, edges[1], bwd[HEAD + 8 : HEAD + 16, c], bwd[:8, c].astype(F32))
         return carry
 
@@ -237,7 +264,7 @@
 
 
 def filter_kernel(
-    stats, fwd, mixed, mixed_e, gp, kmr, qse, up, qmr, kse, vse, gain, gext, fxh, th,
+    stats, fwd, p, g_in, mixed, mixed_e, gp, kmr, qse, gain, gext, fxh, th, spots,
     payload, halo, prod, small, scale_s, coef_s, pms
 ):
     steps = gext.shape[1] // CB
@@ -245,8 +272,8 @@
 
     def step(b, carry):
         c = block(b)
-        prod[:8] = fwd[:, c].astype(F32)
-        prod[8:] = rounded(kse[:, c].astype(F32) * vse[:, c].astype(F32))
+        keep(prod, slice(0, 8), fwd[:, c].astype(F32))
+        keep(prod, slice(8, None), p[:, c])
         gains = gain[:, c]
         sums = [jnp.zeros((8, CB), F32) for _ in range(9)]
         for at in range(0, ROWS, CHUNK):
@@ -254,18 +281,19 @@
             mix = merged_rows(mixed, mixed_e, at, CHUNK, c)
             scale = wide(scale_s[s])
             key = kmr[s, c].astype(F32)
-            gn = gp[s, c] * key
+            grad = gp[s, c]
+            gn = grad * key
             ms = mix * scale
-            pm = (key * (ms * gains)).astype(BF)
+            normed = ms * gains
+            pm = (key * normed).astype(BF)
             pms[s] = pm
             if at >= ROWS - HALO:
                 halo[at - (ROWS - HALO) : at - (ROWS - HALO) + CHUNK, c] = pm
             gm = gains * scale * gn - mix * wide(coef_s[s])
             gc = rounded(gm * qse[s, c].astype(F32))
-            g = rounded(up[s, c].astype(F32) * qmr[s, c].astype(F32))
             for tap in range(7):
-                sums[tap] = sums[tap] + eights(gc * prod[pl.ds(8 + at - tap, CHUNK), :])
-            sums[7] = sums[7] + eights(g * pm.astype(F32))
+                sums[tap] = sums[tap] + eights(gc * shifted(prod, 8 + at - tap, CHUNK))
+            sums[7] = sums[7] + eights(g_in[s, c] * pm.astype(F32))
             sums[8] = sums[8] + eights(gn * ms)
         parts = [jnp.sum(x, axis=0, keepdims=True) for x in sums]
         small[b] = jnp.concatenate(parts + [jnp.zeros((7, CB), F32)], 0)
@@ -287,18 +315,14 @@
     row = lax.broadcasted_iota(jnp.int32, (16, 128), 0)
     spread = (lane % 16 == row).astype(BF)
     chan = lax.broadcasted_iota(jnp.int32, (CB, 128), 0)
-    keep = chan % 8 == lax.broadcasted_iota(jnp.int32, (CB, 128), 1) // 16
-    out_row = lax.broadcasted_iota(jnp.int32, (128, CB), 0)
-    out_chan = lax.broadcasted_iota(jnp.int32, (128, CB), 1)
+    own = chan % 8 == lax.broadcasted_iota(jnp.int32, (CB, 128), 1) // 16
     packed = None
     for b in range(steps):
         tiled = lax.dot_general(
             small[b].astype(BF), spread, (((0,), (0,)), ((), ())), preferred_element_type=F32
         )
-        masked = jnp.where(keep, tiled, 0.0).astype(BF)
-        ch = out_chan + b * CB
-        take = (out_row // 32 == (ch // 16) % 4) & ((out_row // 2) % 16 == ch // 64) & (out_row % 2 == (ch // 8) % 2)
-        part = dot(take.astype(BF), masked)
+        masked = jnp.where(own, tiled, 0.0).astype(BF)
+        part = dot(spots[:, b * CB : b * CB + CB], masked)
         packed = part if packed is None else packed + part
     packed = packed.astype(BF)
     for yc in range(4):
@@ -324,11 +348,11 @@
         gkmr[s] = (grad * normed).astype(BF)
         gm = gains * scale * (grad * key) - mix * wide(coef_s[s])
         gqse[s] = (gm * con).astype(BF)
-        gcs[s] = rounded(gm * qse[s].astype(F32))
+        keep(gcs, s, rounded(gm * qse[s].astype(F32)))
     nxt = slice(ROWS, ROWS + 8)
     gn = gp[nxt] * bwd[HEAD + 8 : HEAD + 16].astype(F32)
     gm = gains * wide(scale_s[nxt]) * gn - mixed_e[8:] * wide(coef_s[nxt])
-    gcs[nxt] = rounded(gm * bwd[HEAD : HEAD + 8].astype(F32))
+    keep(gcs, nxt, rounded(gm * bwd[HEAD : HEAD + 8].astype(F32)))
     x, h = dot(fxh[...], pms[...]) + dot(fhalo[...], halo[...]), hspec[...]
     xr, xi, hr, hi = x[:HALF], x[HALF:], h[:HALF], h[HALF:]
     spec = jnp.concatenate([(xr * hr - xi * hi).astype(BF), (xi * hr + xr * hi).astype(BF)], 0)
@@ -336,10 +360,7 @@
     for at in range(0, ROWS, CHUNK):
         s = slice(at, at + CHUNK)
         gqmr[s] = (up[s].astype(F32) * (ym[s] + skips * pms[s].astype(F32))).astype(BF)
-        gps = None
-        for tap in range(7):
-            term = taps[tap : tap + 1, :] * gcs[pl.ds(at + tap, CHUNK), :]
-            gps = term if gps is None else gps + term
+        gps = short_adjoint(gcs, taps, at, CHUNK)
         gkse[s] = (gps * vse[s].astype(F32)).astype(BF)
         gvse[s] = (gps * kse[s].astype(F32)).astype(BF)
 
@@ -349,15 +370,16 @@
     for k in range(1, 4):
         total = total + got[k].astype(F32)
     for z in range(16):
-        out[z, :16] = total[z * 16 : z * 16 + 16].astype(BF)
-        pair = total[256 + z * 2 : 256 + z * 2 + 2]
-        out[z, 16:] = jnp.concatenate([pair, jnp.zeros((6, 128), F32)], 0).astype(BF)
+        for k in range(9):
+            at = z * 16 + 2 * k if k < 8 else 256 + 2 * z
+            out[z, :, 128 * k : 128 * k + 128] = total[at : at + 2].astype(BF)
 
 
 def final_kernel(got, se_o, mr_o, skip_o, gain_o, *, factor):
-    total = got[0].astype(F32)
+    packed = got[0].astype(F32)
     for k in range(1, 16):
-        total = total + got[k].astype(F32)
+        packed = packed + got[k].astype(F32)
+    total = jnp.concatenate([packed[:, 128 * k : 128 * k + 128] for k in range(9)], 0)
     total = total * factor
     mr_o[...] = total[:16]
     chan = lax.broadcasted_iota(jnp.int32, (16, 128), 0)
@@ -391,6 +413,9 @@
     def vmem(rows, width, dtype):
         return pltpu.VMEM((rows, width), dtype)
 
+    def shifts(rows):
+        return pltpu.VMEM((CB // 128, rows, 128), F32)
+
     def kept(x):
         return pltpu.with_memory_space_constraint(x, pltpu.HBM)
 
@@ -411,12 +436,12 @@
     bwd = lax.ppermute(bwd, "ctx", upward)
     fwd = lax.ppermute(fwd, "ctx", down)
 
-    gloc, hspec, conv, mixed, acc = pl.pallas_call(
+    gloc, hspec, conv, mixed, acc, p, g = pl.pallas_call(
         local_kernel,
         in_specs=[here] * 6 + [hbm] * 3,
         out_shape=[shape(LEN, F32), shape(LEN, F32), shape(ROWS, F32), shape(ROWS, F32),
-                   jax.ShapeDtypeStruct((256, 128), F32)],
-        scratch_shapes=[vmem(ROWS + 8, CB, F32), vmem(filter_mr.shape[0], chans, F32), vmem(LEN, ROWS, BF),
+                   jax.ShapeDtypeStruct((256, 128), F32), shape(ROWS, F32), shape(ROWS, F32)],
+        scratch_shapes=[shifts(ROWS + 8), vmem(filter_mr.shape[0], chans, F32), vmem(LEN, ROWS, BF),
                         vmem(LEN, ROWS, BF), pltpu.SemaphoreType.DMA((3,))],
         compiler_params=params,
         name="local",
@@ -426,10 +451,10 @@
         norm_kernel,
         out_shape=[shape(EXT, F32), shape(LEN, F32), shape(16, F32), shape(16, F32),
                    jax.ShapeDtypeStruct((8, 8, 128), F32)],
-        scratch_shapes=[vmem(32, CB, F32), vmem(256, 128, F32), vmem(256, 128, F32)],
+        scratch_shapes=[shifts(32), vmem(256, 128, F32), vmem(256, 128, F32)],
         compiler_params=params,
         name="norm",
-    )(fwd, bwd, key_se, value_se, query_se, key_mr, upstream, query_mr, filter_se, gain2, skip2, gloc, hspec,
+    )(fwd, bwd, p, g, query_se, key_mr, filter_se, gain2, skip2, gloc, hspec,
       mixed, acc, fhead, back)
 
     stats = lax.all_to_all(stats, "tp", 0, 0, tiled=True)
@@ -437,11 +462,11 @@
     payload, halo = pl.pallas_call(
         filter_kernel,
         out_shape=[jax.ShapeDtypeStruct((4, 288, 128), BF), shape(HALO, BF)],
-        scratch_shapes=[vmem(ROWS + 8, CB, F32), pltpu.VMEM((steps, 16, CB), F32), vmem(256, 128, F32),
-                        vmem(256, 128, F32), vmem(ROWS, CB, BF)],
+        scratch_shapes=[shifts(ROWS + 8), pltpu.VMEM((steps, 16, CB), F32), vmem(256, 128, F32), vmem(256, 128, F32),
+                        vmem(ROWS, CB, BF)],
         compiler_params=params,
         name="filters",
-    )(stats, fwd, mixed, mixed_e, gp, key_mr, query_se, upstream, query_mr, key_se, value_se, gain2, gext, fxh, back)
+    )(stats, fwd, p, g, mixed, mixed_e, gp, key_mr, query_se, gain2, gext, fxh, back, owner_rows(chans).astype(BF))
     halo = lax.ppermute(halo, "ctx", down)
 
     def cols(rows):
@@ -450,24 +475,25 @@
     def whole(*dims):
         return pl.BlockSpec(dims, lambda i: (0,) * len(dims))
 
-    late = (stats, halo, hspec, mixed, conv, mixed_e, conv_e, gp, bwd, upstream, key_mr, key_se, value_se, query_se,
-            gain2, skip2, filter_se, fxh, fhalo, back)
-    outs = pl.pallas_call(
+    late = (hspec, mixed, conv, mixed_e, conv_e, gp, bwd, upstream, key_mr, key_se, value_se, query_se, gain2, skip2,
+            filter_se)
+    bases = (fxh, fhalo, back)
+    gqse, gkse, gvse, gqmr, gkmr = pl.pallas_call(
         rest_kernel,
         grid=(steps,),
-        in_specs=[whole(8, 8, 128)] + [cols(x.shape[0]) for x in late[1:17]] + [whole(*x.shape) for x in late[17:]],
+        in_specs=[whole(8, 8, 128), cols(HALO)] + [cols(x.shape[0]) for x in late] + [whole(*x.shape) for x in bases],
         out_specs=[cols(ROWS)] * 5,
         out_shape=[shape(ROWS, BF)] * 5,
-        scratch_shapes=[vmem(256, 128, F32), vmem(256, 128, F32), vmem(EXT, CB, F32), vmem(ROWS, CB, BF)],
+        scratch_shapes=[vmem(256, 128, F32), vmem(256, 128, F32), shifts(EXT), vmem(ROWS, CB, BF)],
         compiler_params=params,
         name="rest",
-    )(*(kept(x) for x in late))
+    )(kept(stats), halo, *(kept(x) for x in late + bases))
 
     near = [[4 * a + b for b in range(4)] for a in range(size // 4)]
     far = [[4 * a + b for a in range(size // 4)] for b in range(4)]
     got = lax.all_to_all(payload, "ctx", 0, 0, axis_index_groups=near, tiled=True)
     merged = pl.pallas_call(
-        merge_kernel, out_shape=jax.ShapeDtypeStruct((16, 24, 128), BF), compiler_params=params, name="merge"
+        merge_kernel, out_shape=jax.ShapeDtypeStruct((16, 2, 1152), BF), compiler_params=params, name="merge"
     )(got)
     got = lax.all_to_all(merged, "ctx", 0, 0, axis_index_groups=far, tiled=True)
     factor = 1.0 / math.sqrt(ROWS * size)
@@ -478,7 +504,7 @@
         compiler_params=params,
         name="final",
     )(got)
-    return (*outs, se, mr.T, sk.reshape(16), ga.reshape(16))
+    return (gqse, gkse, gvse, gqmr, gkmr, se, mr.T, sk.reshape(16), ga.reshape(16))
 
 
 def solution(mesh):

time: 77.1 us -> 75 us (0.973)
  Pallas kernels: 20.3 us -> 19.2 us
    pallas_call x1, Pallas kernels: 4.83 us -> 4.05 us  [local(): pl.pallas_call(filter_kernel, out_shape=[jax.ShapeDtypeStruct((4, 288, 12...]
where the time goes in v6:
time: 75 us; the launch traced here: 74.5 us
  blocking collectives  23.3 us (31%)
  starting transfers between devices  22.3 us (30%)
  Pallas kernels  19.2 us (26%)
  waiting for transfers between devices  8.64 us (12%)
  between operations  0.99 us (1%)
    all_to_all x1, starting transfers between devices, local(): got = lax.all_to_all(merged, 'ctx', 0, 0, axis_index_groups=far, tiled=True)  15.9 us
    all_to_all x1, blocking collectives, local(): stats = lax.all_to_all(stats, 'tp', 0, 0, tiled=True)  14.2 us
    all_to_all x1, blocking collectives, local(): lax.all_to_all(payload, 'ctx', 0, 0, axis_index_groups=near, tiled=True)  9.15 us
    ppermute x1, waiting for transfers between devices, local(): halo = lax.ppermute(halo, 'ctx', down)  7.46 us
    pallas_call x1, Pallas kernels, local(): pl.pallas_call(rest_kernel, grid=(steps,), in_specs=[whole(8, 8, 128), co...  7.09 us
    pallas_call x1, Pallas kernels, local(): pl.pallas_call(filter_kernel, out_shape=[jax.ShapeDtypeStruct((4, 288, 12...  4.05 us
    pallas_call x1, Pallas kernels, local(): pl.pallas_call(local_kernel, in_specs=[here] * 6 + [hbm] * 3, out_shape=[...  2.84 us
    ppermute x1, starting transfers between devices, local(): bwd = lax.ppermute(bwd, 'ctx', upward)  2.47 us
  transfers between devices with their start and end apart: 4, of which 2 were waited for; matrix products, arithmetic and copies ran while one was open for 0% of the time, Pallas kernels for 13%

profile of v6, /device:TPU:32, one launch (start us, length us, event | category | flops | bytes accessed | tf_op | source)
XLA Modules:
  0.0 74.5 jit_solution(16178332598021701616)
XLA Ops:
  0.6 0.0 copy-start
  0.7 0.0 copy-start.6
  0.7 0.0 copy-start.5
  0.7 0.0 copy-start.4
  0.7 0.0 copy-start.13
  0.7 1.4 %send.1 = (bf16[8,1024]{1,0:T(8,128)(2,1)S(1)}, bf16[160,1024]{1,0:T(8,128)(2,1)S(1)}) custom-call(bf16[224,1024]{1,0:T(8,128)(2,1)} %kse.5, bf16[224,1024]{1,0:T(8,128)(2,1)} %vse.5, bf16[224,1024]{1,0:T(8,128)(2,1)} %qse.9, bf16[224,1024]{1,0:T(8,128)(2,1)} %kmr.7, bf16[224,1024]{1,0:T(8,128)(2,1)} %up.5, bf16[224,1024]{1,0:T(8,128)(2,1)} %qmr.3), custom_call_target="tpu_custom_call" | custom-call | tf_op jit(solution)/shard_map/send/pallas_call | solution.py:425
  2.1 2.5 %collective-permute-start.1 = (bf16[160,1024]{1,0:T(8,128)(2,1)S(1)}, bf16[160,1024]{1,0:T(8,128)(2,1)S(1)}, u32[]{:S(2)}, u32[]{:S(2)}) collective-permute-start(bf16[160,1024]{1,0:T(8,128)(2,1)S(1)} %get-tuple-element.35), channel_id=1, source_target_pairs={{8,0},{16,8},{24,16},{32,24},{40,32},{48,40},{56,48},{64,56},{72,6... | collective-permute-start | bytes 983048 | tf_op jit(solution)/shard_map/ppermute | solution.py:436
  4.6 0.0 copy-start.2
  4.6 0.0 copy-start.10
  4.6 0.0 copy-start.17
  4.6 0.0 copy-start.19
  4.6 0.0 copy-start.20
  4.6 2.1 %collective-permute-start = (bf16[8,1024]{1,0:T(8,128)(2,1)S(1)}, bf16[8,1024]{1,0:T(8,128)(2,1)S(1)}, u32[]{:S(2)}, u32[]{:S(2)}) collective-permute-start(bf16[8,1024]{1,0:T(8,128)(2,1)S(1)} %get-tuple-element.34), channel_id=1, source_target_pairs={{0,8},{8,16},{16,24},{24,32},{32,40},{40,48},{48,56},{56,64},{64,7... | collective-permute-start | bytes 49160 | tf_op jit(solution)/shard_map/ppermute | solution.py:437
  6.7 0.0 copy-done
  6.7 0.0 copy-done.6
  6.7 2.8 %local.1 = (f32[384,1024]{1,0:T(8,128)S(1)}, f32[384,1024]{1,0:T(8,128)S(1)}, f32[224,1024]{1,0:T(8,128)S(1)}, f32[224,1024]{1,0:T(8,128)S(1)}, f32[256,128]{1,0...) custom-call(bf16[224,1024]{1,0:T(8,128)(2,1)S(1)} %copy-done.6, bf16[224,1024]{1,0:T(8,128)(2,1)S(1)} %copy-done.8, ...), custom_call_target="tpu_custom_call" | custom-call | tf_op jit(solution)/shard_map/local/pallas_call | solution.py:439
  9.6 1.2 %collective-permute-done.fwd = bf16[8,1024]{1,0:T(8,128)(2,1)S(1)} collective-permute-done((bf16[8,1024]{1,0:T(8,128)(2,1)S(1)}, bf16[8,1024]{1,0:T(8,128)(2,1)S(1)}, u32[]{:S(2)}, u32[]{:S(2)}) %collective-permute-start) | collective-permute-done | bytes 16416 | tf_op jit(solution)/shard_map/ppermute | solution.py:437
  10.8 0.0 collective-permute-done.1.bwd
  10.8 0.0 copy-start.9
  10.9 0.0 copy-start.16
  10.9 2.4 %norm.1 = (f32[232,1024]{1,0:T(8,128)S(1)}, f32[384,1024]{1,0:T(8,128)S(1)}, f32[16,1024]{1,0:T(8,128)S(1)}, f32[16,1024]{1,0:T(8,128)S(1)}, f32[8,8,128]{2,1,0:T(8,128)S(1)}) custom-call(bf16[8,1024]{1,0:T(8,128)(2,1)S(1)} %collective-permute-done.fwd, bf16[160,1024]{1,0:T(8,128)(2,1)S(1)} %collective-permute-done.1.bwd, ...), custom_call_target="tpu_custom_call" | custom-call | tf_op jit(solution)/shard_map/norm/pallas_call | solution.py:450
  13.2 0.0 copy-done.12
  13.3 14.2 %all_to_all.15.stats = f32[8,8,128]{2,1,0:T(8,128)S(1)} all-to-all(f32[8,8,128]{2,1,0:T(8,128)S(1)} %get-tuple-element.42), channel_id=1, replica_groups=mesh['ctx'=64,'tp'=8] {'tp'}, dimensions={0} | all-to-all | bytes 65536 | tf_op jit(solution)/shard_map/all_to_all | solution.py:460
  27.5 4.1 %filters.1 = (bf16[4,288,128]{2,1,0:T(8,128)(2,1)S(1)}, bf16[128,1024]{1,0:T(8,128)(2,1)S(1)}) custom-call(f32[8,8,128]{2,1,0:T(8,128)S(1)} %all_to_all.15.stats, bf16[8,1024]{1,0:T(8,128)(2,1)S(1)} %collective-permute-done.fwd, f32[224,1024]{1,0:T(8,128)S(1)} %get-tuple-element.36.p, f32[224,1024]{1,0:T(8,128)S(1)} %get-tuple-element.37.g_in, ...), custom_call_target="tpu_custom_call" | custom-call | tf_op jit(solution)/shard_map/filters/pallas_call | solution.py:462
  31.6 9.1 %all_to_all.16.got = bf16[4,288,128]{2,1,0:T(8,128)(2,1)S(1)} all-to-all(bf16[4,288,128]{2,1,0:T(8,128)(2,1)S(1)} %get-tuple-element.54), channel_id=1, replica_groups={{0,8,16,24},{32,40,48,56},{64,72,80,88},{96,104,112,120},{128,136,144,1..., dimensions={0} | all-to-all | bytes 589824 | tf_op jit(solution)/shard_map/all_to_all | solution.py:494
  40.7 0.7 merge.1
  41.4 15.9 %all-to-all-start.2 = ((bf16[16,2,1152]{2,1,0:T(2,128)(2,1)}), bf16[16,2,1152]{2,1,0:T(2,128)(2,1)S(1)}, u32[]{:S(2)}, u32[]{:S(2)}) async-start(bf16[16,2,1152]{2,1,0:T(2,128)(2,1)} %merge.1), calls=%async_computation.2 | async-start | bytes 147456 | tf_op jit(solution)/shard_map/all_to_all | solution.py:498
  57.3 1.9 %collective-permute-start.2 = (bf16[128,1024]{1,0:T(8,128)(2,1)S(1)}, bf16[128,1024]{1,0:T(8,128)(2,1)S(1)}, u32[]{:S(2)}, u32[]{:S(2)}) collective-permute-start(bf16[128,1024]{1,0:T(8,128)(2,1)S(1)} %get-tuple-element.46), channel_id=1, source_target_pairs={{0,8},{8,16},{16,24},{24,32},{32,40},{40,48},{48,56},{56,64},{64,7... | collective-permute-start | bytes 786440 | tf_op jit(solution)/shard_map/ppermute | solution.py:470
  59.2 7.5 %collective-permute-done.2.halo = bf16[128,1024]{1,0:T(8,128)(2,1)S(1)} collective-permute-done((bf16[128,1024]{1,0:T(8,128)(2,1)S(1)}, bf16[128,1024]{1,0:T(8,128)(2,1)S(1)}, u32[]{:S(2)}, u32[]{:S(2)}) %collective-permute-start.2) | collective-permute-done | bytes 262176 | tf_op jit(solution)/shard_map/ppermute | solution.py:470
  66.7 7.1 %rest.1 = (bf16[224,1024]{1,0:T(8,128)(2,1)}, bf16[224,1024]{1,0:T(8,128)(2,1)}, bf16[224,1024]{1,0:T(8,128)(2,1)}, bf16[224,1024]{1,0:T(8,128)(2,1)}, bf16[224,1024]{1,0:T(8,128)(2,1)}) custom-call(f32[8,8,128]{2,1,0:T(8,128)} %copy-done.14, bf16[128,1024]{1,0:T(8,128)(2,1)S(1)} %collective-permute-done.2.halo, f32[384,1024]{1,0:T(8,128)} %copy-done.3, ...), custom_call_target="tpu_custom_call" | custom-call | tf_op jit(solution)/shard_map/rest/pallas_call | solution.py:481
  73.8 0.0 all-to-all-done.2.refs_0_
  73.8 0.8 %final.1 = (f32[7,16]{1,0:T(8,128)}, f32[16,128]{1,0:T(8,128)}, f32[1,16]{1,0:T(1,128)}, f32[1,16]{1,0:T(1,128)}) custom-call(bf16[16,2,1152]{2,1,0:T(2,128)(2,1)S(1)} %all-to-all-done.2.refs_0_), custom_call_target="tpu_custom_call" | custom-call | tf_op jit(solution)/shard_map/final/pallas_call | solution.py:500
  (27 shorter events, 0.1 us)
Async XLA Ops:
  0.6 6.0 %copy-start = (bf16[224,1024]{1,0:T(8,128)(2,1)S(1)}, bf16[224,1024]{1,0:T(8,128)(2,1)}, u32[]{:S(2)}) copy-start(bf16[224,1024]{1,0:T(8,128)(2,1)} %qse.9) | copy-start | bytes 1376260
  0.7 6.0 %copy-start.6 = (bf16[224,1024]{1,0:T(8,128)(2,1)S(1)}, bf16[224,1024]{1,0:T(8,128)(2,1)}, u32[]{:S(2)}) copy-start(bf16[224,1024]{1,0:T(8,128)(2,1)} %up.5) | copy-start | bytes 1376260
  0.7 6.0 %copy-start.5 = (bf16[224,1024]{1,0:T(8,128)(2,1)S(1)}, bf16[224,1024]{1,0:T(8,128)(2,1)}, u32[]{:S(2)}) copy-start(bf16[224,1024]{1,0:T(8,128)(2,1)} %vse.5) | copy-start | bytes 1376260
  0.7 6.0 %copy-start.4 = (bf16[224,1024]{1,0:T(8,128)(2,1)S(1)}, bf16[224,1024]{1,0:T(8,128)(2,1)}, u32[]{:S(2)}) copy-start(bf16[224,1024]{1,0:T(8,128)(2,1)} %kse.5) | copy-start | bytes 1376260
  0.7 6.0 %copy-start.8 = (bf16[224,1024]{1,0:T(8,128)(2,1)S(1)}, bf16[224,1024]{1,0:T(8,128)(2,1)}, u32[]{:S(2)}) copy-start(bf16[224,1024]{1,0:T(8,128)(2,1)} %qmr.3) | copy-start | bytes 1376260
  0.7 6.0 %copy-start.13 = (f32[7,1024]{1,0:T(8,128)S(1)}, f32[7,1024]{1,0:T(8,128)}, u32[]{:S(2)}) copy-start(f32[7,1024]{1,0:T(8,128)} %fse.5) | copy-start | bytes 86020
  2.1 8.7 %collective-permute-start.1 = (bf16[160,1024]{1,0:T(8,128)(2,1)S(1)}, bf16[160,1024]{1,0:T(8,128)(2,1)S(1)}, u32[]{:S(2)}, u32[]{:S(2)}) collective-permute-start(bf16[160,1024]{1,0:T(8,128)(2,1)S(1)} %get-tuple-element.35), channel_id=1, source_target_pairs={{8,0},{16,8},{24,16},{32,24},{40,32},{48,40},{56,48},{64,56},{72,6... | collective-permute-start | bytes 983048 | tf_op jit(solution)/shard_map/ppermute | solution.py:436
  4.6 6.2 %copy-start.2 = (bf16[224,1024]{1,0:T(8,128)(2,1)S(1)}, bf16[224,1024]{1,0:T(8,128)(2,1)}, u32[]{:S(2)}) copy-start(bf16[224,1024]{1,0:T(8,128)(2,1)} %kmr.7) | copy-start | bytes 1376260
  4.6 6.2 %copy-start.10 = (bf16[232,384]{1,0:T(8,128)(2,1)S(1)}, bf16[232,384]{1,0:T(8,128)(2,1)}, u32[]{:S(2)}) copy-start(bf16[232,384]{1,0:T(8,128)(2,1)} %constant.15.clone.th) | copy-start | bytes 534532
  4.6 6.2 %copy-start.17 = (bf16[384,136]{1,0:T(8,128)(2,1)S(1)}, bf16[384,136]{1,0:T(8,128)(2,1)}, u32[]{:S(2)}) copy-start(bf16[384,136]{1,0:T(8,128)(2,1)} %constant.14.clone.fhh) | copy-start | bytes 313348
  4.6 6.2 %copy-start.19 = (f32[1024]{0:T(1024)S(1)}, f32[1024]{0:T(1024)}, u32[]{:S(2)}) copy-start(f32[1024]{0:T(1024)} %param.25) | copy-start | bytes 12292
  4.6 6.2 %copy-start.20 = (f32[1024]{0:T(1024)S(1)}, f32[1024]{0:T(1024)}, u32[]{:S(2)}) copy-start(f32[1024]{0:T(1024)} %param.24) | copy-start | bytes 12292
  4.6 6.2 %collective-permute-start = (bf16[8,1024]{1,0:T(8,128)(2,1)S(1)}, bf16[8,1024]{1,0:T(8,128)(2,1)S(1)}, u32[]{:S(2)}, u32[]{:S(2)}) collective-permute-start(bf16[8,1024]{1,0:T(8,128)(2,1)S(1)} %get-tuple-element.34), channel_id=1, source_target_pairs={{0,8},{8,16},{16,24},{24,32},{32,40},{40,48},{48,56},{56,64},{64,7... | collective-permute-start | bytes 49160 | tf_op jit(solution)/shard_map/ppermute | solution.py:437
  9.6 3.6 %copy-start.3 = (f32[384,1024]{1,0:T(8,128)}, f32[384,1024]{1,0:T(8,128)S(1)}, u32[]{:S(2)}) copy-start(f32[384,1024]{1,0:T(8,128)S(1)} %get-tuple-element.39.hspec) | copy-start | bytes 4718596
  9.6 3.6 %copy-start.12 = (f32[224,1024]{1,0:T(8,128)}, f32[224,1024]{1,0:T(8,128)S(1)}, u32[]{:S(2)}) copy-start(f32[224,1024]{1,0:T(8,128)S(1)} %get-tuple-element.47.conv) | copy-start | bytes 2752516
  9.6 17.9 %copy-start.1 = (f32[224,1024]{1,0:T(8,128)}, f32[224,1024]{1,0:T(8,128)S(1)}, u32[]{:S(2)}) copy-start(f32[224,1024]{1,0:T(8,128)S(1)} %get-tuple-element.40.mixed) | copy-start | bytes 2752516
  10.8 2.5 %copy-start.11 = (bf16[160,1024]{1,0:T(8,128)(2,1)}, bf16[160,1024]{1,0:T(8,128)(2,1)S(1)}, u32[]{:S(2)}) copy-start(bf16[160,1024]{1,0:T(8,128)(2,1)S(1)} %collective-permute-done.1.bwd) | copy-start | bytes 983044
  10.8 16.6 %copy-start.9 = (bf16[384,224]{1,0:T(8,128)(2,1)S(1)}, bf16[384,224]{1,0:T(8,128)(2,1)}, u32[]{:S(2)}) copy-start(bf16[384,224]{1,0:T(8,128)(2,1)} %constant.12.clone.fxh_in.fxh) | copy-start | bytes 516100
  10.9 16.6 %copy-start.16 = (bf16[128,1024]{1,0:T(8,128)(2,1)S(1)}, bf16[128,1024]{1,0:T(8,128)(2,1)}, u32[]{:S(2)}) copy-start(bf16[128,1024]{1,0:T(8,128)(2,1)} %constant.16.clone.spots) | copy-start | bytes 786436
  13.3 18.3 %copy-start.7 = (f32[232,1024]{1,0:T(8,128)}, f32[232,1024]{1,0:T(8,128)S(1)}, u32[]{:S(2)}) copy-start(f32[232,1024]{1,0:T(8,128)S(1)} %get-tuple-element.44.gp) | copy-start | bytes 2850820
  13.3 18.3 %copy-start.15 = (f32[16,1024]{1,0:T(8,128)}, f32[16,1024]{1,0:T(8,128)S(1)}, u32[]{:S(2)}) copy-start(f32[16,1024]{1,0:T(8,128)S(1)} %get-tuple-element.43.mixed_e) | copy-start | bytes 196612
  13.3 18.3 %copy-start.18 = (f32[16,1024]{1,0:T(8,128)}, f32[16,1024]{1,0:T(8,128)S(1)}, u32[]{:S(2)}) copy-start(f32[16,1024]{1,0:T(8,128)S(1)} %get-tuple-element.48.conv_e) | copy-start | bytes 196612
  27.5 4.1 %copy-start.14 = (f32[8,8,128]{2,1,0:T(8,128)}, f32[8,8,128]{2,1,0:T(8,128)S(1)}, u32[]{:S(2)}) copy-start(f32[8,8,128]{2,1,0:T(8,128)S(1)} %all_to_all.15.stats) | copy-start | bytes 98308
  41.4 32.4 %all-to-all-start.2 = ((bf16[16,2,1152]{2,1,0:T(2,128)(2,1)}), bf16[16,2,1152]{2,1,0:T(2,128)(2,1)S(1)}, u32[]{:S(2)}, u32[]{:S(2)}) async-start(bf16[16,2,1152]{2,1,0:T(2,128)(2,1)} %merge.1), calls=%async_computation.2 | async-start | bytes 147456 | tf_op jit(solution)/shard_map/all_to_all | solution.py:498
  57.3 9.4 %collective-permute-start.2 = (bf16[128,1024]{1,0:T(8,128)(2,1)S(1)}, bf16[128,1024]{1,0:T(8,128)(2,1)S(1)}, u32[]{:S(2)}, u32[]{:S(2)}) collective-permute-start(bf16[128,1024]{1,0:T(8,128)(2,1)S(1)} %get-tuple-element.46), channel_id=1, source_target_pairs={{0,8},{8,16},{16,24},{24,32},{32,40},{40,48},{48,56},{56,64},{64,7... | collective-permute-start | bytes 786440 | tf_op jit(solution)/shard_map/ppermute | solution.py:470

commit v7 on v6

--- a/solution.py
+++ b/solution.py
@@ -141,7 +141,7 @@
 
 
 def local_kernel(
-    up, qmr, kse, vse, qse, fse, fmr_in, fxh_in, fxl_in, gloc, hspec, conv_o, mixed_o, acc_o, p_o, g_o,
+    up, qmr, kse, vse, qse, fse, fmr_in, fxh_in, fxl_in, gloc, hspec, hlate, conv_o, mixed_o, acc_o, p_o, g_o,
     prod, fmr, fxh, fxl, sems
 ):
     pieces = ((fmr_in, fmr), (fxh_in, fxh), (fxl_in, fxl))
@@ -181,7 +181,9 @@
         gloc[:, c] = forward(fxh[...], fxl[...], g)
         high, low = split(fmr[:, c])
         fh = fxh[:, :128]
-        hspec[:, c] = dot(fh, high) + dot(fxl[:, :128], high) + dot(fh, low)
+        h = dot(fh, high) + dot(fxl[:, :128], high) + dot(fh, low)
+        hspec[:, c] = h
+        hlate[:, c] = h.astype(BF)
         return carry
 
     lax.fori_loop(0, steps, spectra, 0)
@@ -330,21 +332,21 @@
 
 
 def rest_kernel(
-    stats, halo, hspec, mixed, conv, mixed_e, conv_e, gp, bwd, up, kmr, kse, vse, qse, gain, skip, fse, fxh, fhalo, th,
-    gqse, gkse, gvse, gqmr, gkmr, scale_s, coef_s, gcs, pms
+    stats, mixed, conv, mixed_e, conv_e, gp, bwd, kmr, kse, vse, qse, gain, fse,
+    gqse, gkse, gvse, gkmr, pm_o, scale_s, coef_s, gcs
 ):
     @pl.when(pl.program_id(0) == 0)
     def _():
         scales(stats, scale_s, coef_s)
 
-    gains, taps, skips = gain[...], fse[...], skip[...]
+    gains, taps = gain[...], fse[...]
     for at in range(0, ROWS, CHUNK):
         s = slice(at, at + CHUNK)
         mix = merged_rows(mixed, mixed_e, at, CHUNK)
         con = merged_rows(conv, conv_e, at, CHUNK)
         scale, key, grad = wide(scale_s[s]), kmr[s].astype(F32), gp[s]
         normed = mix * scale * gains
-        pms[s] = (key * normed).astype(BF)
+        pm_o[s] = (key * normed).astype(BF)
         gkmr[s] = (grad * normed).astype(BF)
         gm = gains * scale * (grad * key) - mix * wide(coef_s[s])
         gqse[s] = (gm * con).astype(BF)
@@ -353,16 +355,57 @@
     gn = gp[nxt] * bwd[HEAD + 8 : HEAD + 16].astype(F32)
     gm = gains * wide(scale_s[nxt]) * gn - mixed_e[8:] * wide(coef_s[nxt])
     keep(gcs, nxt, rounded(gm * bwd[HEAD : HEAD + 8].astype(F32)))
-    x, h = dot(fxh[...], pms[...]) + dot(fhalo[...], halo[...]), hspec[...]
-    xr, xi, hr, hi = x[:HALF], x[HALF:], h[:HALF], h[HALF:]
-    spec = jnp.concatenate([(xr * hr - xi * hi).astype(BF), (xi * hr + xr * hi).astype(BF)], 0)
-    ym = dot(th[:ROWS], spec)
     for at in range(0, ROWS, CHUNK):
         s = slice(at, at + CHUNK)
-        gqmr[s] = (up[s].astype(F32) * (ym[s] + skips * pms[s].astype(F32))).astype(BF)
         gps = short_adjoint(gcs, taps, at, CHUNK)
         gkse[s] = (gps * vse[s].astype(F32)).astype(BF)
         gvse[s] = (gps * kse[s].astype(F32)).astype(BF)
+
+
+def query_kernel(
+    halo, pm_in, hspec_in, up_in, skip, fxh_in, fhalo_in, th_in, gqmr,
+    pm, hspec, up, fxh, fhalo, th, out, sems, fixed_sems
+):
+    steps = pm.shape[1] // CB
+
+    def copies(b):
+        c = block(b)
+        pairs = ((pm_in, pm), (hspec_in, hspec), (up_in, up))
+        return [pltpu.make_async_copy(src.at[:, c], dst.at[:, c], sems.at[k, b]) for k, (src, dst) in enumerate(pairs)]
+
+    def out_copy(b):
+        c = block(b)
+        return pltpu.make_async_copy(out.at[:, c], gqmr.at[:, c], sems.at[3, b])
+
+    bases = [
+        pltpu.make_async_copy(src, dst, fixed_sems.at[k])
+        for k, (src, dst) in enumerate(((fxh_in, fxh), (fhalo_in, fhalo), (th_in, th)))
+    ]
+    for copy in bases:
+        copy.start()
+    for b in range(steps):
+        for copy in copies(b):
+            copy.start()
+    for copy in bases:
+        copy.wait()
+
+    def step(b, carry):
+        for copy in copies(b):
+            copy.wait()
+        c = block(b)
+        x, h = dot(fxh[...], pm[:, c]) + dot(fhalo[...], halo[:, c]), hspec[:, c].astype(F32)
+        xr, xi, hr, hi = x[:HALF], x[HALF:], h[:HALF], h[HALF:]
+        spec = jnp.concatenate([(xr * hr - xi * hi).astype(BF), (xi * hr + xr * hi).astype(BF)], 0)
+        ym = dot(th[...], spec)
+        for at in range(0, ROWS, CHUNK):
+            s = slice(at, at + CHUNK)
+            out[s, c] = (up[s, c].astype(F32) * (ym[s] + skip[:, c] * pm[s, c].astype(F32))).astype(BF)
+        out_copy(b).start()
+        return carry
+
+    lax.fori_loop(0, steps, step, 0)
+    for b in range(steps):
+        out_copy(b).wait()
 
 
 def merge_kernel(got, out):
@@ -436,10 +479,10 @@
     bwd = lax.ppermute(bwd, "ctx", upward)
     fwd = lax.ppermute(fwd, "ctx", down)
 
-    gloc, hspec, conv, mixed, acc, p, g = pl.pallas_call(
+    gloc, hspec, hlate, conv, mixed, acc, p, g = pl.pallas_call(
         local_kernel,
         in_specs=[here] * 6 + [hbm] * 3,
-        out_shape=[shape(LEN, F32), shape(LEN, F32), shape(ROWS, F32), shape(ROWS, F32),
+        out_shape=[shape(LEN, F32), shape(LEN, F32), shape(LEN, BF), shape(ROWS, F32), shape(ROWS, F32),
                    jax.ShapeDtypeStruct((256, 128), F32), shape(ROWS, F32), shape(ROWS, F32)],
         scratch_shapes=[shifts(ROWS + 8), vmem(filter_mr.shape[0], chans, F32), vmem(LEN, ROWS, BF),
                         vmem(LEN, ROWS, BF), pltpu.SemaphoreType.DMA((3,))],
@@ -475,19 +518,28 @@
     def whole(*dims):
         return pl.BlockSpec(dims, lambda i: (0,) * len(dims))
 
-    late = (hspec, mixed, conv, mixed_e, conv_e, gp, bwd, upstream, key_mr, key_se, value_se, query_se, gain2, skip2,
-            filter_se)
-    bases = (fxh, fhalo, back)
-    gqse, gkse, gvse, gqmr, gkmr = pl.pallas_call(
+    late = (mixed, conv, mixed_e, conv_e, gp, bwd, key_mr, key_se, value_se, query_se, gain2, filter_se)
+    gqse, gkse, gvse, gkmr, pm = pl.pallas_call(
         rest_kernel,
         grid=(steps,),
-        in_specs=[whole(8, 8, 128), cols(HALO)] + [cols(x.shape[0]) for x in late] + [whole(*x.shape) for x in bases],
+        in_specs=[whole(8, 8, 128)] + [cols(x.shape[0]) for x in late],
         out_specs=[cols(ROWS)] * 5,
-        out_shape=[shape(ROWS, BF)] * 5,
-        scratch_shapes=[vmem(256, 128, F32), vmem(256, 128, F32), shifts(EXT), vmem(ROWS, CB, BF)],
+        out_shape=[shape(ROWS, BF)] * 4 + [pltpu.HBM((ROWS, chans), BF)],
+        scratch_shapes=[vmem(256, 128, F32), vmem(256, 128, F32), shifts(EXT)],
         compiler_params=params,
         name="rest",
-    )(kept(stats), halo, *(kept(x) for x in late + bases))
+    )(kept(stats), *(kept(x) for x in late))
+    gqmr = pl.pallas_call(
+        query_kernel,
+        in_specs=[here] + [hbm] * 3 + [here] + [hbm] * 3,
+        out_specs=hbm,
+        out_shape=shape(ROWS, BF),
+        scratch_shapes=[vmem(ROWS, chans, BF), vmem(LEN, chans, BF), vmem(ROWS, chans, BF), vmem(LEN, ROWS, BF),
+                        vmem(LEN, HALO, BF), vmem(EXT, LEN, BF), vmem(ROWS, chans, BF),
+                        pltpu.SemaphoreType.DMA((4, steps)), pltpu.SemaphoreType.DMA((3,))],
+        compiler_params=params,
+        name="query",
+    )(halo, kept(pm), kept(hlate), kept(upstream), skip2, kept(fxh), kept(fhalo), kept(back))
 
     near = [[4 * a + b for b in range(4)] for a in range(size // 4)]
     far = [[4 * a + b for a in range(size // 4)] for b in range(4)]

time: 75 us -> 72.7 us (0.969)
  the two profiles are of different devices: /device:TPU:32 before, /device:TPU:9 now
where the time goes in v7:
time: 72.7 us; the launch traced here: 72.3 us
  starting transfers between devices  27 us (37%)
  Pallas kernels  22.2 us (31%)
  blocking collectives  20.9 us (29%)
  local copies, waits for them, and re-layouts  1.06 us (1%)
  between operations  1.01 us (1%)
    all_to_all x1, starting transfers between devices, local(): got = lax.all_to_all(merged, 'ctx', 0, 0, axis_index_groups=far, tiled=True)  15.1 us
    all_to_all x1, blocking collectives, local(): stats = lax.all_to_all(stats, 'tp', 0, 0, tiled=True)  12.1 us
    all_to_all x1, blocking collectives, local(): lax.all_to_all(payload, 'ctx', 0, 0, axis_index_groups=near, tiled=True)  8.82 us
    pallas_call x1, Pallas kernels, local(): pl.pallas_call(rest_kernel, grid=(steps,), in_specs=[whole(8, 8, 128)] +...  5.49 us
    ppermute x1, starting transfers between devices, local(): halo = lax.ppermute(halo, 'ctx', down)  5.35 us
    pallas_call x1, Pallas kernels, local(): pl.pallas_call(query_kernel, in_specs=[here] + [hbm] * 3 + [here] + [hbm]...  4.7 us
    pallas_call x1, Pallas kernels, local(): pl.pallas_call(filter_kernel, out_shape=[jax.ShapeDtypeStruct((4, 288, 12...  4.03 us
    ppermute x1, starting transfers between devices, local(): fwd = lax.ppermute(fwd, 'ctx', down)  4.01 us
  transfers between devices with their start and end apart: 4, of which 0 were waited for; matrix products, arithmetic and copies ran while one was open for 0% of the time, Pallas kernels for 18%

profile of v7, /device:TPU:9, one launch (start us, length us, event | category | flops | bytes accessed | tf_op | source)
XLA Modules:
  0.0 72.3 jit_solution(5037683883684043046)
XLA Ops:
  0.6 0.0 copy-start
  0.7 0.0 copy-start.5
  0.7 0.0 copy-start.4
  0.7 0.0 copy-start.3
  0.7 0.0 copy-start.13
  0.7 1.4 %send.1 = (bf16[8,1024]{1,0:T(8,128)(2,1)S(1)}, bf16[160,1024]{1,0:T(8,128)(2,1)S(1)}) custom-call(bf16[224,1024]{1,0:T(8,128)(2,1)} %kse.5, bf16[224,1024]{1,0:T(8,128)(2,1)} %vse.5, bf16[224,1024]{1,0:T(8,128)(2,1)} %qse.9, bf16[224,1024]{1,0:T(8,128)(2,1)} %kmr.7, bf16[224,1024]{1,0:T(8,128)(2,1)} %up_in.1, bf16[224,1024]{1,0:T(8,128)(2,1)} %qmr.3), custom_call_target="tpu_custom_call" | custom-call | tf_op jit(solution)/shard_map/send/pallas_call | solution.py:468
  2.1 2.6 %collective-permute-start.1 = (bf16[160,1024]{1,0:T(8,128)(2,1)S(1)}, bf16[160,1024]{1,0:T(8,128)(2,1)S(1)}, u32[]{:S(2)}, u32[]{:S(2)}) collective-permute-start(bf16[160,1024]{1,0:T(8,128)(2,1)S(1)} %get-tuple-element.36), channel_id=1, source_target_pairs={{8,0},{16,8},{24,16},{32,24},{40,32},{48,40},{56,48},{64,56},{72,6... | collective-permute-start | bytes 983048 | tf_op jit(solution)/shard_map/ppermute | solution.py:479
  4.7 0.0 copy-start.2
  4.7 0.0 copy-start.9
  4.7 0.0 copy-start.17
  4.7 0.0 copy-start.19
  4.7 0.0 copy-start.20
  4.7 4.0 %collective-permute-start = (bf16[8,1024]{1,0:T(8,128)(2,1)S(1)}, bf16[8,1024]{1,0:T(8,128)(2,1)S(1)}, u32[]{:S(2)}, u32[]{:S(2)}) collective-permute-start(bf16[8,1024]{1,0:T(8,128)(2,1)S(1)} %get-tuple-element.35), channel_id=1, source_target_pairs={{0,8},{8,16},{16,24},{24,32},{32,40},{40,48},{48,56},{56,64},{64,7... | collective-permute-start | bytes 49160 | tf_op jit(solution)/shard_map/ppermute | solution.py:480
  8.8 2.9 %local.1 = (f32[384,1024]{1,0:T(8,128)S(1)}, f32[384,1024]{1,0:T(8,128)S(1)}, bf16[384,1024]{1,0:T(8,128)(2,1)S(1)}, f32[224,1024]{1,0:T(8,128)S(1)}, f32[224,10...) custom-call(bf16[224,1024]{1,0:T(8,128)(2,1)S(1)} %copy-done.5, ...), custom_call_target="tpu_custom_call" | custom-call | tf_op jit(solution)/shard_map/local/pallas_call | solution.py:482
  11.7 0.9 %copy-done.11 = f32[224,1024]{1,0:T(8,128)} copy-done((f32[224,1024]{1,0:T(8,128)}, f32[224,1024]{1,0:T(8,128)S(1)}, u32[]{:S(2)}) %copy-start.11) | copy-done | bytes 917528
  12.6 0.0 collective-permute-done.fwd
  12.6 0.0 collective-permute-done.1.bwd
  12.6 0.0 copy-start.10
  12.7 0.0 copy-start.8
  12.7 0.0 copy-start.16
  12.7 2.3 %norm.1 = (f32[232,1024]{1,0:T(8,128)S(1)}, f32[384,1024]{1,0:T(8,128)S(1)}, f32[16,1024]{1,0:T(8,128)S(1)}, f32[16,1024]{1,0:T(8,128)S(1)}, f32[8,8,128]{2,1,0:T(8,128)S(1)}) custom-call(bf16[8,1024]{1,0:T(8,128)(2,1)S(1)} %collective-permute-done.fwd, bf16[160,1024]{1,0:T(8,128)(2,1)S(1)} %collective-permute-done.1.bwd, ...), custom_call_target="tpu_custom_call" | custom-call | tf_op jit(solution)/shard_map/norm/pallas_call | solution.py:493
  15.1 0.0 copy-done.10
  15.1 12.1 %all_to_all.15.stats = f32[8,8,128]{2,1,0:T(8,128)S(1)} all-to-all(f32[8,8,128]{2,1,0:T(8,128)S(1)} %get-tuple-element.43), channel_id=1, replica_groups=mesh['ctx'=64,'tp'=8] {'tp'}, dimensions={0} | all-to-all | bytes 65536 | tf_op jit(solution)/shard_map/all_to_all | solution.py:503
  27.3 4.0 %filters.1 = (bf16[4,288,128]{2,1,0:T(8,128)(2,1)S(1)}, bf16[128,1024]{1,0:T(8,128)(2,1)S(1)}) custom-call(f32[8,8,128]{2,1,0:T(8,128)S(1)} %all_to_all.15.stats, bf16[8,1024]{1,0:T(8,128)(2,1)S(1)} %collective-permute-done.fwd, f32[224,1024]{1,0:T(8,128)S(1)} %get-tuple-element.37.p, f32[224,1024]{1,0:T(8,128)S(1)} %get-tuple-element.38.g_in, ...), custom_call_target="tpu_custom_call" | custom-call | tf_op jit(solution)/shard_map/filters/pallas_call | solution.py:505
  31.3 8.8 %all_to_all.16.got = bf16[4,288,128]{2,1,0:T(8,128)(2,1)S(1)} all-to-all(bf16[4,288,128]{2,1,0:T(8,128)(2,1)S(1)} %get-tuple-element.56), channel_id=1, replica_groups={{0,8,16,24},{32,40,48,56},{64,72,80,88},{96,104,112,120},{128,136,144,1..., dimensions={0} | all-to-all | bytes 589824 | tf_op jit(solution)/shard_map/all_to_all | solution.py:546
  40.2 0.7 merge.1
  40.9 15.1 %all-to-all-start.2 = ((bf16[16,2,1152]{2,1,0:T(2,128)(2,1)}), bf16[16,2,1152]{2,1,0:T(2,128)(2,1)S(1)}, u32[]{:S(2)}, u32[]{:S(2)}) async-start(bf16[16,2,1152]{2,1,0:T(2,128)(2,1)} %merge.1), calls=%async_computation.2 | async-start | bytes 147456 | tf_op jit(solution)/shard_map/all_to_all | solution.py:550
  55.9 5.3 %collective-permute-start.2 = (bf16[128,1024]{1,0:T(8,128)(2,1)}, bf16[128,1024]{1,0:T(8,128)(2,1)S(1)}, u32[]{:S(2)}, u32[]{:S(2)}) collective-permute-start(bf16[128,1024]{1,0:T(8,128)(2,1)} %copy-done.21), channel_id=1, source_target_pairs={{0,8},{8,16},{16,24},{24,32},{32,40},{40,48},{48,56},{56,64},{64,7... | collective-permute-start | bytes 786440 | tf_op jit(solution)/shard_map/ppermute | solution.py:513
  61.3 5.5 %rest.1 = (bf16[224,1024]{1,0:T(8,128)(2,1)}, bf16[224,1024]{1,0:T(8,128)(2,1)}, bf16[224,1024]{1,0:T(8,128)(2,1)}, bf16[224,1024]{1,0:T(8,128)(2,1)}, bf16[224,1024]{1,0:T(8,128)(2,1)}) custom-call(f32[8,8,128]{2,1,0:T(8,128)} %copy-done.14, f32[224,1024]{1,0:T(8,128)} %copy-done.1, f32[224,1024]{1,0:T(8,128)} %copy-done.11, f32[16,1024]{1,0:T(8,128)} %copy-done.15, ...), custom_call_target="tpu_custom_call" | custom-call | tf_op jit(solution)/shard_map/rest/pallas_call | solution.py:522
  66.8 0.0 collective-permute-done.2.halo
  66.8 4.7 %query.1 = bf16[224,1024]{1,0:T(8,128)(2,1)} custom-call(bf16[128,1024]{1,0:T(8,128)(2,1)S(1)} %collective-permute-done.2.halo, bf16[224,1024]{1,0:T(8,128)(2,1)} %get-tuple-element.53.pm_in, bf16[384,1024]{1,0:T(8,128)(2,1)} %copy-done.12, bf16[224,1024]{1,0:T(8,128)(2,1)} %up_in.1, f32[1,1024]{1,0:T(1,128)S(1)} %bitcast.9, ...), custom_call_target="tpu_custom_call" | custom-call | tf_op jit(solution)/shard_map/query/pallas_call | solution.py:532
  71.5 0.8 %final.1 = (f32[7,16]{1,0:T(8,128)}, f32[16,128]{1,0:T(8,128)}, f32[1,16]{1,0:T(1,128)}, f32[1,16]{1,0:T(1,128)}) custom-call(bf16[16,2,1152]{2,1,0:T(2,128)(2,1)S(1)} %all-to-all-done.2.refs_0_), custom_call_target="tpu_custom_call" | custom-call | tf_op jit(solution)/shard_map/final/pallas_call | solution.py:552
  (30 shorter events, 0.1 us)
Async XLA Ops:
  0.6 8.1 %copy-start = (bf16[224,1024]{1,0:T(8,128)(2,1)S(1)}, bf16[224,1024]{1,0:T(8,128)(2,1)}, u32[]{:S(2)}) copy-start(bf16[224,1024]{1,0:T(8,128)(2,1)} %qse.9) | copy-start | bytes 1376260
  0.7 8.1 %copy-start.5 = (bf16[224,1024]{1,0:T(8,128)(2,1)S(1)}, bf16[224,1024]{1,0:T(8,128)(2,1)}, u32[]{:S(2)}) copy-start(bf16[224,1024]{1,0:T(8,128)(2,1)} %up_in.1) | copy-start | bytes 1376260
  0.7 8.1 %copy-start.4 = (bf16[224,1024]{1,0:T(8,128)(2,1)S(1)}, bf16[224,1024]{1,0:T(8,128)(2,1)}, u32[]{:S(2)}) copy-start(bf16[224,1024]{1,0:T(8,128)(2,1)} %vse.5) | copy-start | bytes 1376260
  0.7 8.1 %copy-start.3 = (bf16[224,1024]{1,0:T(8,128)(2,1)S(1)}, bf16[224,1024]{1,0:T(8,128)(2,1)}, u32[]{:S(2)}) copy-start(bf16[224,1024]{1,0:T(8,128)(2,1)} %kse.5) | copy-start | bytes 1376260
  0.7 8.1 %copy-start.7 = (bf16[224,1024]{1,0:T(8,128)(2,1)S(1)}, bf16[224,1024]{1,0:T(8,128)(2,1)}, u32[]{:S(2)}) copy-start(bf16[224,1024]{1,0:T(8,128)(2,1)} %qmr.3) | copy-start | bytes 1376260
  0.7 8.1 %copy-start.13 = (f32[7,1024]{1,0:T(8,128)S(1)}, f32[7,1024]{1,0:T(8,128)}, u32[]{:S(2)}) copy-start(f32[7,1024]{1,0:T(8,128)} %fse.5) | copy-start | bytes 86020
  2.1 10.5 %collective-permute-start.1 = (bf16[160,1024]{1,0:T(8,128)(2,1)S(1)}, bf16[160,1024]{1,0:T(8,128)(2,1)S(1)}, u32[]{:S(2)}, u32[]{:S(2)}) collective-permute-start(bf16[160,1024]{1,0:T(8,128)(2,1)S(1)} %get-tuple-element.36), channel_id=1, source_target_pairs={{8,0},{16,8},{24,16},{32,24},{40,32},{48,40},{56,48},{64,56},{72,6... | collective-permute-start | bytes 983048 | tf_op jit(solution)/shard_map/ppermute | solution.py:479
  4.7 8.0 %copy-start.2 = (bf16[224,1024]{1,0:T(8,128)(2,1)S(1)}, bf16[224,1024]{1,0:T(8,128)(2,1)}, u32[]{:S(2)}) copy-start(bf16[224,1024]{1,0:T(8,128)(2,1)} %kmr.7) | copy-start | bytes 1376260
  4.7 8.0 %copy-start.9 = (bf16[232,384]{1,0:T(8,128)(2,1)S(1)}, bf16[232,384]{1,0:T(8,128)(2,1)}, u32[]{:S(2)}) copy-start(bf16[232,384]{1,0:T(8,128)(2,1)} %constant.15.clone.th.th_in) | copy-start | bytes 534532
  4.7 8.0 %copy-start.17 = (bf16[384,136]{1,0:T(8,128)(2,1)S(1)}, bf16[384,136]{1,0:T(8,128)(2,1)}, u32[]{:S(2)}) copy-start(bf16[384,136]{1,0:T(8,128)(2,1)} %constant.14.clone.fhh) | copy-start | bytes 313348
  4.7 8.0 %copy-start.19 = (f32[1024]{0:T(1024)S(1)}, f32[1024]{0:T(1024)}, u32[]{:S(2)}) copy-start(f32[1024]{0:T(1024)} %param.25) | copy-start | bytes 12292
  4.7 8.0 %copy-start.20 = (f32[1024]{0:T(1024)S(1)}, f32[1024]{0:T(1024)}, u32[]{:S(2)}) copy-start(f32[1024]{0:T(1024)} %param.24) | copy-start | bytes 12292
  4.7 7.9 %collective-permute-start = (bf16[8,1024]{1,0:T(8,128)(2,1)S(1)}, bf16[8,1024]{1,0:T(8,128)(2,1)S(1)}, u32[]{:S(2)}, u32[]{:S(2)}) collective-permute-start(bf16[8,1024]{1,0:T(8,128)(2,1)S(1)} %get-tuple-element.35), channel_id=1, source_target_pairs={{0,8},{8,16},{16,24},{24,32},{32,40},{40,48},{48,56},{56,64},{64,7... | collective-permute-start | bytes 49160 | tf_op jit(solution)/shard_map/ppermute | solution.py:480
  11.7 0.9 %copy-start.11 = (f32[224,1024]{1,0:T(8,128)}, f32[224,1024]{1,0:T(8,128)S(1)}, u32[]{:S(2)}) copy-start(f32[224,1024]{1,0:T(8,128)S(1)} %get-tuple-element.44.conv) | copy-start | bytes 2752516
  12.6 2.5 %copy-start.12 = (bf16[384,1024]{1,0:T(8,128)(2,1)}, bf16[384,1024]{1,0:T(8,128)(2,1)S(1)}, u32[]{:S(2)}) copy-start(bf16[384,1024]{1,0:T(8,128)(2,1)S(1)} %get-tuple-element.54.hspec_in) | copy-start | bytes 2359300
  12.6 14.6 %copy-start.1 = (f32[224,1024]{1,0:T(8,128)}, f32[224,1024]{1,0:T(8,128)S(1)}, u32[]{:S(2)}) copy-start(f32[224,1024]{1,0:T(8,128)S(1)} %get-tuple-element.41.mixed) | copy-start | bytes 2752516
  12.6 2.5 %copy-start.10 = (bf16[160,1024]{1,0:T(8,128)(2,1)}, bf16[160,1024]{1,0:T(8,128)(2,1)S(1)}, u32[]{:S(2)}) copy-start(bf16[160,1024]{1,0:T(8,128)(2,1)S(1)} %collective-permute-done.1.bwd) | copy-start | bytes 983044
  12.7 14.6 %copy-start.8 = (bf16[384,224]{1,0:T(8,128)(2,1)S(1)}, bf16[384,224]{1,0:T(8,128)(2,1)}, u32[]{:S(2)}) copy-start(bf16[384,224]{1,0:T(8,128)(2,1)} %constant.12.clone.fxh_in.fxh) | copy-start | bytes 516100
  12.7 14.5 %copy-start.16 = (bf16[128,1024]{1,0:T(8,128)(2,1)S(1)}, bf16[128,1024]{1,0:T(8,128)(2,1)}, u32[]{:S(2)}) copy-start(bf16[128,1024]{1,0:T(8,128)(2,1)} %constant.16.clone.spots) | copy-start | bytes 786436
  15.1 16.2 %copy-start.6 = (f32[232,1024]{1,0:T(8,128)}, f32[232,1024]{1,0:T(8,128)S(1)}, u32[]{:S(2)}) copy-start(f32[232,1024]{1,0:T(8,128)S(1)} %get-tuple-element.47.gp) | copy-start | bytes 2850820
  15.1 16.2 %copy-start.15 = (f32[16,1024]{1,0:T(8,128)}, f32[16,1024]{1,0:T(8,128)S(1)}, u32[]{:S(2)}) copy-start(f32[16,1024]{1,0:T(8,128)S(1)} %get-tuple-element.45.mixed_e) | copy-start | bytes 196612
  15.1 16.2 %copy-start.18 = (f32[16,1024]{1,0:T(8,128)}, f32[16,1024]{1,0:T(8,128)S(1)}, u32[]{:S(2)}) copy-start(f32[16,1024]{1,0:T(8,128)S(1)} %get-tuple-element.46.conv_e) | copy-start | bytes 196612
  27.2 4.1 %copy-start.14 = (f32[8,8,128]{2,1,0:T(8,128)}, f32[8,8,128]{2,1,0:T(8,128)S(1)}, u32[]{:S(2)}) copy-start(f32[8,8,128]{2,1,0:T(8,128)S(1)} %all_to_all.15.stats) | copy-start | bytes 98308
  31.3 8.8 %copy-start.21 = (bf16[128,1024]{1,0:T(8,128)(2,1)}, bf16[128,1024]{1,0:T(8,128)(2,1)S(1)}, u32[]{:S(2)}) copy-start(bf16[128,1024]{1,0:T(8,128)(2,1)S(1)} %get-tuple-element.52) | copy-start | bytes 786436
  40.9 30.6 %all-to-all-start.2 = ((bf16[16,2,1152]{2,1,0:T(2,128)(2,1)}), bf16[16,2,1152]{2,1,0:T(2,128)(2,1)S(1)}, u32[]{:S(2)}, u32[]{:S(2)}) async-start(bf16[16,2,1152]{2,1,0:T(2,128)(2,1)} %merge.1), calls=%async_computation.2 | async-start | bytes 147456 | tf_op jit(solution)/shard_map/all_to_all | solution.py:550
  55.9 10.9 %collective-permute-start.2 = (bf16[128,1024]{1,0:T(8,128)(2,1)}, bf16[128,1024]{1,0:T(8,128)(2,1)S(1)}, u32[]{:S(2)}, u32[]{:S(2)}) collective-permute-start(bf16[128,1024]{1,0:T(8,128)(2,1)} %copy-done.21), channel_id=1, source_target_pairs={{0,8},{8,16},{16,24},{24,32},{32,40},{40,48},{48,56},{56,64},{64,7... | collective-permute-start | bytes 786440 | tf_op jit(solution)/shard_map/ppermute | solution.py:513

commit v8 on v7

--- a/solution.py
+++ b/solution.py
@@ -141,7 +141,7 @@
 
 
 def local_kernel(
-    up, qmr, kse, vse, qse, fse, fmr_in, fxh_in, fxl_in, gloc, hspec, hlate, conv_o, mixed_o, acc_o, p_o, g_o,
+    up, qmr, kse, vse, qse, fse, fmr_in, fxh_in, fxl_in, gloc, hspec, conv_o, mixed_o, acc_o, p_o, g_o,
     prod, fmr, fxh, fxl, sems
 ):
     pieces = ((fmr_in, fmr), (fxh_in, fxh), (fxl_in, fxl))
@@ -181,9 +181,7 @@
         gloc[:, c] = forward(fxh[...], fxl[...], g)
         high, low = split(fmr[:, c])
         fh = fxh[:, :128]
-        h = dot(fh, high) + dot(fxl[:, :128], high) + dot(fh, low)
-        hspec[:, c] = h
-        hlate[:, c] = h.astype(BF)
+        hspec[:, c] = dot(fh, high) + dot(fxl[:, :128], high) + dot(fh, low)
         return carry
 
     lax.fori_loop(0, steps, spectra, 0)
@@ -363,8 +361,7 @@
 
 
 def query_kernel(
-    halo, pm_in, hspec_in, up_in, skip, fxh_in, fhalo_in, th_in, gqmr,
-    pm, hspec, up, fxh, fhalo, th, out, sems, fixed_sems
+    halo, pm_in, hspec_in, up_in, skip, fxh, fhalo, th, gqmr, pm, hspec, up, out, sems
 ):
     steps = pm.shape[1] // CB
 
@@ -377,23 +374,15 @@
         c = block(b)
         return pltpu.make_async_copy(out.at[:, c], gqmr.at[:, c], sems.at[3, b])
 
-    bases = [
-        pltpu.make_async_copy(src, dst, fixed_sems.at[k])
-        for k, (src, dst) in enumerate(((fxh_in, fxh), (fhalo_in, fhalo), (th_in, th)))
-    ]
-    for copy in bases:
-        copy.start()
     for b in range(steps):
         for copy in copies(b):
             copy.start()
-    for copy in bases:
-        copy.wait()
 
     def step(b, carry):
         for copy in copies(b):
             copy.wait()
         c = block(b)
-        x, h = dot(fxh[...], pm[:, c]) + dot(fhalo[...], halo[:, c]), hspec[:, c].astype(F32)
+        x, h = dot(fxh[...], pm[:, c]) + dot(fhalo[...], halo[:, c]), hspec[:, c]
         xr, xi, hr, hi = x[:HALF], x[HALF:], h[:HALF], h[HALF:]
         spec = jnp.concatenate([(xr * hr - xi * hi).astype(BF), (xi * hr + xr * hi).astype(BF)], 0)
         ym = dot(th[...], spec)
@@ -479,10 +468,10 @@
     bwd = lax.ppermute(bwd, "ctx", upward)
     fwd = lax.ppermute(fwd, "ctx", down)
 
-    gloc, hspec, hlate, conv, mixed, acc, p, g = pl.pallas_call(
+    gloc, hspec, conv, mixed, acc, p, g = pl.pallas_call(
         local_kernel,
         in_specs=[here] * 6 + [hbm] * 3,
-        out_shape=[shape(LEN, F32), shape(LEN, F32), shape(LEN, BF), shape(ROWS, F32), shape(ROWS, F32),
+        out_shape=[shape(LEN, F32), shape(LEN, F32), shape(ROWS, F32), shape(ROWS, F32),
                    jax.ShapeDtypeStruct((256, 128), F32), shape(ROWS, F32), shape(ROWS, F32)],
         scratch_shapes=[shifts(ROWS + 8), vmem(filter_mr.shape[0], chans, F32), vmem(LEN, ROWS, BF),
                         vmem(LEN, ROWS, BF), pltpu.SemaphoreType.DMA((3,))],
@@ -531,15 +520,14 @@
     )(kept(stats), *(kept(x) for x in late))
     gqmr = pl.pallas_call(
         query_kernel,
-        in_specs=[here] + [hbm] * 3 + [here] + [hbm] * 3,
+        in_specs=[here] + [hbm] * 3 + [here] * 4,
         out_specs=hbm,
         out_shape=shape(ROWS, BF),
-        scratch_shapes=[vmem(ROWS, chans, BF), vmem(LEN, chans, BF), vmem(ROWS, chans, BF), vmem(LEN, ROWS, BF),
-                        vmem(LEN, HALO, BF), vmem(EXT, LEN, BF), vmem(ROWS, chans, BF),
-                        pltpu.SemaphoreType.DMA((4, steps)), pltpu.SemaphoreType.DMA((3,))],
+        scratch_shapes=[vmem(ROWS, chans, BF), vmem(LEN, chans, F32), vmem(ROWS, chans, BF), vmem(ROWS, chans, BF),
+                        pltpu.SemaphoreType.DMA((4, steps))],
         compiler_params=params,
         name="query",
-    )(halo, kept(pm), kept(hlate), kept(upstream), skip2, kept(fxh), kept(fhalo), kept(back))
+    )(halo, kept(pm), kept(hspec), kept(upstream), skip2, fxh, fhalo, back)
 
     near = [[4 * a + b for b in range(4)] for a in range(size // 4)]
     far = [[4 * a + b for a in range(size // 4)] for b in range(4)]

time: 72.7 us -> 72.4 us (level)
  local copies, waits for them, and re-layouts: 1.06 us -> 0.15 us
    unnamed x44 -> x48, local copies, waits for them, and re-layouts: 1.06 us -> 0.15 us
  transfers between devices with their start and end apart: 4 -> 4, of which waited for: 0 -> 0; matrix products, arithmetic and copies ran while one was open for 0% -> 0% of each run, Pallas kernels for 18% -> 17%
where the time goes in v8:
time: 72.4 us; the launch traced here: 71.9 us
  starting transfers between devices  27.5 us (38%)
  Pallas kernels  21.8 us (30%)
  blocking collectives  21.3 us (29%)
  between operations  1.09 us (2%)
    all_to_all x1, starting transfers between devices, local(): got = lax.all_to_all(merged, 'ctx', 0, 0, axis_index_groups=far, tiled=True)  15.6 us
    all_to_all x1, blocking collectives, local(): stats = lax.all_to_all(stats, 'tp', 0, 0, tiled=True)  12.1 us
    all_to_all x1, blocking collectives, local(): lax.all_to_all(payload, 'ctx', 0, 0, axis_index_groups=near, tiled=True)  9.2 us
    pallas_call x1, Pallas kernels, local(): pl.pallas_call(rest_kernel, grid=(steps,), in_specs=[whole(8, 8, 128)] +...  5.58 us
    ppermute x1, starting transfers between devices, local(): halo = lax.ppermute(halo, 'ctx', down)  5.35 us
    pallas_call x1, Pallas kernels, local(): pl.pallas_call(query_kernel, in_specs=[here] + [hbm] * 3 + [here] * 4, ou...  4.16 us
    pallas_call x1, Pallas kernels, local(): pl.pallas_call(filter_kernel, out_shape=[jax.ShapeDtypeStruct((4, 288, 12...  4.05 us
    ppermute x1, starting transfers between devices, local(): fwd = lax.ppermute(fwd, 'ctx', down)  4.01 us
  transfers between devices with their start and end apart: 4, of which 0 were waited for; matrix products, arithmetic and copies ran while one was open for 0% of the time, Pallas kernels for 17%

profile of v8, /device:TPU:9, one launch (start us, length us, event | category | flops | bytes accessed | tf_op | source)
XLA Modules:
  0.0 71.9 jit_solution(534522932803072979)
XLA Ops:
  0.6 0.0 copy-start
  0.7 0.0 copy-start.6
  0.7 0.0 copy-start.5
  0.7 0.0 copy-start.4
  0.7 0.0 copy-start.15
  0.7 1.4 %send.1 = (bf16[8,1024]{1,0:T(8,128)(2,1)S(1)}, bf16[160,1024]{1,0:T(8,128)(2,1)S(1)}) custom-call(bf16[224,1024]{1,0:T(8,128)(2,1)} %kse.5, bf16[224,1024]{1,0:T(8,128)(2,1)} %vse.5, bf16[224,1024]{1,0:T(8,128)(2,1)} %qse.9, bf16[224,1024]{1,0:T(8,128)(2,1)} %kmr.7, bf16[224,1024]{1,0:T(8,128)(2,1)} %up_in.1, bf16[224,1024]{1,0:T(8,128)(2,1)} %qmr.3), custom_call_target="tpu_custom_call" | custom-call | tf_op jit(solution)/shard_map/send/pallas_call | solution.py:457
  2.1 2.6 %collective-permute-start.1 = (bf16[160,1024]{1,0:T(8,128)(2,1)S(1)}, bf16[160,1024]{1,0:T(8,128)(2,1)S(1)}, u32[]{:S(2)}, u32[]{:S(2)}) collective-permute-start(bf16[160,1024]{1,0:T(8,128)(2,1)S(1)} %get-tuple-element.35), channel_id=1, source_target_pairs={{8,0},{16,8},{24,16},{32,24},{40,32},{48,40},{56,48},{64,56},{72,6... | collective-permute-start | bytes 983048 | tf_op jit(solution)/shard_map/ppermute | solution.py:468
  4.7 0.0 copy-start.2
  4.7 0.0 copy-start.11
  4.7 0.0 copy-start.19
  4.7 0.0 copy-start.22
  4.7 0.0 copy-start.23
  4.7 4.0 %collective-permute-start = (bf16[8,1024]{1,0:T(8,128)(2,1)S(1)}, bf16[8,1024]{1,0:T(8,128)(2,1)S(1)}, u32[]{:S(2)}, u32[]{:S(2)}) collective-permute-start(bf16[8,1024]{1,0:T(8,128)(2,1)S(1)} %get-tuple-element.34), channel_id=1, source_target_pairs={{0,8},{8,16},{16,24},{24,32},{32,40},{40,48},{48,56},{56,64},{64,7... | collective-permute-start | bytes 49160 | tf_op jit(solution)/shard_map/ppermute | solution.py:469
  8.8 2.8 %local.1 = (f32[384,1024]{1,0:T(8,128)S(1)}, f32[384,1024]{1,0:T(8,128)S(1)}, f32[224,1024]{1,0:T(8,128)S(1)}, f32[224,1024]{1,0:T(8,128)S(1)}, f32[256,128]{1,0...) custom-call(bf16[224,1024]{1,0:T(8,128)(2,1)S(1)} %copy-done.6, bf16[224,1024]{1,0:T(8,128)(2,1)S(1)} %copy-done.8, ...), custom_call_target="tpu_custom_call" | custom-call | tf_op jit(solution)/shard_map/local/pallas_call | solution.py:471
  11.7 0.0 collective-permute-done.1.bwd
  11.7 0.0 copy-start.13
  11.8 0.0 copy-start.9
  11.8 0.0 copy-start.18
  11.8 2.4 %norm.1 = (f32[232,1024]{1,0:T(8,128)S(1)}, f32[384,1024]{1,0:T(8,128)S(1)}, f32[16,1024]{1,0:T(8,128)S(1)}, f32[16,1024]{1,0:T(8,128)S(1)}, f32[8,8,128]{2,1,0:T(8,128)S(1)}) custom-call(bf16[8,1024]{1,0:T(8,128)(2,1)S(1)} %collective-permute-done.fwd, bf16[160,1024]{1,0:T(8,128)(2,1)S(1)} %collective-permute-done.1.bwd, ...), custom_call_target="tpu_custom_call" | custom-call | tf_op jit(solution)/shard_map/norm/pallas_call | solution.py:482
  14.2 0.0 copy-done.14
  14.2 12.1 %all_to_all.15.stats = f32[8,8,128]{2,1,0:T(8,128)S(1)} all-to-all(f32[8,8,128]{2,1,0:T(8,128)S(1)} %get-tuple-element.42), channel_id=1, replica_groups=mesh['ctx'=64,'tp'=8] {'tp'}, dimensions={0} | all-to-all | bytes 65536 | tf_op jit(solution)/shard_map/all_to_all | solution.py:492
  26.4 4.1 %filters.1 = (bf16[4,288,128]{2,1,0:T(8,128)(2,1)S(1)}, bf16[128,1024]{1,0:T(8,128)(2,1)S(1)}) custom-call(f32[8,8,128]{2,1,0:T(8,128)S(1)} %all_to_all.15.stats, bf16[8,1024]{1,0:T(8,128)(2,1)S(1)} %collective-permute-done.fwd, f32[224,1024]{1,0:T(8,128)S(1)} %get-tuple-element.36.p, f32[224,1024]{1,0:T(8,128)S(1)} %get-tuple-element.37.g_in, ...), custom_call_target="tpu_custom_call" | custom-call | tf_op jit(solution)/shard_map/filters/pallas_call | solution.py:494
  30.5 9.2 %all_to_all.16.got = bf16[4,288,128]{2,1,0:T(8,128)(2,1)S(1)} all-to-all(bf16[4,288,128]{2,1,0:T(8,128)(2,1)S(1)} %get-tuple-element.54), channel_id=1, replica_groups={{0,8,16,24},{32,40,48,56},{64,72,80,88},{96,104,112,120},{128,136,144,1..., dimensions={0} | all-to-all | bytes 589824 | tf_op jit(solution)/shard_map/all_to_all | solution.py:534
  39.7 0.7 merge.1
  40.4 15.6 %all-to-all-start.2 = ((bf16[16,2,1152]{2,1,0:T(2,128)(2,1)}), bf16[16,2,1152]{2,1,0:T(2,128)(2,1)S(1)}, u32[]{:S(2)}, u32[]{:S(2)}) async-start(bf16[16,2,1152]{2,1,0:T(2,128)(2,1)} %merge.1), calls=%async_computation.2 | async-start | bytes 147456 | tf_op jit(solution)/shard_map/all_to_all | solution.py:538
  56.0 5.4 %collective-permute-start.2 = (bf16[128,1024]{1,0:T(8,128)(2,1)S(1)}, bf16[128,1024]{1,0:T(8,128)(2,1)S(1)}, u32[]{:S(2)}, u32[]{:S(2)}) collective-permute-start(bf16[128,1024]{1,0:T(8,128)(2,1)S(1)} %get-tuple-element.51), channel_id=1, source_target_pairs={{0,8},{8,16},{16,24},{24,32},{32,40},{40,48},{48,56},{56,64},{64,7... | collective-permute-start | bytes 786440 | tf_op jit(solution)/shard_map/ppermute | solution.py:502
  61.3 0.0 copy-start.10
  61.3 0.0 copy-start.12
  61.3 0.0 copy-start.20
  61.4 5.6 %rest.1 = (bf16[224,1024]{1,0:T(8,128)(2,1)}, bf16[224,1024]{1,0:T(8,128)(2,1)}, bf16[224,1024]{1,0:T(8,128)(2,1)}, bf16[224,1024]{1,0:T(8,128)(2,1)}, bf16[224,1024]{1,0:T(8,128)(2,1)}) custom-call(f32[8,8,128]{2,1,0:T(8,128)} %copy-done.16, f32[224,1024]{1,0:T(8,128)} %copy-done.1, f32[224,1024]{1,0:T(8,128)} %copy-done.14, f32[16,1024]{1,0:T(8,128)} %copy-done.17, ...), custom_call_target="tpu_custom_call" | custom-call | tf_op jit(solution)/shard_map/rest/pallas_call | solution.py:511
  67.0 4.2 %query.1 = bf16[224,1024]{1,0:T(8,128)(2,1)} custom-call(bf16[128,1024]{1,0:T(8,128)(2,1)S(1)} %collective-permute-done.2.halo, bf16[224,1024]{1,0:T(8,128)(2,1)} %get-tuple-element.52.pm_in, f32[384,1024]{1,0:T(8,128)} %copy-done.3, bf16[224,1024]{1,0:T(8,128)(2,1)} %up_in.1, f32[1,1024]{1,0:T(1,128)S(1)} %bitcast.9, bf16[384,224]{1,0:T(8,128)(2,1)S(1)} %copy-done.10, ...), custom_call_target="tpu_custom_call" | custom-call | tf_op jit(solution)/shard_map/query/pallas_call | solution.py:521
  71.1 0.8 %final.1 = (f32[7,16]{1,0:T(8,128)}, f32[16,128]{1,0:T(8,128)}, f32[1,16]{1,0:T(1,128)}, f32[1,16]{1,0:T(1,128)}) custom-call(bf16[16,2,1152]{2,1,0:T(2,128)(2,1)S(1)} %all-to-all-done.2.refs_0_), custom_call_target="tpu_custom_call" | custom-call | tf_op jit(solution)/shard_map/final/pallas_call | solution.py:540
  (34 shorter events, 0.1 us)
Async XLA Ops:
  0.6 8.1 %copy-start = (bf16[224,1024]{1,0:T(8,128)(2,1)S(1)}, bf16[224,1024]{1,0:T(8,128)(2,1)}, u32[]{:S(2)}) copy-start(bf16[224,1024]{1,0:T(8,128)(2,1)} %qse.9) | copy-start | bytes 1376260
  0.7 8.1 %copy-start.6 = (bf16[224,1024]{1,0:T(8,128)(2,1)S(1)}, bf16[224,1024]{1,0:T(8,128)(2,1)}, u32[]{:S(2)}) copy-start(bf16[224,1024]{1,0:T(8,128)(2,1)} %up_in.1) | copy-start | bytes 1376260
  0.7 8.1 %copy-start.5 = (bf16[224,1024]{1,0:T(8,128)(2,1)S(1)}, bf16[224,1024]{1,0:T(8,128)(2,1)}, u32[]{:S(2)}) copy-start(bf16[224,1024]{1,0:T(8,128)(2,1)} %vse.5) | copy-start | bytes 1376260
  0.7 8.1 %copy-start.4 = (bf16[224,1024]{1,0:T(8,128)(2,1)S(1)}, bf16[224,1024]{1,0:T(8,128)(2,1)}, u32[]{:S(2)}) copy-start(bf16[224,1024]{1,0:T(8,128)(2,1)} %kse.5) | copy-start | bytes 1376260
  0.7 8.1 %copy-start.8 = (bf16[224,1024]{1,0:T(8,128)(2,1)S(1)}, bf16[224,1024]{1,0:T(8,128)(2,1)}, u32[]{:S(2)}) copy-start(bf16[224,1024]{1,0:T(8,128)(2,1)} %qmr.3) | copy-start | bytes 1376260
  0.7 8.1 %copy-start.15 = (f32[7,1024]{1,0:T(8,128)S(1)}, f32[7,1024]{1,0:T(8,128)}, u32[]{:S(2)}) copy-start(f32[7,1024]{1,0:T(8,128)} %fse.5) | copy-start | bytes 86020
  2.1 9.6 %collective-permute-start.1 = (bf16[160,1024]{1,0:T(8,128)(2,1)S(1)}, bf16[160,1024]{1,0:T(8,128)(2,1)S(1)}, u32[]{:S(2)}, u32[]{:S(2)}) collective-permute-start(bf16[160,1024]{1,0:T(8,128)(2,1)S(1)} %get-tuple-element.35), channel_id=1, source_target_pairs={{8,0},{16,8},{24,16},{32,24},{40,32},{48,40},{56,48},{64,56},{72,6... | collective-permute-start | bytes 983048 | tf_op jit(solution)/shard_map/ppermute | solution.py:468
  4.7 7.0 %copy-start.2 = (bf16[224,1024]{1,0:T(8,128)(2,1)S(1)}, bf16[224,1024]{1,0:T(8,128)(2,1)}, u32[]{:S(2)}) copy-start(bf16[224,1024]{1,0:T(8,128)(2,1)} %kmr.7) | copy-start | bytes 1376260
  4.7 7.0 %copy-start.11 = (bf16[232,384]{1,0:T(8,128)(2,1)S(1)}, bf16[232,384]{1,0:T(8,128)(2,1)}, u32[]{:S(2)}) copy-start(bf16[232,384]{1,0:T(8,128)(2,1)} %constant.15.clone.th) | copy-start | bytes 534532
  4.7 7.0 %copy-start.19 = (bf16[384,136]{1,0:T(8,128)(2,1)S(1)}, bf16[384,136]{1,0:T(8,128)(2,1)}, u32[]{:S(2)}) copy-start(bf16[384,136]{1,0:T(8,128)(2,1)} %constant.14.clone.fhh) | copy-start | bytes 313348
  4.7 7.0 %copy-start.22 = (f32[1024]{0:T(1024)S(1)}, f32[1024]{0:T(1024)}, u32[]{:S(2)}) copy-start(f32[1024]{0:T(1024)} %param.25) | copy-start | bytes 12292
  4.7 7.0 %copy-start.23 = (f32[1024]{0:T(1024)S(1)}, f32[1024]{0:T(1024)}, u32[]{:S(2)}) copy-start(f32[1024]{0:T(1024)} %param.24) | copy-start | bytes 12292
  4.7 7.0 %collective-permute-start = (bf16[8,1024]{1,0:T(8,128)(2,1)S(1)}, bf16[8,1024]{1,0:T(8,128)(2,1)S(1)}, u32[]{:S(2)}, u32[]{:S(2)}) collective-permute-start(bf16[8,1024]{1,0:T(8,128)(2,1)S(1)} %get-tuple-element.34), channel_id=1, source_target_pairs={{0,8},{8,16},{16,24},{24,32},{32,40},{40,48},{48,56},{56,64},{64,7... | collective-permute-start | bytes 49160 | tf_op jit(solution)/shard_map/ppermute | solution.py:469
  11.7 2.5 %copy-start.3 = (f32[384,1024]{1,0:T(8,128)}, f32[384,1024]{1,0:T(8,128)S(1)}, u32[]{:S(2)}) copy-start(f32[384,1024]{1,0:T(8,128)S(1)} %get-tuple-element.39.hspec.hspec_in) | copy-start | bytes 4718596
  11.7 2.5 %copy-start.14 = (f32[224,1024]{1,0:T(8,128)}, f32[224,1024]{1,0:T(8,128)S(1)}, u32[]{:S(2)}) copy-start(f32[224,1024]{1,0:T(8,128)S(1)} %get-tuple-element.43.conv) | copy-start | bytes 2752516
  11.7 14.7 %copy-start.1 = (f32[224,1024]{1,0:T(8,128)}, f32[224,1024]{1,0:T(8,128)S(1)}, u32[]{:S(2)}) copy-start(f32[224,1024]{1,0:T(8,128)S(1)} %get-tuple-element.40.mixed) | copy-start | bytes 2752516
  11.7 2.5 %copy-start.13 = (bf16[160,1024]{1,0:T(8,128)(2,1)}, bf16[160,1024]{1,0:T(8,128)(2,1)S(1)}, u32[]{:S(2)}) copy-start(bf16[160,1024]{1,0:T(8,128)(2,1)S(1)} %collective-permute-done.1.bwd) | copy-start | bytes 983044
  11.8 14.6 %copy-start.9 = (bf16[384,224]{1,0:T(8,128)(2,1)S(1)}, bf16[384,224]{1,0:T(8,128)(2,1)}, u32[]{:S(2)}) copy-start(bf16[384,224]{1,0:T(8,128)(2,1)} %constant.12.clone.fxh_in.fxh) | copy-start | bytes 516100
  11.8 14.6 %copy-start.18 = (bf16[128,1024]{1,0:T(8,128)(2,1)S(1)}, bf16[128,1024]{1,0:T(8,128)(2,1)}, u32[]{:S(2)}) copy-start(bf16[128,1024]{1,0:T(8,128)(2,1)} %constant.16.clone.spots) | copy-start | bytes 786436
  14.2 16.2 %copy-start.7 = (f32[232,1024]{1,0:T(8,128)}, f32[232,1024]{1,0:T(8,128)S(1)}, u32[]{:S(2)}) copy-start(f32[232,1024]{1,0:T(8,128)S(1)} %get-tuple-element.46.gp) | copy-start | bytes 2850820
  14.2 16.2 %copy-start.17 = (f32[16,1024]{1,0:T(8,128)}, f32[16,1024]{1,0:T(8,128)S(1)}, u32[]{:S(2)}) copy-start(f32[16,1024]{1,0:T(8,128)S(1)} %get-tuple-element.44.mixed_e) | copy-start | bytes 196612
  14.2 16.2 %copy-start.21 = (f32[16,1024]{1,0:T(8,128)}, f32[16,1024]{1,0:T(8,128)S(1)}, u32[]{:S(2)}) copy-start(f32[16,1024]{1,0:T(8,128)S(1)} %get-tuple-element.45.conv_e) | copy-start | bytes 196612
  26.3 4.1 %copy-start.16 = (f32[8,8,128]{2,1,0:T(8,128)}, f32[8,8,128]{2,1,0:T(8,128)S(1)}, u32[]{:S(2)}) copy-start(f32[8,8,128]{2,1,0:T(8,128)S(1)} %all_to_all.15.stats) | copy-start | bytes 98308
  40.4 30.8 %all-to-all-start.2 = ((bf16[16,2,1152]{2,1,0:T(2,128)(2,1)}), bf16[16,2,1152]{2,1,0:T(2,128)(2,1)S(1)}, u32[]{:S(2)}, u32[]{:S(2)}) async-start(bf16[16,2,1152]{2,1,0:T(2,128)(2,1)} %merge.1), calls=%async_computation.2 | async-start | bytes 147456 | tf_op jit(solution)/shard_map/all_to_all | solution.py:538
  56.0 11.0 %collective-permute-start.2 = (bf16[128,1024]{1,0:T(8,128)(2,1)S(1)}, bf16[128,1024]{1,0:T(8,128)(2,1)S(1)}, u32[]{:S(2)}, u32[]{:S(2)}) collective-permute-start(bf16[128,1024]{1,0:T(8,128)(2,1)S(1)} %get-tuple-element.51), channel_id=1, source_target_pairs={{0,8},{8,16},{16,24},{24,32},{32,40},{40,48},{48,56},{56,64},{64,7... | collective-permute-start | bytes 786440 | tf_op jit(solution)/shard_map/ppermute | solution.py:502
  61.3 5.6 %copy-start.10 = (bf16[384,224]{1,0:T(8,128)(2,1)S(1)}, bf16[384,224]{1,0:T(8,128)(2,1)}, u32[]{:S(2)}) copy-start(bf16[384,224]{1,0:T(8,128)(2,1)} %constant.12.clone.fxh_in.fxh) | copy-start | bytes 516100
  61.3 5.6 %copy-start.12 = (bf16[232,384]{1,0:T(8,128)(2,1)S(1)}, bf16[232,384]{1,0:T(8,128)(2,1)}, u32[]{:S(2)}) copy-start(bf16[232,384]{1,0:T(8,128)(2,1)} %constant.15.clone.th) | copy-start | bytes 534532
  61.3 5.6 %copy-start.20 = (bf16[384,128]{1,0:T(8,128)(2,1)S(1)}, bf16[384,128]{1,0:T(8,128)(2,1)}, u32[]{:S(2)}) copy-start(bf16[384,128]{1,0:T(8,128)(2,1)} %constant.17.clone.fhalo) | copy-start | bytes 294916
